TPU v7x, 32 devices: a whole 2x2x4 slice. The times are simulated.
32 devices in a mesh: band: 8 (over z, y), grid: 4 (over x, core).
Axes of the slice: x: 2, y: 2, z: 4, core: 2. Of those that a mesh axis runs over, the one named last changes fastest.
Arguments:
- own_bands: float32 [32, 128, 128, 128], P('band', 'grid'), may hold values from -1.5 to 1.5
- travel_bands: float32 [32, 128, 128, 128], P('band', 'grid'), may hold values from -1.5 to 1.5
Outputs:
- own_terms: float32 [32, 128, 128, 128], P('band', 'grid')
- partner_terms: float32 [32, 128, 128, 128], P('band', 'grid')
All inputs are finite; a program needn't handle non-finite values.
Results may differ from a plain program's by a relative error of at most 0.00011.
Values sent between devices are 32-bit elements; how exact they have to be, the bound alone decides.
A program may use at most 192 MiB of HBM per device.

v0:
```python
import math

import jax
import jax.numpy as jnp
from jax import lax
from jax.sharding import PartitionSpec as P

NX = 128
NY = 128
NZ = 128


FRACTION = 0.25
HIGHEST_PRECISION = lax.Precision.HIGHEST


def passed_along(block, axis, distance):
    devices = range(lax.axis_size(axis))
    route = [((i - distance) % len(devices), i) for i in devices]
    return lax.ppermute(block, axis, route)


def wave_square(points, first_row, length):
    position = first_row + jnp.arange(points, dtype=jnp.int32)
    position = (position + length // 2) % length - length // 2
    wavenumber = 2.0 * math.pi / length * position.astype(jnp.float32)
    return wavenumber * wavenumber


def coulomb(first_row, row_count):
    squared = (
        wave_square(NZ, 0, NZ)[:, None, None]
        + wave_square(row_count, first_row, NY)[None, :, None]
        + wave_square(NX, 0, NX)[None, None, :]
    )
    safe_square = jnp.where(squared > 0.0, squared, 1.0)
    return jnp.where(squared > 0.0, 4.0 * math.pi / safe_square, 0.0)


def fourier_table(length, inverse):
    position = jnp.arange(length, dtype=jnp.int32)
    phase_turns = position[:, None] * position[None, :] % length
    phase_angle = 2.0 * math.pi / length * phase_turns.astype(jnp.float32)
    cosine = jnp.cos(phase_angle)
    sine_part = jnp.sin(phase_angle)
    norm_factor = 1.0
    if inverse:
        sine_part = -sine_part
        norm_factor = 1.0 / length
    return norm_factor * jnp.stack(
        [jnp.stack([cosine, -sine_part]), jnp.stack([sine_part, cosine])]
    )


def solve_pairs(packed, kernel_slab):
    spectrum = jnp.einsum(
        "pczyx,cdxk->dpzyk", packed, fourier_table(NX, False), precision=HIGHEST_PRECISION
    )
    spectrum = jnp.einsum(
        "cpzyx,cdyk->dpzkx", spectrum, fourier_table(NY, False), precision=HIGHEST_PRECISION
    )
    forward_z = fourier_table(NZ, False)
    inverse_z = fourier_table(NZ, True)
    screened = (
        jnp.einsum(
            "cpzyx,cdzk->dpkyx",
            lax.all_to_all(spectrum, "grid", split_axis=3, concat_axis=2, tiled=True),
            forward_z,
            precision=HIGHEST_PRECISION,
        )
        * kernel_slab
    )
    screened = jnp.einsum("cpzyx,cdzk->dpkyx", screened, inverse_z, precision=HIGHEST_PRECISION)
    planes = lax.all_to_all(screened, "grid", split_axis=2, concat_axis=3, tiled=True)
    planes = jnp.einsum(
        "cpzyx,cdyk->dpzkx", planes, fourier_table(NY, True), precision=HIGHEST_PRECISION
    )
    return jnp.einsum(
        "cpzyx,cdxk->pdzyk", planes, fourier_table(NX, True), precision=HIGHEST_PRECISION
    )


def pair_terms(owned, visitors, kernel_slab):
    count_vis = visitors.shape[0]
    count_own = owned.shape[0]
    density = owned[None] * visitors[:, None]
    packed = density.reshape((count_vis * count_own // 2, 2) + owned.shape[1:])
    potential = solve_pairs(packed, kernel_slab).reshape(density.shape)
    own_part = jnp.sum(potential * visitors[:, None], axis=0)
    partner = jnp.sum(potential * owned[None], axis=1)
    return (own_part, partner)


def body(own_bands, travel_bands):
    rows_local = NY // lax.axis_size("grid")
    kernel_slab = coulomb(lax.axis_index("grid") * rows_local, rows_local)
    count_vis = travel_bands.shape[0]
    own_total = jnp.zeros_like(own_bands)
    returned = []
    for visit_index in range(count_vis):
        visitor = passed_along(travel_bands[visit_index : visit_index + 1], "band", 1)
        own_part, partner = pair_terms(own_bands, visitor, kernel_slab)
        own_total = own_total + own_part
        returned.append(passed_along(partner, "band", -1))
    partner_total = jnp.concatenate(returned, axis=0)
    return (-FRACTION * own_total, -FRACTION * partner_total)


def exchanged(block, bit):
    devices = range(lax.axis_size("grid"))
    return lax.ppermute(block, "grid", [(i, i ^ bit) for i in devices])


def line_table(from_position, to_position, length, inverse):
    phase_turns = from_position[:, None] * to_position[None, :] % length
    phase_angle = 2.0 * math.pi / length * phase_turns.astype(jnp.float32)
    cosine = jnp.cos(phase_angle)
    sine_part = jnp.sin(phase_angle)
    norm_factor = 1.0
    if inverse:
        sine_part = -sine_part
        norm_factor = 1.0 / length
    return norm_factor * jnp.stack(
        [jnp.stack([cosine, -sine_part]), jnp.stack([sine_part, cosine])]
    )


def transform(equation, values, table):
    return jnp.einsum(equation, values, table, precision=lax.Precision.HIGH)


def square_body(own_bands, travel_bands):
    rank = lax.axis_index("grid")
    chip, core = rank // 2, rank % 2
    half_own = own_bands.shape[0] // 2
    half_vis = travel_bands.shape[0] // 2
    depth, ny, nx = own_bands.shape[1:]
    nz = depth * lax.axis_size("grid")

    def planes(first, second):
        steps = jnp.arange(depth, dtype=jnp.int32)
        return jnp.concatenate([first * depth + steps, second * depth + steps])

    every_z = jnp.arange(nz, dtype=jnp.int32)
    every_y = jnp.arange(ny, dtype=jnp.int32)
    every_x = jnp.arange(nx, dtype=jnp.int32)
    piece_z = (planes(rank, rank ^ 1), planes(rank ^ 2, rank ^ 3))
    forward_x = line_table(every_x, every_x, nx, False)
    forward_y = line_table(every_y, every_y, ny, False)
    inverse_x = line_table(every_x, every_x, nx, True)
    inverse_y = line_table(every_y, every_y, ny, True)
    forward_z = [line_table(z, every_z, nz, False) for z in piece_z]
    inverse_z = [line_table(every_z, z, nz, True) for z in piece_z]
    kernel_cube = coulomb(0, ny)

    own_mine = lax.dynamic_slice_in_dim(own_bands, chip * half_own, half_own, 0)
    own_away = lax.dynamic_slice_in_dim(own_bands, (1 - chip) * half_own, half_own, 0)
    own_far = exchanged(own_away, 2)
    owned = [
        jnp.concatenate([block, exchanged(block, 1)], axis=1) for block in (own_mine, own_far)
    ]

    visitors = []
    for k in range(half_vis):
        mine = lax.dynamic_index_in_dim(travel_bands, core * half_vis + k, 0, keepdims=False)
        away = lax.dynamic_index_in_dim(travel_bands, (1 - core) * half_vis + k, 0, keepdims=False)
        away = passed_along(away, "band", 1)
        mine = passed_along(mine, "band", 1)
        away = exchanged(away, 1)
        visitors.append(
            [
                jnp.concatenate([mine, away], axis=0),
                jnp.concatenate([exchanged(mine, 2), exchanged(away, 2)], axis=0),
            ]
        )

    own_sum = [0.0, 0.0]
    held_mine, held_away = [], []
    for k in range(half_vis):
        spectrum = 0.0
        for p in (0, 1):
            part = owned[p] * visitors[k][p][None]
            part = transform("czyx,cdxk->dzyk", part, forward_x)
            part = transform("czyx,cdyk->dzkx", part, forward_y)
            spectrum = spectrum + transform("czyx,cdzk->dkyx", part, forward_z[p])
        spectrum = spectrum * kernel_cube
        held = [None, None]
        for p in (1, 0):
            part = transform("czyx,cdzk->dkyx", spectrum, inverse_z[p])
            part = transform("czyx,cdyk->dzkx", part, inverse_y)
            part = transform("czyx,cdxk->dzyk", part, inverse_x)
            held[p] = jnp.sum(part * owned[p], axis=0)
            own_sum[p] = own_sum[p] + part * visitors[k][p][None]
        held_near = -FRACTION * (held[0] + exchanged(held[1], 2))
        held_mine.append(passed_along(held_near[:depth], "band", -1))
        held_away.append(passed_along(exchanged(held_near[depth:], 1), "band", -1))

    own_near, own_back = [
        -FRACTION * (total[:, :depth] + exchanged(total[:, depth:], 1)) for total in own_sum
    ]
    own_back = exchanged(own_back, 2)
    own_rows = jnp.where(
        chip == 0,
        jnp.concatenate([own_near, own_back], axis=0),
        jnp.concatenate([own_back, own_near], axis=0),
    )
    held_rows = jnp.where(
        core == 0, jnp.stack(held_mine + held_away), jnp.stack(held_away + held_mine)
    )
    return own_rows, held_rows


def solution(mesh):
    in_specs = (P("band", "grid", None, None), P("band", "grid", None, None))
    out_specs = (P("band", "grid", None, None), P("band", "grid", None, None))

    def placed(own_bands, travel_bands):
        group_own = own_bands.shape[0] // mesh.shape["band"]
        group_vis = travel_bands.shape[0] // mesh.shape["band"]
        square = mesh.shape["grid"] == 4 and group_own == 4 and group_vis % 2 == 0
        return jax.shard_map(
            square_body if square else body,
            mesh=mesh,
            in_specs=in_specs,
            out_specs=out_specs,
            check_vma=False,
        )(own_bands, travel_bands)

    return placed
```

profile of v0, /device:TPU:0, one launch (start us, length us, event | category | flops | bytes accessed | tf_op | source)
XLA Modules:
  0.0 992.3 jit_solution(15595370734278157015)
XLA Ops:
  0.7 8.0 constant_dynamic-slice_fusion.1
  8.6 5.7 copy.147
  17.3 6.4 dynamic-slice_bitcast_fusion.3
  28.2 5.6 copy.146
  35.0 40.1 %collective-permute-done.1 = f32[32,128,128]{2,1,0:T(8,128)} collective-permute-done((f32[32,128,128]{2,1,0:T(8,128)}, f32[32,128,128]{2,1,0:T(8,128)}, u32[]{:S(2)}, u32[]{:S(2)}) %collective-permute-start.1) | collective-permute-done | bytes 2097184 | tf_op jit(solution)/shard_map/ppermute | solution.py:20
  75.7 44.4 %collective-permute-done.2 = f32[32,128,128]{2,1,0:T(8,128)} collective-permute-done((f32[32,128,128]{2,1,0:T(8,128)}, f32[32,128,128]{2,1,0:T(8,128)}, u32[]{:S(2)}, u32[]{:S(2)}) %collective-permute-start.2) | collective-permute-done | bytes 2097184 | tf_op jit(solution)/shard_map/ppermute | solution.py:20
  121.5 43.6 %collective-permute-done.9 = f32[32,128,128]{2,1,0:T(8,128)} collective-permute-done((f32[32,128,128]{2,1,0:T(8,128)}, f32[32,128,128]{2,1,0:T(8,128)}, u32[]{:S(2)}, u32[]{:S(2)}) %collective-permute-start.9) | collective-permute-done | bytes 2097184 | tf_op jit(solution)/shard_map/ppermute | solution.py:20
  165.3 6.5 fusion.14
  174.2 34.5 %collective-permute-done.8 = f32[32,128,128]{2,1,0:T(8,128)} collective-permute-done((f32[32,128,128]{2,1,0:T(8,128)S(1)}, f32[32,128,128]{2,1,0:T(8,128)}, u32[]{:S(2)}, u32[]{:S(2)}) %collective-permute-start.8) | collective-permute-done | bytes 2097184 | tf_op jit(solution)/shard_map/ppermute | solution.py:20
  215.5 5.6 copy.26
  225.8 5.6 copy.40
  233.4 7.8 fusion.50
  245.9 6.3 fusion.86
  252.2 5.2 fusion.60
  257.4 6.5 fusion.80
  263.9 83.5 %collective-permute-done.7 = f32[32,128,128]{2,1,0:T(8,128)} collective-permute-done((f32[32,128,128]{2,1,0:T(8,128)}, f32[32,128,128]{2,1,0:T(8,128)}, u32[]{:S(2)}, u32[]{:S(2)}) %collective-permute-start.7) | collective-permute-done | bytes 2097184 | tf_op jit(solution)/shard_map/ppermute | solution.py:111
  352.2 5.6 copy.31
  357.8 32.4 %collective-permute-done.12 = f32[32,128,128]{2,1,0:T(8,128)} collective-permute-done((f32[32,128,128]{2,1,0:T(8,128)}, f32[32,128,128]{2,1,0:T(8,128)}, u32[]{:S(2)}, u32[]{:S(2)}) %collective-permute-start.12) | collective-permute-done | bytes 2097184 | tf_op jit(solution)/shard_map/ppermute | solution.py:111
  395.0 5.7 copy.44
  405.5 6.9 fusion.46
  416.9 6.9 fusion.56
  428.4 16.3 %fusion.44 = f32[2,128,128,128,1]{3,1,4,2,0:T(8,128)} fusion(f32[2,64,128,128]{3,2,1,0:T(8,128)S(1)} %fusion.89, f32[1,2,64,128]{3,2,1,0:T(8,128)S(1)} %get-tuple-element.39, f32[1,2,64,128]{3,2,1,0:T(8,128)S(1)} %get-tuple-element.38), kind=kOutput, calls=%fused_computation.59 | convolution fusion | flops 3221258240 | bytes 25296896 | tf_op jit(solution)/shard_map/czyx,cdzk->dkyx/dot_general | solution.py:129
  444.7 16.2 %fusion.54 = f32[2,128,128,128,1]{3,1,4,2,0:T(8,128)} fusion(f32[2,64,128,128]{3,2,1,0:T(8,128)S(1)} %fusion.83, f32[1,2,64,128]{3,2,1,0:T(8,128)S(1)} %get-tuple-element.39, f32[1,2,64,128]{3,2,1,0:T(8,128)S(1)} %get-tuple-element.38), kind=kOutput, calls=%fused_computation.69 | convolution fusion | flops 3221258240 | bytes 25296896 | tf_op jit(solution)/shard_map/czyx,cdzk->dkyx/dot_general | solution.py:129
  460.9 23.2 %fusion.4 = f32[2,128,128,128]{3,1,2,0:T(8,128)} fusion(f32[2,128,128,128,1]{3,1,4,2,0:T(8,128)} %fusion.44, f32[128,128,128]{2,0,1:T(8,128)} %fusion.14, f32[2,64,128,128]{3,2,1,0:T(8,128)} %fusion.86, f32[1,2,64,128]{3,2,0,1:T(8,128)S(1)} %copy-done.13, f32[1,2,64,128]{3,2,0,1:T(8,128)S(1)} %copy-done.12), kind=kOutput, calls=%fused_computation.5 | convolution fusion | flops 3229646848 | bytes 50462720 | tf_op jit(solution)/shard_map/czyx,cdzk->dkyx/dot_general | solution.py:129
  484.1 22.9 %fusion.9 = f32[2,128,128,128]{3,1,2,0:T(8,128)} fusion(f32[2,128,128,128,1]{3,1,4,2,0:T(8,128)} %fusion.54, f32[128,128,128]{2,0,1:T(8,128)} %fusion.14, f32[2,64,128,128]{3,2,1,0:T(8,128)} %fusion.80, f32[1,2,64,128]{3,2,0,1:T(8,128)S(1)} %copy-done.13, f32[1,2,64,128]{3,2,0,1:T(8,128)S(1)} %copy-done.12), kind=kOutput, calls=%fused_computation.11 | convolution fusion | flops 3229646848 | bytes 50462720 | tf_op jit(solution)/shard_map/czyx,cdzk->dkyx/dot_general | solution.py:129
  507.0 12.1 %fusion.101 = f32[2,64,128,128,1]{3,1,2,0,4:T(8,128)} fusion(f32[2,128,128,128]{3,1,2,0:T(8,128)} %fusion.4, f32[1,2,128,64]{2,3,0,1:T(8,128)S(1)} %copy-done.15, f32[1,2,128,64]{2,3,0,1:T(8,128)S(1)} %copy-done.14), kind=kOutput, calls=%fused_computation.106 | convolution fusion | flops 3221291008 | bytes 25296896 | tf_op jit(solution)/shard_map/czyx,cdzk->dkyx/dot_general | solution.py:129
  520.6 9.3 fusion.95
  529.9 12.3 %fusion.38 = f32[2,128,64,128,1]{3,1,4,0,2:T(8,128)S(1)} fusion(f32[2,64,128,128,1]{3,1,2,0,4:T(8,128)} %fusion.101, f32[2,2,128,128]{2,3,1,0:T(8,128)S(1)} %copy-done.9), kind=kOutput, calls=%fused_computation.53 | convolution fusion | flops 3221225472 | bytes 17039360 | tf_op jit(solution)/shard_map/czyx,cdyk->dzkx/dot_general | solution.py:129
  542.2 13.9 %fusion.40 = f32[2,128,64,128,1]{3,1,4,0,2:T(8,128)} fusion(f32[2,64,128,128,1]{3,1,2,0,4:T(8,128)S(1)} %copy-done.5, f32[2,2,128,128]{2,3,1,0:T(8,128)S(1)} %copy-done.9), kind=kOutput, calls=%fused_computation.55 | convolution fusion | flops 3221225472 | bytes 17039360 | tf_op jit(solution)/shard_map/czyx,cdyk->dzkx/dot_general | solution.py:129
  556.2 6.3 fusion.24
  562.5 18.9 %fusion.36 = (f32[64,128,128]{1,2,0:T(8,128)}, f32[64,128,128]{1,2,0:T(8,128)}, f32[2,64,128,128]{2,3,1,0:T(8,128)}) fusion(f32[2,64,128,128]{2,3,1,0:T(8,128)S(1)} %bitcast.352, f32[2,128,64,128,1]{3,1,4,2,0:T(8,128)} %fusion.24, f32[64,128,128]{1,2,0:T(8,128)} %copy.44, f32[64,128,128]{1,2,0:T(8,128)} %copy.31, f32[2,128,64,128,1]{3,1,4,0,2:T(8,128)} %fusion.40, ...), kind=kOutput, calls=%fused_computation.49 | convolution fusion | flops 3233808384 | bytes 50593792 | tf_op jit(solution)/shard_map/czyx,cdxk->dzyk/dot_general | solution.py:129
  582.1 9.3 fusion.98
  591.4 9.5 fusion.92
  602.3 8.6 fusion.42
  615.5 6.3 fusion.28
  621.9 13.9 %fusion.52 = f32[2,128,64,128,1]{3,1,4,0,2:T(8,128)} fusion(f32[2,64,128,128,1]{3,1,2,0,4:T(8,128)S(1)} %fusion.92, f32[2,2,128,128]{2,3,1,0:T(8,128)S(1)} %copy-done.9), kind=kOutput, calls=%fused_computation.67 | convolution fusion | flops 3221225472 | bytes 17039360 | tf_op jit(solution)/shard_map/czyx,cdyk->dzkx/dot_general | solution.py:129
  635.7 22.9 %fusion.37 = (f32[64,128,128]{1,2,0:T(8,128)}, f32[64,128,128]{1,2,0:T(8,128)}, f32[2,64,128,128]{2,3,1,0:T(8,128)}) fusion(f32[2,32,128,128]{2,3,1,0:T(8,128)} %collective-permute-done, f32[2,32,128,128]{2,3,1,0:T(8,128)S(1)} %copy-done.2, f32[2,128,64,128,1]{3,1,4,2,0:T(8,128)} %fusion.28, f32[64,128,128]{1,2,0:T(8,128)} %copy.40, ...), kind=kOutput, calls=%fused_computation.52 | convolution fusion | flops 3235905536 | bytes 50593792 | tf_op jit(solution)/shard_map/czyx,cdxk->dzyk/dot_general | solution.py:129
  661.8 13.3 %collective-permute-done.16 = f32[64,128,128]{1,2,0:T(8,128)} collective-permute-done((f32[64,128,128]{1,2,0:T(8,128)}, f32[64,128,128]{1,2,0:T(8,128)}, u32[]{:S(2)}, u32[]{:S(2)}) %collective-permute-start.16) | collective-permute-done | bytes 4194336 | tf_op jit(solution)/shard_map/ppermute | solution.py:111
  680.1 82.0 %collective-permute-done.18 = f32[64,128,128]{1,2,0:T(8,128)} collective-permute-done((f32[64,128,128]{1,2,0:T(8,128)}, f32[64,128,128]{1,2,0:T(8,128)}, u32[]{:S(2)}, u32[]{:S(2)}) %collective-permute-start.18) | collective-permute-done | bytes 4194336 | tf_op jit(solution)/shard_map/ppermute | solution.py:111
  777.5 6.6 fusion.75
  784.1 37.6 %collective-permute-done.17 = f32[32,128,128]{1,2,0:T(8,128)S(1)} collective-permute-done((f32[32,128,128]{1,2,0:T(8,128)}, f32[32,128,128]{1,2,0:T(8,128)S(1)}, u32[]{:S(2)}, u32[]{:S(2)}) %collective-permute-start.17) | collective-permute-done | bytes 2097184 | tf_op jit(solution)/shard_map/ppermute | solution.py:20
  821.7 45.0 %collective-permute-done.19 = f32[32,128,128]{1,2,0:T(8,128)} collective-permute-done((f32[32,128,128]{1,2,0:T(8,128)}, f32[32,128,128]{1,2,0:T(8,128)}, u32[]{:S(2)}, u32[]{:S(2)}) %collective-permute-start.19) | collective-permute-done | bytes 2097184 | tf_op jit(solution)/shard_map/ppermute | solution.py:20
  866.8 44.9 %collective-permute-done.21 = f32[32,128,128]{1,2,0:T(8,128)} collective-permute-done((f32[32,128,128]{1,2,0:T(8,128)}, f32[32,128,128]{1,2,0:T(8,128)}, u32[]{:S(2)}, u32[]{:S(2)}) %collective-permute-start.21) | collective-permute-done | bytes 2097184 | tf_op jit(solution)/shard_map/ppermute | solution.py:20
  911.7 44.1 %collective-permute-done.23 = f32[32,128,128]{1,2,0:T(8,128)} collective-permute-done((f32[32,128,128]{1,2,0:T(8,128)}, f32[32,128,128]{1,2,0:T(8,128)}, u32[]{:S(2)}, u32[]{:S(2)}) %collective-permute-start.23) | collective-permute-done | bytes 2097184 | tf_op jit(solution)/shard_map/ppermute | solution.py:20
  955.8 8.7 maximum_select_fusion.1
  964.5 8.9 copy.63
  973.4 9.7 maximum_select_fusion
  983.1 8.9 copy.62
  (117 shorter events, 86.6 us)
Async XLA Ops:
  14.3 157.5 %collective-permute-start.4 = (f32[2,32,128,128]{2,3,1,0:T(8,128)}, f32[2,32,128,128]{2,3,1,0:T(8,128)}, u32[]{:S(2)}, u32[]{:S(2)}) collective-permute-start(f32[2,32,128,128]{2,3,1,0:T(8,128)} %copy.147), channel_id=1, source_target_pairs={{0,2},{1,3},{2,0},{3,1},{4,6},{5,7},{6,4},{7,5},{8,10},{9,11},{10,... | collective-permute-start | bytes 12582920 | tf_op jit(solution)/shard_map/ppermute | solution.py:111
  23.7 51.5 %collective-permute-start.1 = (f32[32,128,128]{2,1,0:T(8,128)}, f32[32,128,128]{2,1,0:T(8,128)}, u32[]{:S(2)}, u32[]{:S(2)}) collective-permute-start(f32[32,128,128]{2,1,0:T(8,128)} %get-tuple-element.14), channel_id=1, source_target_pairs={{28,0},{0,4},{4,8},{8,12},{12,16},{16,20},{20,24},{24,28},{29,1},{... | collective-permute-start | bytes 6291464 | tf_op jit(solution)/shard_map/ppermute | solution.py:20
  25.2 94.9 %collective-permute-start.2 = (f32[32,128,128]{2,1,0:T(8,128)}, f32[32,128,128]{2,1,0:T(8,128)}, u32[]{:S(2)}, u32[]{:S(2)}) collective-permute-start(f32[32,128,128]{2,1,0:T(8,128)} %get-tuple-element.15), channel_id=1, source_target_pairs={{28,0},{0,4},{4,8},{8,12},{12,16},{16,20},{20,24},{24,28},{29,1},{... | collective-permute-start | bytes 6291464 | tf_op jit(solution)/shard_map/ppermute | solution.py:20
  26.7 138.4 %collective-permute-start.9 = (f32[32,128,128]{2,1,0:T(8,128)}, f32[32,128,128]{2,1,0:T(8,128)}, u32[]{:S(2)}, u32[]{:S(2)}) collective-permute-start(f32[32,128,128]{2,1,0:T(8,128)} %get-tuple-element.16), channel_id=1, source_target_pairs={{28,0},{0,4},{4,8},{8,12},{12,16},{16,20},{20,24},{24,28},{29,1},{... | collective-permute-start | bytes 6291464 | tf_op jit(solution)/shard_map/ppermute | solution.py:20
  33.9 198.1 %collective-permute-start = (f32[2,32,128,128]{2,3,1,0:T(8,128)}, f32[2,32,128,128]{2,3,1,0:T(8,128)}, u32[]{:S(2)}, u32[]{:S(2)}) collective-permute-start(f32[2,32,128,128]{2,3,1,0:T(8,128)} %copy.146), channel_id=1, source_target_pairs={{0,1},{1,0},{2,3},{3,2},{4,5},{5,4},{6,7},{7,6},{8,9},{9,8},{10,11... | collective-permute-start | bytes 12582920 | tf_op jit(solution)/shard_map/ppermute | solution.py:111
  75.2 133.5 %collective-permute-start.8 = (f32[32,128,128]{2,1,0:T(8,128)S(1)}, f32[32,128,128]{2,1,0:T(8,128)}, u32[]{:S(2)}, u32[]{:S(2)}) collective-permute-start(f32[32,128,128]{2,1,0:T(8,128)S(1)} %get-tuple-element.17), channel_id=1, source_target_pairs={{28,0},{0,4},{4,8},{8,12},{12,16},{16,20},{20,24},{24,28},{29,1},{... | collective-permute-start | bytes 6291464 | tf_op jit(solution)/shard_map/ppermute | solution.py:20
  120.1 89.1 %collective-permute-start.3 = (f32[32,128,128]{2,1,0:T(8,128)}, f32[32,128,128]{2,1,0:T(8,128)}, u32[]{:S(2)}, u32[]{:S(2)}) collective-permute-start(f32[32,128,128]{2,1,0:T(8,128)} %collective-permute-done.2), channel_id=1, source_target_pairs={{0,1},{1,0},{2,3},{3,2},{4,5},{5,4},{6,7},{7,6},{8,9},{9,8},{10,11... | collective-permute-start | bytes 6291464 | tf_op jit(solution)/shard_map/ppermute | solution.py:111
  165.1 56.0 %collective-permute-start.10 = (f32[32,128,128]{2,1,0:T(8,128)}, f32[32,128,128]{2,1,0:T(8,128)}, u32[]{:S(2)}, u32[]{:S(2)}) collective-permute-start(f32[32,128,128]{2,1,0:T(8,128)} %collective-permute-done.9), channel_id=1, source_target_pairs={{0,1},{1,0},{2,3},{3,2},{4,5},{5,4},{6,7},{7,6},{8,9},{9,8},{10,11... | collective-permute-start | bytes 6291464 | tf_op jit(solution)/shard_map/ppermute | solution.py:111
  171.8 228.8 %collective-permute-start.5 = (f32[2,32,128,128]{2,3,1,0:T(8,128)}, f32[2,32,128,128]{2,3,1,0:T(8,128)}, u32[]{:S(2)}, u32[]{:S(2)}) collective-permute-start(f32[2,32,128,128]{2,3,1,0:T(8,128)} %collective-permute-done.4), channel_id=1, source_target_pairs={{0,1},{1,0},{2,3},{3,2},{4,5},{5,4},{6,7},{7,6},{8,9},{9,8},{10,11... | collective-permute-start | bytes 12582920 | tf_op jit(solution)/shard_map/ppermute | solution.py:111
  208.7 55.2 %collective-permute-start.6 = (f32[32,128,128]{2,1,0:T(8,128)}, f32[32,128,128]{2,1,0:T(8,128)}, u32[]{:S(2)}, u32[]{:S(2)}) collective-permute-start(f32[32,128,128]{2,1,0:T(8,128)} %collective-permute-done.1), channel_id=1, source_target_pairs={{0,2},{1,3},{2,0},{3,1},{4,6},{5,7},{6,4},{7,5},{8,10},{9,11},{10,... | collective-permute-start | bytes 6291464 | tf_op jit(solution)/shard_map/ppermute | solution.py:111
  209.2 148.6 %collective-permute-start.11 = (f32[32,128,128]{2,1,0:T(8,128)}, f32[32,128,128]{2,1,0:T(8,128)}, u32[]{:S(2)}, u32[]{:S(2)}) collective-permute-start(f32[32,128,128]{2,1,0:T(8,128)} %collective-permute-done.8), channel_id=1, source_target_pairs={{0,2},{1,3},{2,0},{3,1},{4,6},{5,7},{6,4},{7,5},{8,10},{9,11},{10,... | collective-permute-start | bytes 6291464 | tf_op jit(solution)/shard_map/ppermute | solution.py:111
  231.4 116.0 %collective-permute-start.7 = (f32[32,128,128]{2,1,0:T(8,128)}, f32[32,128,128]{2,1,0:T(8,128)}, u32[]{:S(2)}, u32[]{:S(2)}) collective-permute-start(f32[32,128,128]{2,1,0:T(8,128)} %collective-permute-done.3), channel_id=1, source_target_pairs={{0,2},{1,3},{2,0},{3,1},{4,6},{5,7},{6,4},{7,5},{8,10},{9,11},{10,... | collective-permute-start | bytes 6291464 | tf_op jit(solution)/shard_map/ppermute | solution.py:111
  232.0 158.2 %collective-permute-start.12 = (f32[32,128,128]{2,1,0:T(8,128)}, f32[32,128,128]{2,1,0:T(8,128)}, u32[]{:S(2)}, u32[]{:S(2)}) collective-permute-start(f32[32,128,128]{2,1,0:T(8,128)} %collective-permute-done.10), channel_id=1, source_target_pairs={{0,2},{1,3},{2,0},{3,1},{4,6},{5,7},{6,4},{7,5},{8,10},{9,11},{10,... | collective-permute-start | bytes 6291464 | tf_op jit(solution)/shard_map/ppermute | solution.py:111
  245.9 6.3 copy-start.1
  245.9 6.3 copy-start.3
  400.6 4.9 copy-start.4
  405.5 11.3 %slice-start = ((s8[8388608]{0:T(1024)(128)(4,1)}), s8[4194304]{0:T(1024)(128)(4,1)S(1)}, s32[]{:S(2)}) async-start(s8[8388608]{0:T(1024)(128)(4,1)} %bitcast.349), calls=%async_computation | async-start | bytes 8388608
  412.4 4.5 slice-start.1
  444.7 16.2 %copy-start.12 = (f32[1,2,64,128]{3,2,0,1:T(8,128)S(1)}, f32[1,2,64,128]{3,2,0,1:T(8,128)}, u32[]{:S(2)}) copy-start(f32[1,2,64,128]{3,2,0,1:T(8,128)} %get-tuple-element.36) | copy-start | bytes 196612
  444.7 16.2 %copy-start.13 = (f32[1,2,64,128]{3,2,0,1:T(8,128)S(1)}, f32[1,2,64,128]{3,2,0,1:T(8,128)}, u32[]{:S(2)}) copy-start(f32[1,2,64,128]{3,2,0,1:T(8,128)} %get-tuple-element.37) | copy-start | bytes 196612
  484.1 22.9 %copy-start.14 = (f32[1,2,128,64]{2,3,0,1:T(8,128)S(1)}, f32[1,2,128,64]{2,3,0,1:T(8,128)}, u32[]{:S(2)}) copy-start(f32[1,2,128,64]{2,3,0,1:T(8,128)} %get-tuple-element.34) | copy-start | bytes 196612
  484.1 22.9 %copy-start.15 = (f32[1,2,128,64]{2,3,0,1:T(8,128)S(1)}, f32[1,2,128,64]{2,3,0,1:T(8,128)}, u32[]{:S(2)}) copy-start(f32[1,2,128,64]{2,3,0,1:T(8,128)} %get-tuple-element.35) | copy-start | bytes 196612
  507.0 13.6 %copy-start = (f32[2,128,128,128]{3,1,2,0:T(8,128)S(1)}, f32[2,128,128,128]{3,1,2,0:T(8,128)}, u32[]{:S(2)}) copy-start(f32[2,128,128,128]{3,1,2,0:T(8,128)} %fusion.9) | copy-start | bytes 50331652
  520.6 9.3 copy-start.9
  529.9 12.3 %copy-start.5 = (f32[2,64,128,128,1]{3,1,2,0,4:T(8,128)S(1)}, f32[2,64,128,128,1]{3,1,2,0,4:T(8,128)}, u32[]{:S(2)}) copy-start(f32[2,64,128,128,1]{3,1,2,0,4:T(8,128)} %fusion.95) | copy-start | bytes 25165828
  542.2 14.0 %copy-start.8 = (f32[2,2,128,128,1]{2,3,1,0,4:T(8,128)S(1)}, f32[2,2,128,128,1]{2,3,1,0,4:T(8,128)}, u32[]{:S(2)}) copy-start(f32[2,2,128,128,1]{2,3,1,0,4:T(8,128)} %get-tuple-element.24) | copy-start | bytes 786436
  542.2 20.3 %slice-start.2 = ((s8[8388608]{0:T(1024)(128)(4,1)}), s8[4194304]{0:T(1024)(128)(4,1)S(1)}, s32[]{:S(2)}) async-start(s8[8388608]{0:T(1024)(128)(4,1)} %bitcast.351), calls=%async_computation.2 | async-start | bytes 8388608
  556.2 6.3 slice-start.3
  562.5 19.6 %copy-start.10 = (f32[1,2,128,64]{2,3,1,0:T(8,128)S(1)}, f32[1,2,128,64]{2,3,1,0:T(8,128)}, u32[]{:S(2)}) copy-start(f32[1,2,128,64]{2,3,1,0:T(8,128)} %get-tuple-element.32) | copy-start | bytes 196612
  562.5 19.6 %copy-start.11 = (f32[1,2,128,64]{2,3,1,0:T(8,128)S(1)}, f32[1,2,128,64]{2,3,1,0:T(8,128)}, u32[]{:S(2)}) copy-start(f32[1,2,128,64]{2,3,1,0:T(8,128)} %get-tuple-element.33) | copy-start | bytes 196612
  581.4 93.8 %collective-permute-start.16 = (f32[64,128,128]{1,2,0:T(8,128)}, f32[64,128,128]{1,2,0:T(8,128)}, u32[]{:S(2)}, u32[]{:S(2)}) collective-permute-start(f32[64,128,128]{1,2,0:T(8,128)} %get-tuple-element.8), channel_id=1, source_target_pairs={{0,2},{1,3},{2,0},{3,1},{4,6},{5,7},{6,4},{7,5},{8,10},{9,11},{10,... | collective-permute-start | bytes 12582920 | tf_op jit(solution)/shard_map/ppermute | solution.py:111
  600.9 161.1 %collective-permute-start.18 = (f32[64,128,128]{1,2,0:T(8,128)}, f32[64,128,128]{1,2,0:T(8,128)}, u32[]{:S(2)}, u32[]{:S(2)}) collective-permute-start(f32[64,128,128]{1,2,0:T(8,128)} %get-tuple-element.9), channel_id=1, source_target_pairs={{0,2},{1,3},{2,0},{3,1},{4,6},{5,7},{6,4},{7,5},{8,10},{9,11},{10,... | collective-permute-start | bytes 12582920 | tf_op jit(solution)/shard_map/ppermute | solution.py:111
  615.5 151.4 %collective-permute-start.14 = (f32[2,32,128,128]{2,3,1,0:T(8,128)}, f32[2,32,128,128]{2,3,1,0:T(8,128)}, u32[]{:S(2)}, u32[]{:S(2)}) collective-permute-start(f32[2,32,128,128]{2,3,1,0:T(8,128)} %slice.35), channel_id=1, source_target_pairs={{0,1},{1,0},{2,3},{3,2},{4,5},{5,4},{6,7},{7,6},{8,9},{9,8},{10,11... | collective-permute-start | bytes 12582920 | tf_op jit(solution)/shard_map/ppermute | solution.py:111
  621.9 13.9 %copy-start.2 = (f32[2,32,128,128]{2,3,1,0:T(8,128)S(1)}, f32[2,32,128,128]{2,3,1,0:T(8,128)}, u32[]{:S(2)}) copy-start(f32[2,32,128,128]{2,3,1,0:T(8,128)} %copy.146) | copy-start | bytes 12582916
  658.6 16.5 %copy-start.7 = (f32[64,128,128]{1,2,0:T(8,128)S(1)}, f32[64,128,128]{1,2,0:T(8,128)}, u32[]{:S(2)}) copy-start(f32[64,128,128]{1,2,0:T(8,128)} %get-tuple-element.10) | copy-start | bytes 12582916
  661.3 112.9 %collective-permute-start.13 = (f32[2,32,128,128]{2,3,1,0:T(8,128)S(1)}, f32[2,32,128,128]{2,3,1,0:T(8,128)}, u32[]{:S(2)}, u32[]{:S(2)}) collective-permute-start(f32[2,32,128,128]{2,3,1,0:T(8,128)S(1)} %slice.33), channel_id=1, source_target_pairs={{0,1},{1,0},{2,3},{3,2},{4,5},{5,4},{6,7},{7,6},{8,9},{9,8},{10,11... | collective-permute-start | bytes 12582920 | tf_op jit(solution)/shard_map/ppermute | solution.py:111
  675.2 86.9 %copy-start.6 = (f32[64,128,128]{1,2,0:T(8,128)S(1)}, f32[64,128,128]{1,2,0:T(8,128)}, u32[]{:S(2)}) copy-start(f32[64,128,128]{1,2,0:T(8,128)} %get-tuple-element.11) | copy-start | bytes 12582916
  680.1 95.5 %collective-permute-start.20 = (f32[32,128,128]{1,2,0:T(8,128)S(1)}, f32[32,128,128]{1,2,0:T(8,128)}, u32[]{:S(2)}, u32[]{:S(2)}) collective-permute-start(f32[32,128,128]{1,2,0:T(8,128)S(1)} %get-tuple-element.21), channel_id=1, source_target_pairs={{0,1},{1,0},{2,3},{3,2},{4,5},{5,4},{6,7},{7,6},{8,9},{9,8},{10,11... | collective-permute-start | bytes 6291464 | tf_op jit(solution)/shard_map/ppermute | solution.py:111
  762.0 4.9 slice-start.4
  762.0 5.1 slice-start.5
  767.0 9.2 collective-permute-start.22
  772.1 201.2 %collective-permute-start.15 = (f32[2,32,128,128]{2,3,1,0:T(8,128)}, f32[2,32,128,128]{2,3,1,0:T(8,128)}, u32[]{:S(2)}, u32[]{:S(2)}) collective-permute-start(f32[2,32,128,128]{2,3,1,0:T(8,128)} %fusion.74), channel_id=1, source_target_pairs={{0,2},{1,3},{2,0},{3,1},{4,6},{5,7},{6,4},{7,5},{8,10},{9,11},{10,... | collective-permute-start | bytes 12582920 | tf_op jit(solution)/shard_map/ppermute | solution.py:111
  773.0 48.7 %collective-permute-start.17 = (f32[32,128,128]{1,2,0:T(8,128)}, f32[32,128,128]{1,2,0:T(8,128)S(1)}, u32[]{:S(2)}, u32[]{:S(2)}) collective-permute-start(f32[32,128,128]{1,2,0:T(8,128)} %get-tuple-element.20), channel_id=1, source_target_pairs={{4,0},{8,4},{12,8},{16,12},{20,16},{24,20},{28,24},{0,28},{5,1},{9... | collective-permute-start | bytes 6291464 | tf_op jit(solution)/shard_map/ppermute | solution.py:20
  774.2 92.6 %collective-permute-start.19 = (f32[32,128,128]{1,2,0:T(8,128)}, f32[32,128,128]{1,2,0:T(8,128)}, u32[]{:S(2)}, u32[]{:S(2)}) collective-permute-start(f32[32,128,128]{1,2,0:T(8,128)} %get-tuple-element.22), channel_id=1, source_target_pairs={{4,0},{8,4},{12,8},{16,12},{20,16},{24,20},{28,24},{0,28},{5,1},{9... | collective-permute-start | bytes 6291464 | tf_op jit(solution)/shard_map/ppermute | solution.py:20
  775.6 136.1 %collective-permute-start.21 = (f32[32,128,128]{1,2,0:T(8,128)}, f32[32,128,128]{1,2,0:T(8,128)}, u32[]{:S(2)}, u32[]{:S(2)}) collective-permute-start(f32[32,128,128]{1,2,0:T(8,128)} %collective-permute-done.20), channel_id=1, source_target_pairs={{4,0},{8,4},{12,8},{16,12},{20,16},{24,20},{28,24},{0,28},{5,1},{9... | collective-permute-start | bytes 6291464 | tf_op jit(solution)/shard_map/ppermute | solution.py:20
  776.1 179.6 %collective-permute-start.23 = (f32[32,128,128]{1,2,0:T(8,128)}, f32[32,128,128]{1,2,0:T(8,128)}, u32[]{:S(2)}, u32[]{:S(2)}) collective-permute-start(f32[32,128,128]{1,2,0:T(8,128)} %collective-permute-done.22), channel_id=1, source_target_pairs={{4,0},{8,4},{12,8},{16,12},{20,16},{24,20},{28,24},{0,28},{5,1},{9... | collective-permute-start | bytes 6291464 | tf_op jit(solution)/shard_map/ppermute | solution.py:20
where the time goes:
time: 996 us; the launch traced here: 992 us
  waiting for transfers between devices  546 us (55%)
  matrix products  271 us (27%)
  local copies, waits for them, and re-layouts  88 us (9%)
  other arithmetic  66.4 us (7%)
  starting transfers between devices  20.6 us (2%)
    ppermute x8, waiting for transfers between devices, passed_along(): return lax.ppermute(block, axis, route)  334 us
    dot_general x24, matrix products, transform(): return jnp.einsum(equation, values, table, precision=lax.Precision.HIGH)  271 us
    ppermute x16, waiting for transfers between devices, exchanged(): return lax.ppermute(block, 'grid', [(i, i ^ bit) for i in devices])  211 us
    unnamed x49, local copies, waits for them, and re-layouts  35.6 us
  transfers between devices with their start and end apart: 24, of which 12 were waited for; matrix products, arithmetic and copies ran while one was open for 21% of the time, Pallas kernels for 0%

commit v1 on v0

v1 whole, which is shorter than its diff:
```python
import functools
import math

import jax
import jax.numpy as jnp
import numpy as np
from jax import lax
from jax.experimental import pallas as pl
from jax.experimental.pallas import tpu as pltpu
from jax.sharding import PartitionSpec as P


FRACTION = 0.25
HIGHEST_PRECISION = lax.Precision.HIGHEST
CHUNK = 8


def passed_along(block, axis, distance):
    devices = range(lax.axis_size(axis))
    route = [((i - distance) % len(devices), i) for i in devices]
    return lax.ppermute(block, axis, route)


def wave_square(points, first_row, length):
    position = first_row + jnp.arange(points, dtype=jnp.int32)
    return squared_wavenumber(position, length)


def squared_wavenumber(position, length):
    position = (position + length // 2) % length - length // 2
    wavenumber = 2.0 * math.pi / length * position.astype(jnp.float32)
    return wavenumber * wavenumber


def coulomb(square_z, square_y, square_x):
    squared = square_z[:, None, None] + square_y[None, :, None] + square_x[None, None, :]
    safe_square = jnp.where(squared > 0.0, squared, 1.0)
    return jnp.where(squared > 0.0, 4.0 * math.pi / safe_square, 0.0)


def fourier_table(length, inverse):
    position = jnp.arange(length, dtype=jnp.int32)
    phase_turns = position[:, None] * position[None, :] % length
    phase_angle = 2.0 * math.pi / length * phase_turns.astype(jnp.float32)
    cosine = jnp.cos(phase_angle)
    sine_part = jnp.sin(phase_angle)
    norm_factor = 1.0
    if inverse:
        sine_part = -sine_part
        norm_factor = 1.0 / length
    return norm_factor * jnp.stack(
        [jnp.stack([cosine, -sine_part]), jnp.stack([sine_part, cosine])]
    )


def solve_pairs(packed, kernel_slab, nz):
    ny, nx = packed.shape[3:]
    spectrum = jnp.einsum(
        "pczyx,cdxk->dpzyk", packed, fourier_table(nx, False), precision=HIGHEST_PRECISION
    )
    spectrum = jnp.einsum(
        "cpzyx,cdyk->dpzkx", spectrum, fourier_table(ny, False), precision=HIGHEST_PRECISION
    )
    forward_z = fourier_table(nz, False)
    inverse_z = fourier_table(nz, True)
    screened = (
        jnp.einsum(
            "cpzyx,cdzk->dpkyx",
            lax.all_to_all(spectrum, "grid", split_axis=3, concat_axis=2, tiled=True),
            forward_z,
            precision=HIGHEST_PRECISION,
        )
        * kernel_slab
    )
    screened = jnp.einsum("cpzyx,cdzk->dpkyx", screened, inverse_z, precision=HIGHEST_PRECISION)
    planes = lax.all_to_all(screened, "grid", split_axis=2, concat_axis=3, tiled=True)
    planes = jnp.einsum(
        "cpzyx,cdyk->dpzkx", planes, fourier_table(ny, True), precision=HIGHEST_PRECISION
    )
    return jnp.einsum(
        "cpzyx,cdxk->pdzyk", planes, fourier_table(nx, True), precision=HIGHEST_PRECISION
    )


def pair_terms(owned, visitors, kernel_slab, nz):
    count_vis = visitors.shape[0]
    count_own = owned.shape[0]
    density = owned[None] * visitors[:, None]
    packed = density.reshape((count_vis * count_own // 2, 2) + owned.shape[1:])
    potential = solve_pairs(packed, kernel_slab, nz).reshape(density.shape)
    own_part = jnp.sum(potential * visitors[:, None], axis=0)
    partner = jnp.sum(potential * owned[None], axis=1)
    return (own_part, partner)


def body(own_bands, travel_bands):
    depth, ny, nx = own_bands.shape[1:]
    nz = depth * lax.axis_size("grid")
    rows_local = ny // lax.axis_size("grid")
    kernel_slab = coulomb(
        wave_square(nz, 0, nz),
        wave_square(rows_local, lax.axis_index("grid") * rows_local, ny),
        wave_square(nx, 0, nx),
    )
    count_vis = travel_bands.shape[0]
    own_total = jnp.zeros_like(own_bands)
    returned = []
    for visit_index in range(count_vis):
        visitor = passed_along(travel_bands[visit_index : visit_index + 1], "band", 1)
        own_part, partner = pair_terms(own_bands, visitor, kernel_slab, nz)
        own_total = own_total + own_part
        returned.append(passed_along(partner, "band", -1))
    partner_total = jnp.concatenate(returned, axis=0)
    return (-FRACTION * own_total, -FRACTION * partner_total)


def halves(table):
    high = table.astype(jnp.bfloat16)
    return high, (table - high.astype(np.float32)).astype(jnp.bfloat16)


def complex_matrix(length, inverse, left):
    position = np.arange(length)
    angle = 2.0 * np.pi / length * (position[:, None] * position[None, :] % length)
    cosine, sine = np.cos(angle), np.sin(angle)
    if inverse:
        sine = -sine
    matrix = np.block([[cosine, -sine], [sine, cosine]])
    return (matrix.T if left else matrix).astype(np.float32)


def times(value, factor):
    (a, b), (c, d) = value, factor
    if abs(d) < 1e-12:
        return (a, b) if c > 0.5 else (-a, -b)
    if abs(c) < 1e-12:
        return (-b, a) if d > 0.0 else (b, -a)
    if abs(abs(c) - abs(d)) < 1e-12:
        size = abs(c)
        first = a if c > 0 else -a
        other = b if c > 0 else -b
        if (c > 0) == (d > 0):
            return size * (first - other), size * (first + other)
        return size * (first + other), size * (other - first)
    return a * c - b * d, a * d + b * c


def turn(numerator, length, sign):
    angle = 2.0 * math.pi * (numerator % length) / length
    return math.cos(angle), sign * math.sin(angle)


def fourier(values, sign):
    count = len(values)
    if count == 1:
        return values
    half = count // 2
    sums, differences = [], []
    for i in range(half):
        (a, b), (c, d) = values[i], values[i + half]
        sums.append((a + c, b + d))
        differences.append(times((a - c, b - d), turn(i, count, sign)))
    even = fourier(sums, sign)
    odd = fourier(differences, sign)
    return [pair for both in zip(even, odd) for pair in both]


def split(value):
    high = value.astype(jnp.bfloat16)
    return high, (value - high.astype(jnp.float32)).astype(jnp.bfloat16)


def dot(a, b):
    return jnp.dot(a, b, preferred_element_type=jnp.float32)


def product(left, right):
    (a, b), (c, d) = left, right
    return dot(a, c) + dot(b, c) + dot(a, d)


def field_kernel(radix, first_call, rank_ref, *refs):
    refs = list(refs)

    def take(count):
        taken = refs[:count]
        del refs[:count]
        return taken

    own_hbm, vis_hbm = take(4), take(4)
    (weights_hbm,) = take(1)
    tables = take(8)
    before_hbm = [] if first_call else take(2)
    held_hbm, sums_hbm = take(2), take(2)
    own_ref, vis_ref, real_ref, imag_ref, weights_ref, total_ref = take(6)
    own_sem, vis_sem, weights_sem, before_sem, held_sem, sums_sem = refs
    nz, ny, nx = real_ref.shape
    depth = nz // 4
    rank = rank_ref[0]

    def planes(slot):
        return pl.ds(lax.bitwise_xor(rank, slot) * depth, depth)

    own_in, vis_in, before_in, held_out, sums_out = [], [], [], [], []
    for s in range(4):
        own_in.append(
            pltpu.make_async_copy(own_hbm[s], own_ref.at[:, planes(s)], own_sem.at[s])
        )
        vis_in.append(pltpu.make_async_copy(vis_hbm[s], vis_ref.at[planes(s)], vis_sem.at[s]))
    weights_in = pltpu.make_async_copy(weights_hbm, weights_ref, weights_sem)
    for s in range(2):
        part = total_ref.at[:, pl.ds(s * depth, depth)]
        if not first_call:
            before_in.append(pltpu.make_async_copy(before_hbm[s], part, before_sem.at[s]))
        sums_out.append(pltpu.make_async_copy(part, sums_hbm[s], sums_sem.at[s]))
        held_out.append(
            pltpu.make_async_copy(vis_ref.at[planes(s)], held_hbm[s], held_sem.at[s])
        )
    for copy in [c for both in zip(own_in, vis_in) for c in both] + [weights_in] + before_in:
        copy.start()

    def loaded(index):
        return tables[index][...], tables[index + 1][...]

    def forward(z):
        visitor = vis_ref[pl.ds(z, 2)]
        real = (own_ref[0, pl.ds(z, 2)] * visitor).reshape(2 * ny, nx)
        imag = (own_ref[1, pl.ds(z, 2)] * visitor).reshape(2 * ny, nx)
        rows = jnp.concatenate([real, imag], axis=1)
        rows = product(split(rows), loaded(0))
        columns = jnp.concatenate(
            [
                jnp.concatenate([rows[:ny, :nx], rows[ny:, :nx]], axis=1),
                jnp.concatenate([rows[:ny, nx:], rows[ny:, nx:]], axis=1),
            ],
            axis=0,
        )
        columns = product(loaded(2), split(columns))
        for i in (0, 1):
            real_ref[z + i] = columns[:ny, i * nx : (i + 1) * nx]
            imag_ref[z + i] = columns[ny:, i * nx : (i + 1) * nx]

    def backward(z, kept):
        columns = jnp.concatenate(
            [
                jnp.concatenate([ref[z], ref[z + 1]], axis=1)
                for ref in (real_ref, imag_ref)
            ],
            axis=0,
        )
        columns = product(loaded(4), split(columns))
        rows = jnp.concatenate(
            [
                jnp.concatenate([columns[:ny, :nx], columns[ny:, :nx]], axis=1),
                jnp.concatenate([columns[:ny, nx:], columns[ny:, nx:]], axis=1),
            ],
            axis=0,
        )
        rows = product(split(rows), loaded(6))
        real = rows[:, :nx].reshape(2, ny, nx)
        imag = rows[:, nx:].reshape(2, ny, nx)
        visitor = vis_ref[pl.ds(z, 2)]
        vis_ref[pl.ds(z, 2)] = real * own_ref[0, pl.ds(z, 2)] + imag * own_ref[1, pl.ds(z, 2)]
        for i, part in enumerate((real, imag)):
            part = part * visitor
            if not first_call:
                part = part + total_ref[i, pl.ds(kept, 2)]
            total_ref[i, pl.ds(kept, 2)] = part

    def tile(index, carry):
        here = pl.ds(pl.multiple_of(8 * index, 8), 8)
        outer = nz // radix

        def load(z):
            return real_ref[z, here, :], imag_ref[z, here, :]

        def store(z, value):
            real_ref[z, here, :], imag_ref[z, here, :] = value

        for fine in range(radix):
            values = fourier([load(radix * n + fine) for n in range(outer)], -1.0)
            for k, value in enumerate(values):
                store(radix * k + fine, times(value, turn(fine * k, nz, -1.0)))
        for k in range(outer):
            values = fourier([load(radix * k + n) for n in range(radix)], -1.0)
            for n, (a, b) in enumerate(values):
                weight = weights_ref[radix * k + n, here, :]
                values[n] = (a * weight, b * weight)
            for n, value in enumerate(fourier(values, 1.0)):
                store(radix * k + n, value)
        for fine in range(radix):
            values = [times(load(radix * k + fine), turn(fine * k, nz, 1.0)) for k in range(outer)]
            for n, value in enumerate(fourier(values, 1.0)):
                store(radix * n + fine, value)
        return carry

    def forward_slot(s, carry):
        here = planes(s)
        pltpu.make_async_copy(own_hbm[0], own_ref.at[:, here], own_sem.at[s]).wait()
        pltpu.make_async_copy(vis_hbm[0], vis_ref.at[here], vis_sem.at[s]).wait()
        base = lax.bitwise_xor(rank, s) * depth

        def forward_chunk(chunk, carry):
            for pair in range(CHUNK // 2):
                forward(base + chunk * CHUNK + 2 * pair)
            return carry

        return lax.fori_loop(0, depth // CHUNK, forward_chunk, carry)

    lax.fori_loop(0, 4, forward_slot, 0)
    weights_in.wait()
    lax.fori_loop(0, ny // 8, tile, 0)
    for s in (1, 0):
        if not first_call:
            before_in[s].wait()
        base = lax.bitwise_xor(rank, s) * depth

        def backward_chunk(chunk, carry):
            for pair in range(CHUNK // 2):
                offset = chunk * CHUNK + 2 * pair
                backward(base + offset, s * depth + offset)
            return carry

        lax.fori_loop(0, depth // CHUNK, backward_chunk, 0)
        held_out[s].start()
        sums_out[s].start()
    for copy in held_out + sums_out:
        copy.wait()


def solve_field(rank, owned, visitor, weights, tables, before):
    depth, ny, nx = visitor[0].shape
    nz = 4 * depth
    first_call = before is None
    operands = list(owned) + list(visitor) + [weights] + list(tables)
    anywhere = pl.BlockSpec(memory_space=pl.ANY)
    in_specs = [pl.BlockSpec(memory_space=pltpu.SMEM)] + [anywhere] * 9
    in_specs += [pl.BlockSpec(memory_space=pltpu.VMEM)] * 8
    if not first_call:
        in_specs += [anywhere] * 2
        operands += list(before)
    shapes = [jax.ShapeDtypeStruct(v.shape, v.dtype) for v in visitor[:2]]
    shapes += [jax.ShapeDtypeStruct(v.shape, v.dtype) for v in owned[:2]]
    points = nz * ny * nx
    grid = pltpu.VMEM((nz, ny, nx), jnp.float32)
    results = pl.pallas_call(
        functools.partial(field_kernel, 8, first_call),
        out_shape=shapes,
        in_specs=in_specs,
        out_specs=[anywhere] * 4,
        scratch_shapes=[
            pltpu.VMEM((2, nz, ny, nx), jnp.float32),
            grid,
            grid,
            grid,
            grid,
            pltpu.VMEM((2, 2 * depth, ny, nx), jnp.float32),
            pltpu.SemaphoreType.DMA((4,)),
            pltpu.SemaphoreType.DMA((4,)),
            pltpu.SemaphoreType.DMA,
            pltpu.SemaphoreType.DMA((2,)),
            pltpu.SemaphoreType.DMA((2,)),
            pltpu.SemaphoreType.DMA((2,)),
        ],
        compiler_params=pltpu.CompilerParams(vmem_limit_bytes=67043328),
        cost_estimate=pl.CostEstimate(
            flops=2 * points * 3 * 4 * nx, bytes_accessed=4 * points * 10, transcendentals=0
        ),
        name="solve_field",
    )(rank, *operands)
    return results[:2], results[2:]


def exchanged(block, bit):
    devices = range(lax.axis_size("grid"))
    return lax.ppermute(block, "grid", [(i, i ^ bit) for i in devices])


def picked(bands, first, count):
    return lax.dynamic_slice_in_dim(bands, first, count, 0)


def square_body(own_bands, travel_bands):
    rank = lax.axis_index("grid")
    core = rank % 2
    half_own = own_bands.shape[0] // 2
    count_vis = travel_bands.shape[0]
    depth, ny, nx = own_bands.shape[1:]
    nz = depth * lax.axis_size("grid")

    own_mine = picked(own_bands, core * half_own, half_own)
    own_far = exchanged(own_mine, 2)
    own_bands, travel_bands, _ = lax.optimization_barrier((own_bands, travel_bands, own_mine))
    own_side = exchanged(picked(own_bands, (1 - core) * half_own, half_own), 1)
    own_cross = exchanged(own_side, 2)
    owned = [own_mine, own_side, own_far, own_cross]

    visitors = []
    for j in range(count_vis):
        near = passed_along(travel_bands[j], "band", 1)
        far = exchanged(near, 2)
        side = exchanged(near, 1)
        cross = exchanged(far, 1)
        visitors.append([near, side, far, cross])

    radix = 8
    slot = jnp.arange(nz, dtype=jnp.int32)
    z_of_slot = slot // radix + (nz // radix) * (slot % radix)
    weights = (-FRACTION / (nz * ny * nx)) * coulomb(
        squared_wavenumber(z_of_slot, nz), wave_square(ny, 0, ny), wave_square(nx, 0, nx)
    )
    tables = []
    for length, inverse, left in (
        (nx, False, False),
        (ny, False, True),
        (ny, True, True),
        (nx, True, False),
    ):
        tables += halves(complex_matrix(length, inverse, left))
    rank_operand = rank.astype(jnp.int32).reshape(1)

    sums = None
    returned = []
    for j in range(count_vis):
        held, sums = solve_field(rank_operand, owned, visitors[j], weights, tables, sums)
        other = exchanged(held[1], 1)
        returned.append(passed_along(held[0] + other, "band", -1))
    held_rows = jnp.stack(returned)

    own_other = exchanged(sums[1], 1)
    own_rows = jnp.zeros(own_bands.shape, own_bands.dtype)
    own_rows = lax.dynamic_update_slice_in_dim(own_rows, sums[0], core * half_own, 0)
    own_rows = lax.dynamic_update_slice_in_dim(own_rows, own_other, (1 - core) * half_own, 0)
    return own_rows, held_rows


def whole_body(own_bands, travel_bands):
    return square_body(own_bands, travel_bands)


def solution(mesh):
    spec = P("band", "grid", None, None)

    def placed(own_bands, travel_bands):
        group_own = own_bands.shape[0] // mesh.shape["band"]
        group_vis = travel_bands.shape[0] // mesh.shape["band"]
        square = mesh.shape["grid"] == 4 and group_own == 4 and group_vis % 2 == 0
        step = jax.shard_map(
            whole_body if square else body,
            mesh=mesh,
            in_specs=(spec, spec),
            out_specs=(spec, spec),
            check_vma=False,
        )
        return step(own_bands, travel_bands)

    return placed
```

time: 996 us -> 854 us (0.86)
  matrix products: 271 us -> 0 us
  Pallas kernels: 0 us -> 223 us
  local copies, waits for them, and re-layouts: 88 us -> 17.6 us
  other arithmetic: 66.4 us -> 13.6 us
  waiting for transfers between devices: 546 us -> 576 us
    dot_general x24 -> x0, matrix products: 271 us -> none  [transform(): return jnp.einsum(equation, values, table, precision=lax.Precision.HIGH)]
    pallas_call x0 -> x4, Pallas kernels: none -> 223 us  [solve_field(): pl.pallas_call(functools.partial(field_kernel, 8, first_call), out_shape=...]
    unnamed x49 -> x36, local copies, waits for them, and re-layouts: 35.6 us -> 4.24 us
    concatenate x5 -> x0, local copies, waits for them, and re-layouts: 27.3 us -> none  [the longest x2 11.3 us: square_body(): jnp.concatenate([exchanged(mine, 2), exchanged(away, 2)], axis=0)]
    select_n x3 -> x0, other arithmetic: 25 us -> none  [the longest x1 9.74 us: square_body(): jnp.where(chip == 0, jnp.concatenate([own_near, own_back], axis=0), jnp.c...]
    ppermute x16 -> x20, waiting for transfers between devices: 211 us -> 231 us  [exchanged(): return lax.ppermute(block, 'grid', [(i, i ^ bit) for i in devices])]
    concatenate x5 -> x0, other arithmetic: 19.1 us -> none  [the longest x2 9.56 us: square_body(): jnp.concatenate([exchanged(mine, 2), exchanged(away, 2)], axis=0)]
    mul x6 -> x3, other arithmetic: 18.8 us -> 7.11 us  [the longest x1 7.09 us: square_body(): -FRACTION / (nz * ny * nx) * coulomb(squared_wavenumber(z_of_slot, nz), w...]
  transfers between devices with their start and end apart: 24 -> 28, of which waited for: 12 -> 14; matrix products, arithmetic and copies ran while one was open for 21% -> 2% of each run, Pallas kernels for 0% -> 20%
where the time goes in v1:
time: 854 us; the launch traced here: 853 us
  waiting for transfers between devices  576 us (67%)
  Pallas kernels  223 us (26%)
  starting transfers between devices  22.1 us (3%)
  local copies, waits for them, and re-layouts  17.6 us (2%)
  other arithmetic  13.6 us (2%)
    ppermute x8, waiting for transfers between devices, passed_along(): return lax.ppermute(block, axis, route)  345 us
    ppermute x20, waiting for transfers between devices, exchanged(): return lax.ppermute(block, 'grid', [(i, i ^ bit) for i in devices])  231 us
    pallas_call x4, Pallas kernels, solve_field(): pl.pallas_call(functools.partial(field_kernel, 8, first_call), out_shape=...  223 us
  transfers between devices with their start and end apart: 28, of which 14 were waited for; matrix products, arithmetic and copies ran while one was open for 2% of the time, Pallas kernels for 20%

profile of v1, /device:TPU:0, one launch (start us, length us, event | category | flops | bytes accessed | tf_op | source)
XLA Modules:
  0.0 853.4 jit_solution(10096472146245189861)
XLA Ops:
  0.7 5.0 constant_dynamic-slice_fusion.1.refs_0_
  5.6 1.2 copy-done.4
  6.8 3.5 slice_bitcast_fusion
  10.3 3.0 collective-permute-start.15
  13.3 2.6 constant_dynamic-slice_fusion
  16.0 1.6 collective-permute-start.11
  17.6 1.5 collective-permute-start.7
  19.1 1.5 collective-permute-start.1
  20.6 42.4 %collective-permute-done.15.refs_4_ = f32[32,128,128]{2,1,0:T(8,128)S(1)} collective-permute-done((f32[32,128,128]{2,1,0:T(8,128)}, f32[32,128,128]{2,1,0:T(8,128)S(1)}, u32[]{:S(2)}, u32[]{:S(2)}) %collective-permute-start.15) | collective-permute-done | bytes 2097184 | tf_op jit(solution)/shard_map/ppermute | solution.py:21
  63.0 44.9 %collective-permute-done.11.refs_4_ = f32[32,128,128]{2,1,0:T(8,128)S(1)} collective-permute-done((f32[32,128,128]{2,1,0:T(8,128)}, f32[32,128,128]{2,1,0:T(8,128)S(1)}, u32[]{:S(2)}, u32[]{:S(2)}) %collective-permute-start.11) | collective-permute-done | bytes 2097184 | tf_op jit(solution)/shard_map/ppermute | solution.py:21
  108.0 1.7 collective-permute-start.17
  109.6 43.4 %collective-permute-done.7.refs_4_ = f32[32,128,128]{2,1,0:T(8,128)} collective-permute-done((f32[32,128,128]{2,1,0:T(8,128)S(1)}, f32[32,128,128]{2,1,0:T(8,128)}, u32[]{:S(2)}, u32[]{:S(2)}) %collective-permute-start.7) | collective-permute-done | bytes 2097184 | tf_op jit(solution)/shard_map/ppermute | solution.py:21
  153.0 44.1 %collective-permute-done.3.refs_4_ = f32[32,128,128]{2,1,0:T(8,128)} collective-permute-done((f32[32,128,128]{2,1,0:T(8,128)S(1)}, f32[32,128,128]{2,1,0:T(8,128)}, u32[]{:S(2)}, u32[]{:S(2)}) %collective-permute-start.3) | collective-permute-done | bytes 2097184 | tf_op jit(solution)/shard_map/ppermute | solution.py:21
  197.1 1.5 collective-permute-start.13
  198.6 0.5 collective-permute-start.2
  199.2 1.6 collective-permute-start.9
  200.7 0.6 collective-permute-start.5
  201.3 1.9 copy-done.2
  203.2 42.5 %collective-permute-done.13.refs_6_ = f32[32,128,128]{2,1,0:T(8,128)} collective-permute-done((f32[32,128,128]{2,1,0:T(8,128)S(1)}, f32[32,128,128]{2,1,0:T(8,128)}, u32[]{:S(2)}, u32[]{:S(2)}) %collective-permute-start.13) | collective-permute-done | bytes 2097184 | tf_op jit(solution)/shard_map/ppermute | solution.py:376
  245.8 0.6 collective-permute-start.14
  246.4 134.1 %collective-permute-done.9.refs_6_ = f32[32,128,128]{2,1,0:T(8,128)} collective-permute-done((f32[32,128,128]{2,1,0:T(8,128)}, f32[32,128,128]{2,1,0:T(8,128)}, u32[]{:S(2)}, u32[]{:S(2)}) %collective-permute-start.9) | collective-permute-done | bytes 2097184 | tf_op jit(solution)/shard_map/ppermute | solution.py:376
  380.5 43.2 %collective-permute-done.5.refs_6_ = f32[32,128,128]{2,1,0:T(8,128)} collective-permute-done((f32[32,128,128]{2,1,0:T(8,128)}, f32[32,128,128]{2,1,0:T(8,128)}, u32[]{:S(2)}, u32[]{:S(2)}) %collective-permute-start.5) | collective-permute-done | bytes 2097184 | tf_op jit(solution)/shard_map/ppermute | solution.py:376
  423.8 0.5 collective-permute-start.10
  424.4 7.1 fusion.1.refs_8_
  431.5 55.7 %solve_field.4 = (f32[32,128,128]{2,1,0:T(8,128)}, f32[32,128,128]{2,1,0:T(8,128)}, f32[2,32,128,128]{3,2,1,0:T(8,128)}, f32[2,32,128,128]{3,2,1,0:T(8,128)}) custom-call(s32[1]{0:T(128)} %bitcast.rank_ref, f32[2,32,128,128]{3,2,1,0:T(8,128)} %constant_dynamic-slice_fusion.1.refs_0_, f32[2,32,128,128]{3,2,1,0:T(8,128)} %copy-done.1, ...), custom_call_target="tpu_custom_call" | custom-call | flops 6442450944 | bytes 83886080 | tf_op jit(solution)/shard_map/solve_field/pallas_call | solution.py:346
  487.3 55.8 %solve_field.5 = (f32[32,128,128]{2,1,0:T(8,128)}, f32[32,128,128]{2,1,0:T(8,128)}, f32[2,32,128,128]{3,2,1,0:T(8,128)}, f32[2,32,128,128]{3,2,1,0:T(8,128)}) custom-call(s32[1]{0:T(128)} %bitcast.rank_ref, f32[2,32,128,128]{3,2,1,0:T(8,128)} %constant_dynamic-slice_fusion.1.refs_0_, f32[2,32,128,128]{3,2,1,0:T(8,128)} %copy-done.1, ...), custom_call_target="tpu_custom_call" | custom-call | flops 6442450944 | bytes 83886080 | tf_op jit(solution)/shard_map/solve_field/pallas_call | solution.py:346
  543.1 55.9 %solve_field.6 = (f32[32,128,128]{2,1,0:T(8,128)}, f32[32,128,128]{2,1,0:T(8,128)}, f32[2,32,128,128]{3,2,1,0:T(8,128)}, f32[2,32,128,128]{3,2,1,0:T(8,128)}) custom-call(s32[1]{0:T(128)} %bitcast.rank_ref, f32[2,32,128,128]{3,2,1,0:T(8,128)} %constant_dynamic-slice_fusion.1.refs_0_, f32[2,32,128,128]{3,2,1,0:T(8,128)} %copy-done.1, ...), custom_call_target="tpu_custom_call" | custom-call | flops 6442450944 | bytes 83886080 | tf_op jit(solution)/shard_map/solve_field/pallas_call | solution.py:346
  599.0 55.7 %solve_field.7 = (f32[32,128,128]{2,1,0:T(8,128)}, f32[32,128,128]{2,1,0:T(8,128)}, f32[2,32,128,128]{3,2,1,0:T(8,128)}, f32[2,32,128,128]{3,2,1,0:T(8,128)}) custom-call(s32[1]{0:T(128)} %bitcast.rank_ref, f32[2,32,128,128]{3,2,1,0:T(8,128)} %constant_dynamic-slice_fusion.1.refs_0_, f32[2,32,128,128]{3,2,1,0:T(8,128)} %copy-done.1, ...), custom_call_target="tpu_custom_call" | custom-call | flops 6442450944 | bytes 83886080 | tf_op jit(solution)/shard_map/solve_field/pallas_call | solution.py:346
  654.8 0.4 collective-permute-start.19
  655.9 0.3 collective-permute-start.26
  656.2 9.0 %collective-permute-done.20 = f32[32,128,128]{2,1,0:T(8,128)S(1)} collective-permute-done((f32[32,128,128]{2,1,0:T(8,128)}, f32[32,128,128]{2,1,0:T(8,128)S(1)}, u32[]{:S(2)}, u32[]{:S(2)}) %collective-permute-start.20) | collective-permute-done | bytes 2097184 | tf_op jit(solution)/shard_map/ppermute | solution.py:376
  665.2 1.8 add.219
  667.1 1.5 collective-permute-start.21
  668.9 1.5 collective-permute-start.23
  670.3 0.9 collective-permute-done.24
  671.2 0.3 add.221
  671.5 1.5 collective-permute-start.25
  673.1 1.1 collective-permute-done.26
  674.5 1.5 collective-permute-start.27
  676.0 1.0 broadcast_in_dim.11
  677.0 1.1 copy-done.6
  678.2 0.6 constant_dynamic-update-slice_fusion.1
  678.8 0.6 constant_dynamic-update-slice_fusion
  679.5 36.2 %collective-permute-done.21 = f32[32,128,128]{2,1,0:T(8,128)S(1)} collective-permute-done((f32[32,128,128]{2,1,0:T(8,128)S(1)}, f32[32,128,128]{2,1,0:T(8,128)S(1)}, u32[]{:S(2)}, u32[]{:S(2)}) %collective-permute-start.21) | collective-permute-done | bytes 2097184 | tf_op jit(solution)/shard_map/ppermute | solution.py:21
  715.6 44.9 %collective-permute-done.23 = f32[32,128,128]{2,1,0:T(8,128)S(1)} collective-permute-done((f32[32,128,128]{2,1,0:T(8,128)S(1)}, f32[32,128,128]{2,1,0:T(8,128)S(1)}, u32[]{:S(2)}, u32[]{:S(2)}) %collective-permute-start.23) | collective-permute-done | bytes 2097184 | tf_op jit(solution)/shard_map/ppermute | solution.py:21
  760.6 44.9 %collective-permute-done.25 = f32[32,128,128]{2,1,0:T(8,128)S(1)} collective-permute-done((f32[32,128,128]{2,1,0:T(8,128)S(1)}, f32[32,128,128]{2,1,0:T(8,128)S(1)}, u32[]{:S(2)}, u32[]{:S(2)}) %collective-permute-start.25) | collective-permute-done | bytes 2097184 | tf_op jit(solution)/shard_map/ppermute | solution.py:21
  805.5 44.3 %collective-permute-done.27 = f32[32,128,128]{2,1,0:T(8,128)S(1)} collective-permute-done((f32[32,128,128]{2,1,0:T(8,128)S(1)}, f32[32,128,128]{2,1,0:T(8,128)S(1)}, u32[]{:S(2)}, u32[]{:S(2)}) %collective-permute-start.27) | collective-permute-done | bytes 2097184 | tf_op jit(solution)/shard_map/ppermute | solution.py:21
  849.8 3.7 pad_maximum_fusion
  (63 shorter events, 1.7 us)
Async XLA Ops:
  0.6 6.2 copy-start.4
  10.3 52.7 %collective-permute-start.15 = (f32[32,128,128]{2,1,0:T(8,128)}, f32[32,128,128]{2,1,0:T(8,128)S(1)}, u32[]{:S(2)}, u32[]{:S(2)}) collective-permute-start(f32[32,128,128]{2,1,0:T(8,128)} %get-tuple-element.38), channel_id=1, source_target_pairs={{28,0},{0,4},{4,8},{8,12},{12,16},{16,20},{20,24},{24,28},{29,1},{... | collective-permute-start | bytes 6291464 | tf_op jit(solution)/shard_map/ppermute | solution.py:21
  13.3 4.3 copy-start.17
  13.3 5.8 copy-start
  13.3 49.7 %copy-start.16 = (f32[32,128,128]{2,1,0:T(8,128)S(1)}, f32[32,128,128]{2,1,0:T(8,128)}, u32[]{:S(2)}) copy-start(f32[32,128,128]{2,1,0:T(8,128)} %get-tuple-element.41) | copy-start | bytes 6291460
  15.9 182.7 %collective-permute-start = (f32[2,32,128,128]{3,2,1,0:T(8,128)S(1)}, f32[2,32,128,128]{3,2,1,0:T(8,128)S(1)}, u32[]{:S(2)}, u32[]{:S(2)}) collective-permute-start(f32[2,32,128,128]{3,2,1,0:T(8,128)S(1)} %constant_dynamic-slice_fusion), channel_id=1, source_target_pairs={{0,1},{1,0},{2,3},{3,2},{4,5},{5,4},{6,7},{7,6},{8,9},{9,8},{10,11... | collective-permute-start | bytes 12582920 | tf_op jit(solution)/shard_map/ppermute | solution.py:376
  16.0 92.0 %collective-permute-start.11 = (f32[32,128,128]{2,1,0:T(8,128)}, f32[32,128,128]{2,1,0:T(8,128)S(1)}, u32[]{:S(2)}, u32[]{:S(2)}) collective-permute-start(f32[32,128,128]{2,1,0:T(8,128)} %get-tuple-element.39), channel_id=1, source_target_pairs={{28,0},{0,4},{4,8},{8,12},{12,16},{16,20},{20,24},{24,28},{29,1},{... | collective-permute-start | bytes 6291464 | tf_op jit(solution)/shard_map/ppermute | solution.py:21
  17.6 135.4 %collective-permute-start.7 = (f32[32,128,128]{2,1,0:T(8,128)S(1)}, f32[32,128,128]{2,1,0:T(8,128)}, u32[]{:S(2)}, u32[]{:S(2)}) collective-permute-start(f32[32,128,128]{2,1,0:T(8,128)S(1)} %copy-done.17), channel_id=1, source_target_pairs={{28,0},{0,4},{4,8},{8,12},{12,16},{16,20},{20,24},{24,28},{29,1},{... | collective-permute-start | bytes 6291464 | tf_op jit(solution)/shard_map/ppermute | solution.py:21
  19.1 181.6 %collective-permute-start.1 = (f32[2,32,128,128]{3,2,1,0:T(8,128)S(1)}, f32[2,32,128,128]{3,2,1,0:T(8,128)S(1)}, u32[]{:S(2)}, u32[]{:S(2)}) collective-permute-start(f32[2,32,128,128]{3,2,1,0:T(8,128)S(1)} %copy-done), channel_id=1, source_target_pairs={{0,2},{1,3},{2,0},{3,1},{4,6},{5,7},{6,4},{7,5},{8,10},{9,11},{10,... | collective-permute-start | bytes 12582920 | tf_op jit(solution)/shard_map/ppermute | solution.py:376
  63.0 361.3 %copy-start.7 = (f32[32,128,128]{2,1,0:T(8,128)}, f32[32,128,128]{2,1,0:T(8,128)S(1)}, u32[]{:S(2)}) copy-start(f32[32,128,128]{2,1,0:T(8,128)S(1)} %collective-permute-done.15.refs_4_) | copy-start | bytes 6291460
  63.0 134.1 %collective-permute-start.3 = (f32[32,128,128]{2,1,0:T(8,128)S(1)}, f32[32,128,128]{2,1,0:T(8,128)}, u32[]{:S(2)}, u32[]{:S(2)}) collective-permute-start(f32[32,128,128]{2,1,0:T(8,128)S(1)} %copy-done.16), channel_id=1, source_target_pairs={{28,0},{0,4},{4,8},{8,12},{12,16},{16,20},{20,24},{24,28},{29,1},{... | collective-permute-start | bytes 6291464 | tf_op jit(solution)/shard_map/ppermute | solution.py:21
  108.0 316.5 %copy-start.8 = (f32[32,128,128]{2,1,0:T(8,128)}, f32[32,128,128]{2,1,0:T(8,128)S(1)}, u32[]{:S(2)}) copy-start(f32[32,128,128]{2,1,0:T(8,128)S(1)} %collective-permute-done.11.refs_4_) | copy-start | bytes 6291460
  108.0 91.2 %collective-permute-start.17 = (f32[32,128,128]{2,1,0:T(8,128)S(1)}, f32[32,128,128]{2,1,0:T(8,128)S(1)}, u32[]{:S(2)}, u32[]{:S(2)}) collective-permute-start(f32[32,128,128]{2,1,0:T(8,128)S(1)} %collective-permute-done.15.refs_4_), channel_id=1, source_target_pairs={{0,2},{1,3},{2,0},{3,1},{4,6},{5,7},{6,4},{7,5},{8,10},{9,11},{10,... | collective-permute-start | bytes 6291464 | tf_op jit(solution)/shard_map/ppermute | solution.py:376
  153.0 46.1 %collective-permute-start.16 = (f32[32,128,128]{2,1,0:T(8,128)S(1)}, f32[32,128,128]{2,1,0:T(8,128)S(1)}, u32[]{:S(2)}, u32[]{:S(2)}) collective-permute-start(f32[32,128,128]{2,1,0:T(8,128)S(1)} %collective-permute-done.15.refs_4_), channel_id=1, source_target_pairs={{0,1},{1,0},{2,3},{3,2},{4,5},{5,4},{6,7},{7,6},{8,9},{9,8},{10,11... | collective-permute-start | bytes 6291464 | tf_op jit(solution)/shard_map/ppermute | solution.py:376
  197.1 48.6 %collective-permute-start.13 = (f32[32,128,128]{2,1,0:T(8,128)S(1)}, f32[32,128,128]{2,1,0:T(8,128)}, u32[]{:S(2)}, u32[]{:S(2)}) collective-permute-start(f32[32,128,128]{2,1,0:T(8,128)S(1)} %collective-permute-done.11.refs_4_), channel_id=1, source_target_pairs={{0,2},{1,3},{2,0},{3,1},{4,6},{5,7},{6,4},{7,5},{8,10},{9,11},{10,... | collective-permute-start | bytes 6291464 | tf_op jit(solution)/shard_map/ppermute | solution.py:376
  198.6 2.1 copy-start.1
  198.6 225.7 %collective-permute-start.2 = (f32[2,32,128,128]{3,2,1,0:T(8,128)S(1)}, f32[2,32,128,128]{3,2,1,0:T(8,128)S(1)}, u32[]{:S(2)}, u32[]{:S(2)}) collective-permute-start(f32[2,32,128,128]{3,2,1,0:T(8,128)S(1)} %collective-permute-done.refs_1_), channel_id=1, source_target_pairs={{0,2},{1,3},{2,0},{3,1},{4,6},{5,7},{6,4},{7,5},{8,10},{9,11},{10,... | collective-permute-start | bytes 12582920 | tf_op jit(solution)/shard_map/ppermute | solution.py:376
  199.1 232.4 %copy-start.9 = (f32[32,128,128]{2,1,0:T(8,128)}, f32[32,128,128]{2,1,0:T(8,128)S(1)}, u32[]{:S(2)}) copy-start(f32[32,128,128]{2,1,0:T(8,128)S(1)} %collective-permute-done.17.refs_6_) | copy-start | bytes 6291460
  199.2 46.6 %collective-permute-start.12 = (f32[32,128,128]{2,1,0:T(8,128)S(1)}, f32[32,128,128]{2,1,0:T(8,128)S(1)}, u32[]{:S(2)}, u32[]{:S(2)}) collective-permute-start(f32[32,128,128]{2,1,0:T(8,128)S(1)} %collective-permute-done.11.refs_4_), channel_id=1, source_target_pairs={{0,1},{1,0},{2,3},{3,2},{4,5},{5,4},{6,7},{7,6},{8,9},{9,8},{10,11... | collective-permute-start | bytes 6291464 | tf_op jit(solution)/shard_map/ppermute | solution.py:376
  199.2 46.6 %copy-start.10 = (f32[32,128,128]{2,1,0:T(8,128)}, f32[32,128,128]{2,1,0:T(8,128)S(1)}, u32[]{:S(2)}) copy-start(f32[32,128,128]{2,1,0:T(8,128)S(1)} %collective-permute-done.16.refs_5_) | copy-start | bytes 6291460
  199.2 181.4 %collective-permute-start.9 = (f32[32,128,128]{2,1,0:T(8,128)}, f32[32,128,128]{2,1,0:T(8,128)}, u32[]{:S(2)}, u32[]{:S(2)}) collective-permute-start(f32[32,128,128]{2,1,0:T(8,128)} %collective-permute-done.7.refs_4_), channel_id=1, source_target_pairs={{0,2},{1,3},{2,0},{3,1},{4,6},{5,7},{6,4},{7,5},{8,10},{9,11},{10,... | collective-permute-start | bytes 6291464 | tf_op jit(solution)/shard_map/ppermute | solution.py:376
  200.7 2.5 copy-start.2
  200.7 223.0 %collective-permute-start.5 = (f32[32,128,128]{2,1,0:T(8,128)}, f32[32,128,128]{2,1,0:T(8,128)}, u32[]{:S(2)}, u32[]{:S(2)}) collective-permute-start(f32[32,128,128]{2,1,0:T(8,128)} %collective-permute-done.3.refs_4_), channel_id=1, source_target_pairs={{0,2},{1,3},{2,0},{3,1},{4,6},{5,7},{6,4},{7,5},{8,10},{9,11},{10,... | collective-permute-start | bytes 6291464 | tf_op jit(solution)/shard_map/ppermute | solution.py:376
  245.7 178.1 %collective-permute-start.18 = (f32[32,128,128]{2,1,0:T(8,128)S(1)}, f32[32,128,128]{2,1,0:T(8,128)S(1)}, u32[]{:S(2)}, u32[]{:S(2)}) collective-permute-start(f32[32,128,128]{2,1,0:T(8,128)S(1)} %collective-permute-done.17.refs_6_), channel_id=1, source_target_pairs={{0,1},{1,0},{2,3},{3,2},{4,5},{5,4},{6,7},{7,6},{8,9},{9,8},{10,11... | collective-permute-start | bytes 6291464 | tf_op jit(solution)/shard_map/ppermute | solution.py:376
  245.7 185.8 %copy-start.13 = (f32[32,128,128]{2,1,0:T(8,128)}, f32[32,128,128]{2,1,0:T(8,128)S(1)}, u32[]{:S(2)}) copy-start(f32[32,128,128]{2,1,0:T(8,128)S(1)} %collective-permute-done.12.refs_5_) | copy-start | bytes 6291460
  245.8 241.5 %collective-permute-start.14 = (f32[32,128,128]{2,1,0:T(8,128)}, f32[32,128,128]{2,1,0:T(8,128)}, u32[]{:S(2)}, u32[]{:S(2)}) collective-permute-start(f32[32,128,128]{2,1,0:T(8,128)} %collective-permute-done.13.refs_6_), channel_id=1, source_target_pairs={{0,1},{1,0},{2,3},{3,2},{4,5},{5,4},{6,7},{7,6},{8,9},{9,8},{10,11... | collective-permute-start | bytes 6291464 | tf_op jit(solution)/shard_map/ppermute | solution.py:376
  380.5 162.5 %collective-permute-start.8 = (f32[32,128,128]{2,1,0:T(8,128)}, f32[32,128,128]{2,1,0:T(8,128)}, u32[]{:S(2)}, u32[]{:S(2)}) collective-permute-start(f32[32,128,128]{2,1,0:T(8,128)} %collective-permute-done.7.refs_4_), channel_id=1, source_target_pairs={{0,1},{1,0},{2,3},{3,2},{4,5},{5,4},{6,7},{7,6},{8,9},{9,8},{10,11... | collective-permute-start | bytes 6291464 | tf_op jit(solution)/shard_map/ppermute | solution.py:376
  423.8 175.2 %collective-permute-start.4 = (f32[32,128,128]{2,1,0:T(8,128)}, f32[32,128,128]{2,1,0:T(8,128)}, u32[]{:S(2)}, u32[]{:S(2)}) collective-permute-start(f32[32,128,128]{2,1,0:T(8,128)} %collective-permute-done.3.refs_4_), channel_id=1, source_target_pairs={{0,1},{1,0},{2,3},{3,2},{4,5},{5,4},{6,7},{7,6},{8,9},{9,8},{10,11... | collective-permute-start | bytes 6291464 | tf_op jit(solution)/shard_map/ppermute | solution.py:376
  423.8 7.7 copy-start.15
  423.8 119.3 %collective-permute-start.10 = (f32[32,128,128]{2,1,0:T(8,128)}, f32[32,128,128]{2,1,0:T(8,128)}, u32[]{:S(2)}, u32[]{:S(2)}) collective-permute-start(f32[32,128,128]{2,1,0:T(8,128)} %collective-permute-done.9.refs_6_), channel_id=1, source_target_pairs={{0,1},{1,0},{2,3},{3,2},{4,5},{5,4},{6,7},{7,6},{8,9},{9,8},{10,11... | collective-permute-start | bytes 6291464 | tf_op jit(solution)/shard_map/ppermute | solution.py:376
  424.3 7.2 copy-start.3
  424.3 174.7 %collective-permute-start.6 = (f32[32,128,128]{2,1,0:T(8,128)}, f32[32,128,128]{2,1,0:T(8,128)}, u32[]{:S(2)}, u32[]{:S(2)}) collective-permute-start(f32[32,128,128]{2,1,0:T(8,128)} %collective-permute-done.5.refs_6_), channel_id=1, source_target_pairs={{0,1},{1,0},{2,3},{3,2},{4,5},{5,4},{6,7},{7,6},{8,9},{9,8},{10,11... | collective-permute-start | bytes 6291464 | tf_op jit(solution)/shard_map/ppermute | solution.py:376
  654.8 13.8 %copy-start.11 = (f32[32,128,128]{2,1,0:T(8,128)S(1)}, f32[32,128,128]{2,1,0:T(8,128)}, u32[]{:S(2)}) copy-start(f32[32,128,128]{2,1,0:T(8,128)} %get-tuple-element.32) | copy-start | bytes 6291460
  654.8 24.0 %collective-permute-start.19 = (f32[2,32,128,128]{3,2,1,0:T(8,128)}, f32[2,32,128,128]{3,2,1,0:T(8,128)S(1)}, u32[]{:S(2)}, u32[]{:S(2)}) collective-permute-start(f32[2,32,128,128]{3,2,1,0:T(8,128)} %get-tuple-element.29), channel_id=1, source_target_pairs={{0,1},{1,0},{2,3},{3,2},{4,5},{5,4},{6,7},{7,6},{8,9},{9,8},{10,11... | collective-permute-start | bytes 12582920 | tf_op jit(solution)/shard_map/ppermute | solution.py:376
  655.1 10.1 %collective-permute-start.20 = (f32[32,128,128]{2,1,0:T(8,128)}, f32[32,128,128]{2,1,0:T(8,128)S(1)}, u32[]{:S(2)}, u32[]{:S(2)}) collective-permute-start(f32[32,128,128]{2,1,0:T(8,128)} %get-tuple-element.31), channel_id=1, source_target_pairs={{0,1},{1,0},{2,3},{3,2},{4,5},{5,4},{6,7},{7,6},{8,9},{9,8},{10,11... | collective-permute-start | bytes 6291464 | tf_op jit(solution)/shard_map/ppermute | solution.py:376
  655.3 13.2 %collective-permute-start.22 = (f32[32,128,128]{2,1,0:T(8,128)}, f32[32,128,128]{2,1,0:T(8,128)S(1)}, u32[]{:S(2)}, u32[]{:S(2)}) collective-permute-start(f32[32,128,128]{2,1,0:T(8,128)} %get-tuple-element.33), channel_id=1, source_target_pairs={{0,1},{1,0},{2,3},{3,2},{4,5},{5,4},{6,7},{7,6},{8,9},{9,8},{10,11... | collective-permute-start | bytes 6291464 | tf_op jit(solution)/shard_map/ppermute | solution.py:376
  655.7 15.5 %collective-permute-start.24 = (f32[32,128,128]{2,1,0:T(8,128)}, f32[32,128,128]{2,1,0:T(8,128)S(1)}, u32[]{:S(2)}, u32[]{:S(2)}) collective-permute-start(f32[32,128,128]{2,1,0:T(8,128)} %get-tuple-element.35), channel_id=1, source_target_pairs={{0,1},{1,0},{2,3},{3,2},{4,5},{5,4},{6,7},{7,6},{8,9},{9,8},{10,11... | collective-permute-start | bytes 6291464 | tf_op jit(solution)/shard_map/ppermute | solution.py:376
  655.9 18.3 %collective-permute-start.26 = (f32[32,128,128]{2,1,0:T(8,128)}, f32[32,128,128]{2,1,0:T(8,128)S(1)}, u32[]{:S(2)}, u32[]{:S(2)}) collective-permute-start(f32[32,128,128]{2,1,0:T(8,128)} %get-tuple-element.37), channel_id=1, source_target_pairs={{0,1},{1,0},{2,3},{3,2},{4,5},{5,4},{6,7},{7,6},{8,9},{9,8},{10,11... | collective-permute-start | bytes 6291464 | tf_op jit(solution)/shard_map/ppermute | solution.py:376
  667.0 4.2 copy-start.12
  667.1 48.6 %collective-permute-start.21 = (f32[32,128,128]{2,1,0:T(8,128)S(1)}, f32[32,128,128]{2,1,0:T(8,128)S(1)}, u32[]{:S(2)}, u32[]{:S(2)}) collective-permute-start(f32[32,128,128]{2,1,0:T(8,128)S(1)} %add.219), channel_id=1, source_target_pairs={{4,0},{8,4},{12,8},{16,12},{20,16},{24,20},{28,24},{0,28},{5,1},{9... | collective-permute-start | bytes 6291464 | tf_op jit(solution)/shard_map/ppermute | solution.py:21
  668.9 5.3 copy-start.14
  668.9 91.7 %collective-permute-start.23 = (f32[32,128,128]{2,1,0:T(8,128)S(1)}, f32[32,128,128]{2,1,0:T(8,128)S(1)}, u32[]{:S(2)}, u32[]{:S(2)}) collective-permute-start(f32[32,128,128]{2,1,0:T(8,128)S(1)} %add.220), channel_id=1, source_target_pairs={{4,0},{8,4},{12,8},{16,12},{20,16},{24,20},{28,24},{0,28},{5,1},{9... | collective-permute-start | bytes 6291464 | tf_op jit(solution)/shard_map/ppermute | solution.py:21
  671.5 133.9 %collective-permute-start.25 = (f32[32,128,128]{2,1,0:T(8,128)S(1)}, f32[32,128,128]{2,1,0:T(8,128)S(1)}, u32[]{:S(2)}, u32[]{:S(2)}) collective-permute-start(f32[32,128,128]{2,1,0:T(8,128)S(1)} %add.221), channel_id=1, source_target_pairs={{4,0},{8,4},{12,8},{16,12},{20,16},{24,20},{28,24},{0,28},{5,1},{9... | collective-permute-start | bytes 6291464 | tf_op jit(solution)/shard_map/ppermute | solution.py:21
  674.5 175.3 %collective-permute-start.27 = (f32[32,128,128]{2,1,0:T(8,128)S(1)}, f32[32,128,128]{2,1,0:T(8,128)S(1)}, u32[]{:S(2)}, u32[]{:S(2)}) collective-permute-start(f32[32,128,128]{2,1,0:T(8,128)S(1)} %add.222), channel_id=1, source_target_pairs={{4,0},{8,4},{12,8},{16,12},{20,16},{24,20},{28,24},{0,28},{5,1},{9... | collective-permute-start | bytes 6291464 | tf_op jit(solution)/shard_map/ppermute | solution.py:21
  676.0 2.2 copy-start.6
  679.4 174.0 %copy-start.5 = (f32[4,32,128,128]{3,2,1,0:T(8,128)}, f32[4,32,128,128]{3,2,1,0:T(8,128)S(1)}, u32[]{:S(2)}) copy-start(f32[4,32,128,128]{3,2,1,0:T(8,128)S(1)} %constant_dynamic-update-slice_fusion) | copy-start | bytes 25165828

commit v2 on v1

--- a/solution.py
+++ b/solution.py
@@ -179,6 +179,96 @@
     return dot(a, c) + dot(b, c) + dot(a, d)
 
 
+def transform_planes(real, imag, x_table, y_table, inverse):
+    _, ny, nx = real.shape
+
+    def along_x(real, imag):
+        rows = jnp.concatenate([part.reshape(2 * ny, nx) for part in (real, imag)], axis=1)
+        rows = product(split(rows), x_table)
+        return [rows[:, i * nx : (i + 1) * nx].reshape(2, ny, nx) for i in (0, 1)]
+
+    def along_y(real, imag):
+        columns = jnp.concatenate(
+            [jnp.concatenate([part[0], part[1]], axis=1) for part in (real, imag)], axis=0
+        )
+        columns = product(y_table, split(columns))
+        return [
+            jnp.stack([columns[i * ny : (i + 1) * ny, p * nx : (p + 1) * nx] for p in (0, 1)])
+            for i in (0, 1)
+        ]
+
+    if inverse:
+        return along_x(*along_y(real, imag))
+    return along_y(*along_x(real, imag))
+
+
+def near_kernel(own_0, own_1, vis_0, vis_1, order, x_high, x_low, y_high, y_low, out, *scratch):
+    own_ref, vis_ref, own_sem, vis_sem, out_sem = scratch
+    depth = vis_0.shape[0]
+    own_hbm, vis_hbm = (own_0, own_1), (vis_0, vis_1)
+    copies = []
+    for s in range(2):
+        part = pl.ds(s * depth, depth)
+        copies.append(
+            [
+                pltpu.make_async_copy(own_hbm[s], own_ref.at[:, part], own_sem.at[s]),
+                pltpu.make_async_copy(vis_hbm[s], vis_ref.at[part], vis_sem.at[s]),
+            ]
+        )
+        for copy in copies[s]:
+            copy.start()
+    x_table = x_high[...], x_low[...]
+    y_table = y_high[...], y_low[...]
+
+    def slot(s, carry):
+        part = pl.ds(s * depth, depth)
+        pltpu.make_async_copy(own_0, own_ref.at[:, part], own_sem.at[s]).wait()
+        pltpu.make_async_copy(vis_0, vis_ref.at[part], vis_sem.at[s]).wait()
+
+        def chunk(index, carry):
+            start = s * depth + index * CHUNK
+            for pair in range(CHUNK // 2):
+                here = pl.ds(start + 2 * pair, 2)
+                visitor = vis_ref[here]
+                real, imag = transform_planes(
+                    own_ref[0, here] * visitor, own_ref[1, here] * visitor, x_table, y_table, False
+                )
+                own_ref[0, here] = real
+                own_ref[1, here] = imag
+            here = pl.ds(start, CHUNK)
+            pltpu.make_async_copy(own_ref.at[:, here], out.at[:, here], out_sem).start()
+            return carry
+
+        return lax.fori_loop(0, depth // CHUNK, chunk, carry)
+
+    lax.fori_loop(0, 2, slot, 0)
+    pltpu.make_async_copy(own_ref, out, out_sem).wait()
+
+
+def near_field(owned, visitor, order, tables):
+    depth, ny, nx = visitor[0].shape
+    anywhere = pl.BlockSpec(memory_space=pl.ANY)
+    points = 2 * depth * ny * nx
+    return pl.pallas_call(
+        near_kernel,
+        out_shape=jax.ShapeDtypeStruct((2, 2 * depth, ny, nx), jnp.float32),
+        in_specs=[anywhere] * 5 + [pl.BlockSpec(memory_space=pltpu.VMEM)] * 4,
+        out_specs=anywhere,
+        scratch_shapes=[
+            pltpu.VMEM((2, 2 * depth, ny, nx), jnp.float32),
+            pltpu.VMEM((2 * depth, ny, nx), jnp.float32),
+            pltpu.SemaphoreType.DMA((2,)),
+            pltpu.SemaphoreType.DMA((2,)),
+            pltpu.SemaphoreType.DMA,
+        ],
+        compiler_params=pltpu.CompilerParams(vmem_limit_bytes=40 * 1024 * 1024),
+        cost_estimate=pl.CostEstimate(
+            flops=2 * points * 2 * 4 * nx, bytes_accessed=4 * points * 5, transcendentals=0
+        ),
+        name="near_field",
+    )(owned[0], owned[1], visitor[0], visitor[1], order, *tables[:4])
+
+
 def field_kernel(radix, first_call, rank_ref, *refs):
     refs = list(refs)
 
@@ -188,79 +278,80 @@
         return taken
 
     own_hbm, vis_hbm = take(4), take(4)
-    (weights_hbm,) = take(1)
+    near_hbm, weights_hbm = take(2)
     tables = take(8)
     before_hbm = [] if first_call else take(2)
     held_hbm, sums_hbm = take(2), take(2)
     own_ref, vis_ref, real_ref, imag_ref, weights_ref, total_ref = take(6)
-    own_sem, vis_sem, weights_sem, before_sem, held_sem, sums_sem = refs
-    nz, ny, nx = real_ref.shape
+    own_sem, vis_sem, near_sem, weights_sem, before_sem, held_sem, sums_sem = refs
+    nz, ny, _ = real_ref.shape
     depth = nz // 4
     rank = rank_ref[0]
 
-    def planes(slot):
-        return pl.ds(lax.bitwise_xor(rank, slot) * depth, depth)
-
-    own_in, vis_in, before_in, held_out, sums_out = [], [], [], [], []
-    for s in range(4):
-        own_in.append(
-            pltpu.make_async_copy(own_hbm[s], own_ref.at[:, planes(s)], own_sem.at[s])
+    def base(slot):
+        return lax.bitwise_xor(rank, slot) * depth
+
+    own_in, vis_in, near_in, before_in, far_in = [], [], [], [], []
+    half = depth // 2
+    for s in range(2):
+        here, part = pl.ds(base(s), depth), pl.ds(s * depth, depth)
+        own_in.append(pltpu.make_async_copy(own_hbm[s], own_ref.at[:, here], own_sem.at[s, 0]))
+        vis_in.append(pltpu.make_async_copy(vis_hbm[s], vis_ref.at[here], vis_sem.at[s, 0]))
+        for i, ref in enumerate((real_ref, imag_ref)):
+            near_in.append(
+                pltpu.make_async_copy(near_hbm.at[i, part], ref.at[here], near_sem.at[s, i])
+            )
+        if not first_call:
+            before_in.append(
+                pltpu.make_async_copy(before_hbm[s], total_ref.at[:, part], before_sem.at[s])
+            )
+    for s in range(2, 4):
+        for h in range(2):
+            here, part = pl.ds(base(s) + h * half, half), pl.ds(h * half, half)
+            far_in.append(
+                [
+                    pltpu.make_async_copy(
+                        own_hbm[s].at[:, part], own_ref.at[:, here], own_sem.at[s, h]
+                    ),
+                    pltpu.make_async_copy(
+                        vis_hbm[s].at[part], vis_ref.at[here], vis_sem.at[s, h]
+                    ),
+                ]
+            )
+    stripes = weights_sem.shape[0]
+    stripe = ny // stripes
+    weights_in = []
+    for i in range(stripes):
+        part = pl.ds(i * stripe, stripe)
+        weights_in.append(
+            pltpu.make_async_copy(
+                weights_hbm.at[:, part], weights_ref.at[:, part], weights_sem.at[i]
+            )
         )
-        vis_in.append(pltpu.make_async_copy(vis_hbm[s], vis_ref.at[planes(s)], vis_sem.at[s]))
-    weights_in = pltpu.make_async_copy(weights_hbm, weights_ref, weights_sem)
-    for s in range(2):
-        part = total_ref.at[:, pl.ds(s * depth, depth)]
-        if not first_call:
-            before_in.append(pltpu.make_async_copy(before_hbm[s], part, before_sem.at[s]))
-        sums_out.append(pltpu.make_async_copy(part, sums_hbm[s], sums_sem.at[s]))
-        held_out.append(
-            pltpu.make_async_copy(vis_ref.at[planes(s)], held_hbm[s], held_sem.at[s])
-        )
-    for copy in [c for both in zip(own_in, vis_in) for c in both] + [weights_in] + before_in:
-        copy.start()
+
+    def start(copies):
+        for copy in copies:
+            copy.start()
+
+    start(far_in[0])
 
     def loaded(index):
         return tables[index][...], tables[index + 1][...]
 
     def forward(z):
-        visitor = vis_ref[pl.ds(z, 2)]
-        real = (own_ref[0, pl.ds(z, 2)] * visitor).reshape(2 * ny, nx)
-        imag = (own_ref[1, pl.ds(z, 2)] * visitor).reshape(2 * ny, nx)
-        rows = jnp.concatenate([real, imag], axis=1)
-        rows = product(split(rows), loaded(0))
-        columns = jnp.concatenate(
-            [
-                jnp.concatenate([rows[:ny, :nx], rows[ny:, :nx]], axis=1),
-                jnp.concatenate([rows[:ny, nx:], rows[ny:, nx:]], axis=1),
-            ],
-            axis=0,
+        here = pl.ds(z, 2)
+        visitor = vis_ref[here]
+        real, imag = transform_planes(
+            own_ref[0, here] * visitor, own_ref[1, here] * visitor, loaded(0), loaded(2), False
         )
-        columns = product(loaded(2), split(columns))
-        for i in (0, 1):
-            real_ref[z + i] = columns[:ny, i * nx : (i + 1) * nx]
-            imag_ref[z + i] = columns[ny:, i * nx : (i + 1) * nx]
+        real_ref[here] = real
+        imag_ref[here] = imag
 
     def backward(z, kept):
-        columns = jnp.concatenate(
-            [
-                jnp.concatenate([ref[z], ref[z + 1]], axis=1)
-                for ref in (real_ref, imag_ref)
-            ],
-            axis=0,
-        )
-        columns = product(loaded(4), split(columns))
-        rows = jnp.concatenate(
-            [
-                jnp.concatenate([columns[:ny, :nx], columns[ny:, :nx]], axis=1),
-                jnp.concatenate([columns[:ny, nx:], columns[ny:, nx:]], axis=1),
-            ],
-            axis=0,
-        )
-        rows = product(split(rows), loaded(6))
-        real = rows[:, :nx].reshape(2, ny, nx)
-        imag = rows[:, nx:].reshape(2, ny, nx)
-        visitor = vis_ref[pl.ds(z, 2)]
-        vis_ref[pl.ds(z, 2)] = real * own_ref[0, pl.ds(z, 2)] + imag * own_ref[1, pl.ds(z, 2)]
+        here = pl.ds(z, 2)
+        real, imag = transform_planes(real_ref[here], imag_ref[here], loaded(6), loaded(4), True)
+        visitor = vis_ref[here]
+        vis_ref[here] = real * own_ref[0, here] + imag * own_ref[1, here]
         for i, part in enumerate((real, imag)):
             part = part * visitor
             if not first_call:
@@ -294,47 +385,89 @@
                 store(radix * n + fine, value)
         return carry
 
-    def forward_slot(s, carry):
-        here = planes(s)
-        pltpu.make_async_copy(own_hbm[0], own_ref.at[:, here], own_sem.at[s]).wait()
-        pltpu.make_async_copy(vis_hbm[0], vis_ref.at[here], vis_sem.at[s]).wait()
-        base = lax.bitwise_xor(rank, s) * depth
-
-        def forward_chunk(chunk, carry):
-            for pair in range(CHUNK // 2):
-                forward(base + chunk * CHUNK + 2 * pair)
-            return carry
-
-        return lax.fori_loop(0, depth // CHUNK, forward_chunk, carry)
-
-    lax.fori_loop(0, 4, forward_slot, 0)
-    weights_in.wait()
-    lax.fori_loop(0, ny // 8, tile, 0)
+    per_slot = depth // CHUNK
+
+    def arrived(copies):
+        for copy in copies:
+            copy.wait()
+
+    arrived(far_in[0])
+    start(far_in[1] + near_in[:2])
+
+    def forward_chunk(index, carry):
+        per_half = per_slot // 2
+        for h, later in (
+            (1, far_in[2] + near_in[2:]),
+            (2, far_in[3] + weights_in[:1]),
+            (3, weights_in[1:]),
+        ):
+
+            @pl.when(index == h * per_half)
+            def _():
+                arrived(far_in[h])
+                start(later)
+
+        first = base(2 + index // per_slot) + index % per_slot * CHUNK
+        for pair in range(CHUNK // 2):
+            forward(first + 2 * pair)
+        return carry
+
+    lax.fori_loop(0, 2 * per_slot, forward_chunk, 0)
+    arrived(near_in)
+
+    def tile_and_wait(index, carry):
+        for i in range(stripes):
+
+            @pl.when(index == i * (stripe // 8))
+            def _():
+                arrived(weights_in[i : i + 1])
+                if i == 1:
+                    start(own_in[1::-1] + vis_in[1::-1] + before_in)
+
+        return tile(index, carry)
+
+    lax.fori_loop(0, ny // 8, tile_and_wait, 0)
+    arrived(own_in + vis_in + before_in)
+
+    def backward_chunk(index, carry):
+        slot = 1 - index // per_slot
+        first = index % per_slot * CHUNK
+        for pair in range(CHUNK // 2):
+            offset = first + 2 * pair
+            backward(base(slot) + offset, slot * depth + offset)
+        here = pl.ds(first, CHUNK)
+        for s in range(2):
+
+            @pl.when(slot == s)
+            def _():
+                pltpu.make_async_copy(
+                    vis_ref.at[pl.ds(base(s) + first, CHUNK)], held_hbm[s].at[here], held_sem.at[s]
+                ).start()
+                pltpu.make_async_copy(
+                    total_ref.at[:, pl.ds(s * depth + first, CHUNK)],
+                    sums_hbm[s].at[:, here],
+                    sums_sem.at[s],
+                ).start()
+
+        return carry
+
+    lax.fori_loop(0, 2 * per_slot, backward_chunk, 0)
     for s in (1, 0):
-        if not first_call:
-            before_in[s].wait()
-        base = lax.bitwise_xor(rank, s) * depth
-
-        def backward_chunk(chunk, carry):
-            for pair in range(CHUNK // 2):
-                offset = chunk * CHUNK + 2 * pair
-                backward(base + offset, s * depth + offset)
-            return carry
-
-        lax.fori_loop(0, depth // CHUNK, backward_chunk, 0)
-        held_out[s].start()
-        sums_out[s].start()
-    for copy in held_out + sums_out:
-        copy.wait()
-
-
-def solve_field(rank, owned, visitor, weights, tables, before):
+        pltpu.make_async_copy(
+            vis_ref.at[pl.ds(base(s), depth)], held_hbm[s], held_sem.at[s]
+        ).wait()
+        pltpu.make_async_copy(
+            total_ref.at[:, pl.ds(s * depth, depth)], sums_hbm[s], sums_sem.at[s]
+        ).wait()
+
+
+def solve_field(rank, owned, visitor, near, weights, tables, before):
     depth, ny, nx = visitor[0].shape
     nz = 4 * depth
     first_call = before is None
-    operands = list(owned) + list(visitor) + [weights] + list(tables)
+    operands = list(owned) + list(visitor) + [near, weights] + list(tables)
     anywhere = pl.BlockSpec(memory_space=pl.ANY)
-    in_specs = [pl.BlockSpec(memory_space=pltpu.SMEM)] + [anywhere] * 9
+    in_specs = [pl.BlockSpec(memory_space=pltpu.SMEM)] + [anywhere] * 10
     in_specs += [pl.BlockSpec(memory_space=pltpu.VMEM)] * 8
     if not first_call:
         in_specs += [anywhere] * 2
@@ -355,9 +488,10 @@
             grid,
             grid,
             pltpu.VMEM((2, 2 * depth, ny, nx), jnp.float32),
+            pltpu.SemaphoreType.DMA((4, 2)),
+            pltpu.SemaphoreType.DMA((4, 2)),
+            pltpu.SemaphoreType.DMA((2, 2)),
             pltpu.SemaphoreType.DMA((4,)),
-            pltpu.SemaphoreType.DMA((4,)),
-            pltpu.SemaphoreType.DMA,
             pltpu.SemaphoreType.DMA((2,)),
             pltpu.SemaphoreType.DMA((2,)),
             pltpu.SemaphoreType.DMA((2,)),
@@ -419,18 +553,25 @@
         tables += halves(complex_matrix(length, inverse, left))
     rank_operand = rank.astype(jnp.int32).reshape(1)
 
+    nears = []
+    for j in range(count_vis):
+        order = nears[-1] if nears else weights
+        nears.append(near_field(owned, visitors[j], order, tables))
+
     sums = None
     returned = []
     for j in range(count_vis):
-        held, sums = solve_field(rank_operand, owned, visitors[j], weights, tables, sums)
+        held, sums = solve_field(rank_operand, owned, visitors[j], nears[j], weights, tables, sums)
         other = exchanged(held[1], 1)
         returned.append(passed_along(held[0] + other, "band", -1))
-    held_rows = jnp.stack(returned)
 
     own_other = exchanged(sums[1], 1)
     own_rows = jnp.zeros(own_bands.shape, own_bands.dtype)
     own_rows = lax.dynamic_update_slice_in_dim(own_rows, sums[0], core * half_own, 0)
     own_rows = lax.dynamic_update_slice_in_dim(own_rows, own_other, (1 - core) * half_own, 0)
+    held_rows = jnp.zeros(travel_bands.shape, travel_bands.dtype)
+    for j in range(count_vis):
+        held_rows = lax.dynamic_update_slice_in_dim(held_rows, returned[j][None], j, 0)
     return own_rows, held_rows
 
 

time: 854 us -> 824 us (0.965)
  waiting for transfers between devices: 576 us -> 540 us
    pallas_call x0 -> x4, Pallas kernels: none -> 50.9 us  [near_field(): pl.pallas_call(near_kernel, out_shape=jax.ShapeDtypeStruct((2, 2 * depth,...]
    pallas_call x4, Pallas kernels: 223 us -> 174 us  [solve_field(): pl.pallas_call(functools.partial(field_kernel, 8, first_call), out_shape=...]
    ppermute x20, waiting for transfers between devices: 231 us -> 197 us  [exchanged(): return lax.ppermute(block, 'grid', [(i, i ^ bit) for i in devices])]
  transfers between devices with their start and end apart: 28 -> 28, of which waited for: 14 -> 16; matrix products, arithmetic and copies ran while one was open for 2% -> 2% of each run, Pallas kernels for 20% -> 22%
where the time goes in v2:
time: 824 us; the launch traced here: 823 us
  waiting for transfers between devices  540 us (66%)
  Pallas kernels  225 us (27%)
  local copies, waits for them, and re-layouts  24 us (3%)
  starting transfers between devices  23.4 us (3%)
  other arithmetic  9.41 us (1%)
    ppermute x8, waiting for transfers between devices, passed_along(): return lax.ppermute(block, axis, route)  343 us
    ppermute x20, waiting for transfers between devices, exchanged(): return lax.ppermute(block, 'grid', [(i, i ^ bit) for i in devices])  197 us
    pallas_call x4, Pallas kernels, solve_field(): pl.pallas_call(functools.partial(field_kernel, 8, first_call), out_shape=...  174 us
    pallas_call x4, Pallas kernels, near_field(): pl.pallas_call(near_kernel, out_shape=jax.ShapeDtypeStruct((2, 2 * depth,...  50.9 us
  transfers between devices with their start and end apart: 28, of which 16 were waited for; matrix products, arithmetic and copies ran while one was open for 2% of the time, Pallas kernels for 22%

profile of v2, /device:TPU:0, one launch (start us, length us, event | category | flops | bytes accessed | tf_op | source)
XLA Modules:
  0.0 823.5 jit_solution(15517846494576174244)
XLA Ops:
  0.7 5.0 constant_dynamic-slice_fusion.1.own_0.refs_0_
  5.6 1.2 copy-done.16
  6.8 3.5 slice_bitcast_fusion
  10.3 3.0 collective-permute-start.11
  13.3 1.5 collective-permute-start.9
  14.8 2.6 constant_dynamic-slice_fusion
  17.6 1.5 collective-permute-start.7
  19.2 1.5 collective-permute-start.1
  20.6 42.3 %collective-permute-done.11.vis_0.refs_4_ = f32[32,128,128]{2,1,0:T(8,128)S(1)} collective-permute-done((f32[32,128,128]{2,1,0:T(8,128)}, f32[32,128,128]{2,1,0:T(8,128)S(1)}, u32[]{:S(2)}, u32[]{:S(2)}) %collective-permute-start.11) | collective-permute-done | bytes 2097184 | tf_op jit(solution)/shard_map/ppermute | solution.py:21
  63.0 45.0 %collective-permute-done.9.vis_0.refs_4_ = f32[32,128,128]{2,1,0:T(8,128)} collective-permute-done((f32[32,128,128]{2,1,0:T(8,128)}, f32[32,128,128]{2,1,0:T(8,128)}, u32[]{:S(2)}, u32[]{:S(2)}) %collective-permute-start.9) | collective-permute-done | bytes 2097184 | tf_op jit(solution)/shard_map/ppermute | solution.py:21
  108.0 44.8 %collective-permute-done.7.vis_0.refs_4_ = f32[32,128,128]{2,1,0:T(8,128)S(1)} collective-permute-done((f32[32,128,128]{2,1,0:T(8,128)S(1)}, f32[32,128,128]{2,1,0:T(8,128)S(1)}, u32[]{:S(2)}, u32[]{:S(2)}) %collective-permute-start.7) | collective-permute-done | bytes 2097184 | tf_op jit(solution)/shard_map/ppermute | solution.py:21
  152.9 1.7 collective-permute-start.17
  154.5 42.4 %collective-permute-done.3.vis_0.refs_4_ = f32[32,128,128]{2,1,0:T(8,128)S(1)} collective-permute-done((f32[32,128,128]{2,1,0:T(8,128)S(1)}, f32[32,128,128]{2,1,0:T(8,128)S(1)}, u32[]{:S(2)}, u32[]{:S(2)}) %collective-permute-start.3) | collective-permute-done | bytes 2097184 | tf_op jit(solution)/shard_map/ppermute | solution.py:21
  197.0 1.6 collective-permute-start.15
  198.9 1.3 collective-permute-start.2
  200.2 0.7 collective-permute-start.13
  201.3 1.6 copy-done.11
  203.0 42.9 %collective-permute-done.15.refs_6_ = f32[32,128,128]{2,1,0:T(8,128)} collective-permute-done((f32[32,128,128]{2,1,0:T(8,128)}, f32[32,128,128]{2,1,0:T(8,128)}, u32[]{:S(2)}, u32[]{:S(2)}) %collective-permute-start.15) | collective-permute-done | bytes 2097184 | tf_op jit(solution)/shard_map/ppermute | solution.py:510
  245.9 1.5 collective-permute-start.5
  247.4 1.5 copy-done.13
  249.0 131.7 %collective-permute-done.13.refs_6_ = f32[32,128,128]{2,1,0:T(8,128)} collective-permute-done((f32[32,128,128]{2,1,0:T(8,128)S(1)}, f32[32,128,128]{2,1,0:T(8,128)}, u32[]{:S(2)}, u32[]{:S(2)}) %collective-permute-start.13) | collective-permute-done | bytes 2097184 | tf_op jit(solution)/shard_map/ppermute | solution.py:510
  381.2 6.5 fusion.1.order.refs_9_
  387.7 12.4 %near_field.4.order.refs_8_ = f32[2,64,128,128]{3,2,1,0:T(8,128)} custom-call(f32[2,32,128,128]{3,2,1,0:T(8,128)S(1)} %copy-done, f32[2,32,128,128]{3,2,1,0:T(8,128)S(1)} %collective-permute-done.own_1.refs_1_, f32[32,128,128]{2,1,0:T(8,128)S(1)} %collective-permute-done.11.vis_0.refs_4_, f32[32,128,128]{2,1,0:T(8,128)S(1)} %collective-permute-done.12.vis_1.refs_5_, ...), custom_call_target="tpu_custom_call" | custom-call | flops 2147483648 | bytes 20971520 | tf_op jit(solution)/shard_map/near_field/pallas_call | solution.py:252
  400.1 13.6 %near_field.5.order.refs_8_ = f32[2,64,128,128]{3,2,1,0:T(8,128)} custom-call(f32[2,32,128,128]{3,2,1,0:T(8,128)S(1)} %copy-done, f32[2,32,128,128]{3,2,1,0:T(8,128)S(1)} %collective-permute-done.own_1.refs_1_, f32[32,128,128]{2,1,0:T(8,128)} %collective-permute-done.9.vis_0.refs_4_, f32[32,128,128]{2,1,0:T(8,128)S(1)} %copy-done.12, ...), custom_call_target="tpu_custom_call" | custom-call | flops 2147483648 | bytes 20971520 | tf_op jit(solution)/shard_map/near_field/pallas_call | solution.py:252
  413.7 11.4 %collective-permute-done.5.refs_6_ = f32[32,128,128]{2,1,0:T(8,128)} collective-permute-done((f32[32,128,128]{2,1,0:T(8,128)S(1)}, f32[32,128,128]{2,1,0:T(8,128)}, u32[]{:S(2)}, u32[]{:S(2)}) %collective-permute-start.5) | collective-permute-done | bytes 2097184 | tf_op jit(solution)/shard_map/ppermute | solution.py:510
  425.1 12.5 %near_field.6.order.refs_8_ = f32[2,64,128,128]{3,2,1,0:T(8,128)} custom-call(f32[2,32,128,128]{3,2,1,0:T(8,128)S(1)} %copy-done, f32[2,32,128,128]{3,2,1,0:T(8,128)S(1)} %collective-permute-done.own_1.refs_1_, f32[32,128,128]{2,1,0:T(8,128)S(1)} %collective-permute-done.7.vis_0.refs_4_, f32[32,128,128]{2,1,0:T(8,128)S(1)} %copy-done.14, ...), custom_call_target="tpu_custom_call" | custom-call | flops 2147483648 | bytes 20971520 | tf_op jit(solution)/shard_map/near_field/pallas_call | solution.py:252
  437.6 12.5 %near_field.7.refs_8_ = f32[2,64,128,128]{3,2,1,0:T(8,128)} custom-call(f32[2,32,128,128]{3,2,1,0:T(8,128)S(1)} %copy-done, f32[2,32,128,128]{3,2,1,0:T(8,128)S(1)} %collective-permute-done.own_1.refs_1_, f32[32,128,128]{2,1,0:T(8,128)S(1)} %collective-permute-done.3.vis_0.refs_4_, f32[32,128,128]{2,1,0:T(8,128)S(1)} %collective-permute-done.4.vis_1.refs_5_, ...), custom_call_target="tpu_custom_call" | custom-call | flops 2147483648 | bytes 20971520 | tf_op jit(solution)/shard_map/near_field/pallas_call | solution.py:252
  450.1 43.1 %solve_field.4 = (f32[32,128,128]{2,1,0:T(8,128)}, f32[32,128,128]{2,1,0:T(8,128)}, f32[2,32,128,128]{3,2,1,0:T(8,128)}, f32[2,32,128,128]{3,2,1,0:T(8,128)}) custom-call(s32[1]{0:T(128)} %bitcast.rank_ref, f32[2,32,128,128]{3,2,1,0:T(8,128)} %constant_dynamic-slice_fusion.1.own_0.refs_0_, f32[2,32,128,128]{3,2,1,0:T(8,128)} %copy-done.1, ...), custom_call_target="tpu_custom_call" | custom-call | flops 6442450944 | bytes 83886080 | tf_op jit(solution)/shard_map/solve_field/pallas_call | solution.py:479
  493.2 43.8 %solve_field.5 = (f32[32,128,128]{2,1,0:T(8,128)}, f32[32,128,128]{2,1,0:T(8,128)}, f32[2,32,128,128]{3,2,1,0:T(8,128)}, f32[2,32,128,128]{3,2,1,0:T(8,128)}) custom-call(s32[1]{0:T(128)} %bitcast.rank_ref, f32[2,32,128,128]{3,2,1,0:T(8,128)} %constant_dynamic-slice_fusion.1.own_0.refs_0_, f32[2,32,128,128]{3,2,1,0:T(8,128)} %copy-done.1, ...), custom_call_target="tpu_custom_call" | custom-call | flops 6442450944 | bytes 83886080 | tf_op jit(solution)/shard_map/solve_field/pallas_call | solution.py:479
  537.0 43.8 %solve_field.6 = (f32[32,128,128]{2,1,0:T(8,128)}, f32[32,128,128]{2,1,0:T(8,128)}, f32[2,32,128,128]{3,2,1,0:T(8,128)}, f32[2,32,128,128]{3,2,1,0:T(8,128)}) custom-call(s32[1]{0:T(128)} %bitcast.rank_ref, f32[2,32,128,128]{3,2,1,0:T(8,128)} %constant_dynamic-slice_fusion.1.own_0.refs_0_, f32[2,32,128,128]{3,2,1,0:T(8,128)} %copy-done.1, ...), custom_call_target="tpu_custom_call" | custom-call | flops 6442450944 | bytes 83886080 | tf_op jit(solution)/shard_map/solve_field/pallas_call | solution.py:479
  580.8 43.8 %solve_field.7 = (f32[32,128,128]{2,1,0:T(8,128)}, f32[32,128,128]{2,1,0:T(8,128)}, f32[2,32,128,128]{3,2,1,0:T(8,128)}, f32[2,32,128,128]{3,2,1,0:T(8,128)}) custom-call(s32[1]{0:T(128)} %bitcast.rank_ref, f32[2,32,128,128]{3,2,1,0:T(8,128)} %constant_dynamic-slice_fusion.1.own_0.refs_0_, f32[2,32,128,128]{3,2,1,0:T(8,128)} %copy-done.1, ...), custom_call_target="tpu_custom_call" | custom-call | flops 6442450944 | bytes 83886080 | tf_op jit(solution)/shard_map/solve_field/pallas_call | solution.py:479
  624.6 0.6 collective-permute-start.19
  626.1 9.0 %collective-permute-done.20 = f32[32,128,128]{2,1,0:T(8,128)S(1)} collective-permute-done((f32[32,128,128]{2,1,0:T(8,128)}, f32[32,128,128]{2,1,0:T(8,128)S(1)}, u32[]{:S(2)}, u32[]{:S(2)}) %collective-permute-start.20) | collective-permute-done | bytes 2097184 | tf_op jit(solution)/shard_map/ppermute | solution.py:510
  635.1 1.9 add.245
  637.1 1.8 collective-permute-start.21
  639.2 1.5 collective-permute-start.23
  641.5 1.8 collective-permute-start.25
  643.3 0.9 collective-permute-done.26
  644.4 1.8 collective-permute-start.27
  646.2 1.0 broadcast.199
  647.2 1.1 copy-done.19
  648.4 0.6 constant_dynamic-update-slice_fusion.1
  649.6 36.1 %collective-permute-done.21 = f32[32,128,128]{2,1,0:T(8,128)S(1)} collective-permute-done((f32[32,128,128]{2,1,0:T(8,128)S(1)}, f32[32,128,128]{2,1,0:T(8,128)S(1)}, u32[]{:S(2)}, u32[]{:S(2)}) %collective-permute-start.21) | collective-permute-done | bytes 2097184 | tf_op jit(solution)/shard_map/ppermute | solution.py:21
  685.6 1.0 dynamic_update_slice.20
  686.7 43.9 %collective-permute-done.23 = f32[32,128,128]{2,1,0:T(8,128)S(1)} collective-permute-done((f32[32,128,128]{2,1,0:T(8,128)S(1)}, f32[32,128,128]{2,1,0:T(8,128)S(1)}, u32[]{:S(2)}, u32[]{:S(2)}) %collective-permute-start.23) | collective-permute-done | bytes 2097184 | tf_op jit(solution)/shard_map/ppermute | solution.py:21
  730.8 44.7 %collective-permute-done.25 = f32[32,128,128]{2,1,0:T(8,128)S(1)} collective-permute-done((f32[32,128,128]{2,1,0:T(8,128)S(1)}, f32[32,128,128]{2,1,0:T(8,128)S(1)}, u32[]{:S(2)}, u32[]{:S(2)}) %collective-permute-start.25) | collective-permute-done | bytes 2097184 | tf_op jit(solution)/shard_map/ppermute | solution.py:21
  775.7 44.1 %collective-permute-done.27 = f32[32,128,128]{2,1,0:T(8,128)S(1)} collective-permute-done((f32[32,128,128]{2,1,0:T(8,128)S(1)}, f32[32,128,128]{2,1,0:T(8,128)S(1)}, u32[]{:S(2)}, u32[]{:S(2)}) %collective-permute-start.27) | collective-permute-done | bytes 2097184 | tf_op jit(solution)/shard_map/ppermute | solution.py:21
  820.1 3.4 copy-done.17
  (84 shorter events, 5.3 us)
Async XLA Ops:
  0.6 6.2 copy-start.16
  10.3 52.7 %collective-permute-start.11 = (f32[32,128,128]{2,1,0:T(8,128)}, f32[32,128,128]{2,1,0:T(8,128)S(1)}, u32[]{:S(2)}, u32[]{:S(2)}) collective-permute-start(f32[32,128,128]{2,1,0:T(8,128)} %get-tuple-element.38), channel_id=1, source_target_pairs={{28,0},{0,4},{4,8},{8,12},{12,16},{16,20},{20,24},{24,28},{29,1},{... | collective-permute-start | bytes 6291464 | tf_op jit(solution)/shard_map/ppermute | solution.py:21
  13.3 94.8 %collective-permute-start.9 = (f32[32,128,128]{2,1,0:T(8,128)}, f32[32,128,128]{2,1,0:T(8,128)}, u32[]{:S(2)}, u32[]{:S(2)}) collective-permute-start(f32[32,128,128]{2,1,0:T(8,128)} %get-tuple-element.39), channel_id=1, source_target_pairs={{28,0},{0,4},{4,8},{8,12},{12,16},{16,20},{20,24},{24,28},{29,1},{... | collective-permute-start | bytes 6291464 | tf_op jit(solution)/shard_map/ppermute | solution.py:21
  14.8 4.4 copy-start
  14.8 48.2 %copy-start.23 = (f32[32,128,128]{2,1,0:T(8,128)S(1)}, f32[32,128,128]{2,1,0:T(8,128)}, u32[]{:S(2)}) copy-start(f32[32,128,128]{2,1,0:T(8,128)} %get-tuple-element.41) | copy-start | bytes 6291460
  17.4 181.1 %collective-permute-start = (f32[2,32,128,128]{3,2,1,0:T(8,128)S(1)}, f32[2,32,128,128]{3,2,1,0:T(8,128)S(1)}, u32[]{:S(2)}, u32[]{:S(2)}) collective-permute-start(f32[2,32,128,128]{3,2,1,0:T(8,128)S(1)} %constant_dynamic-slice_fusion), channel_id=1, source_target_pairs={{0,1},{1,0},{2,3},{3,2},{4,5},{5,4},{6,7},{7,6},{8,9},{9,8},{10,11... | collective-permute-start | bytes 12582920 | tf_op jit(solution)/shard_map/ppermute | solution.py:510
  17.6 135.2 %collective-permute-start.7 = (f32[32,128,128]{2,1,0:T(8,128)S(1)}, f32[32,128,128]{2,1,0:T(8,128)S(1)}, u32[]{:S(2)}, u32[]{:S(2)}) collective-permute-start(f32[32,128,128]{2,1,0:T(8,128)S(1)} %copy-done.24), channel_id=1, source_target_pairs={{28,0},{0,4},{4,8},{8,12},{12,16},{16,20},{20,24},{24,28},{29,1},{... | collective-permute-start | bytes 6291464 | tf_op jit(solution)/shard_map/ppermute | solution.py:21
  19.2 181.1 %collective-permute-start.1 = (f32[2,32,128,128]{3,2,1,0:T(8,128)S(1)}, f32[2,32,128,128]{3,2,1,0:T(8,128)S(1)}, u32[]{:S(2)}, u32[]{:S(2)}) collective-permute-start(f32[2,32,128,128]{3,2,1,0:T(8,128)S(1)} %copy-done), channel_id=1, source_target_pairs={{0,2},{1,3},{2,0},{3,1},{4,6},{5,7},{6,4},{7,5},{8,10},{9,11},{10,... | collective-permute-start | bytes 12582920 | tf_op jit(solution)/shard_map/ppermute | solution.py:510
  63.0 324.7 %copy-start.6 = (f32[32,128,128]{2,1,0:T(8,128)}, f32[32,128,128]{2,1,0:T(8,128)S(1)}, u32[]{:S(2)}) copy-start(f32[32,128,128]{2,1,0:T(8,128)S(1)} %collective-permute-done.11.vis_0.refs_4_) | copy-start | bytes 6291460
  63.0 134.0 %collective-permute-start.3 = (f32[32,128,128]{2,1,0:T(8,128)S(1)}, f32[32,128,128]{2,1,0:T(8,128)S(1)}, u32[]{:S(2)}, u32[]{:S(2)}) collective-permute-start(f32[32,128,128]{2,1,0:T(8,128)S(1)} %copy-done.23), channel_id=1, source_target_pairs={{28,0},{0,4},{4,8},{8,12},{12,16},{16,20},{20,24},{24,28},{29,1},{... | collective-permute-start | bytes 6291464 | tf_op jit(solution)/shard_map/ppermute | solution.py:21
  108.0 88.9 %collective-permute-start.12 = (f32[32,128,128]{2,1,0:T(8,128)S(1)}, f32[32,128,128]{2,1,0:T(8,128)S(1)}, u32[]{:S(2)}, u32[]{:S(2)}) collective-permute-start(f32[32,128,128]{2,1,0:T(8,128)S(1)} %collective-permute-done.11.vis_0.refs_4_), channel_id=1, source_target_pairs={{0,1},{1,0},{2,3},{3,2},{4,5},{5,4},{6,7},{7,6},{8,9},{9,8},{10,11... | collective-permute-start | bytes 6291464 | tf_op jit(solution)/shard_map/ppermute | solution.py:510
  152.9 272.2 %copy-start.9 = (f32[32,128,128]{2,1,0:T(8,128)}, f32[32,128,128]{2,1,0:T(8,128)S(1)}, u32[]{:S(2)}) copy-start(f32[32,128,128]{2,1,0:T(8,128)S(1)} %collective-permute-done.7.vis_0.refs_4_) | copy-start | bytes 6291460
  152.9 46.0 %collective-permute-start.17 = (f32[32,128,128]{2,1,0:T(8,128)S(1)}, f32[32,128,128]{2,1,0:T(8,128)}, u32[]{:S(2)}, u32[]{:S(2)}) collective-permute-start(f32[32,128,128]{2,1,0:T(8,128)S(1)} %collective-permute-done.11.vis_0.refs_4_), channel_id=1, source_target_pairs={{0,2},{1,3},{2,0},{3,1},{4,6},{5,7},{6,4},{7,5},{8,10},{9,11},{10,... | collective-permute-start | bytes 6291464 | tf_op jit(solution)/shard_map/ppermute | solution.py:510
  197.0 240.6 %copy-start.8 = (f32[32,128,128]{2,1,0:T(8,128)}, f32[32,128,128]{2,1,0:T(8,128)S(1)}, u32[]{:S(2)}) copy-start(f32[32,128,128]{2,1,0:T(8,128)S(1)} %collective-permute-done.3.vis_0.refs_4_) | copy-start | bytes 6291460
  197.0 4.4 collective-permute-start.10
  197.0 190.7 %copy-start.7 = (f32[32,128,128]{2,1,0:T(8,128)}, f32[32,128,128]{2,1,0:T(8,128)S(1)}, u32[]{:S(2)}) copy-start(f32[32,128,128]{2,1,0:T(8,128)S(1)} %collective-permute-done.12.vis_1.refs_5_) | copy-start | bytes 6291460
  197.0 48.9 %collective-permute-start.15 = (f32[32,128,128]{2,1,0:T(8,128)}, f32[32,128,128]{2,1,0:T(8,128)}, u32[]{:S(2)}, u32[]{:S(2)}) collective-permute-start(f32[32,128,128]{2,1,0:T(8,128)} %collective-permute-done.9.vis_0.refs_4_), channel_id=1, source_target_pairs={{0,2},{1,3},{2,0},{3,1},{4,6},{5,7},{6,4},{7,5},{8,10},{9,11},{10,... | collective-permute-start | bytes 6291464 | tf_op jit(solution)/shard_map/ppermute | solution.py:510
  198.5 239.0 %copy-start.1 = (f32[2,32,128,128]{3,2,1,0:T(8,128)}, f32[2,32,128,128]{3,2,1,0:T(8,128)S(1)}, u32[]{:S(2)}) copy-start(f32[2,32,128,128]{3,2,1,0:T(8,128)S(1)} %collective-permute-done.own_1.refs_1_) | copy-start | bytes 12582916
  198.5 48.8 %collective-permute-start.8 = (f32[32,128,128]{2,1,0:T(8,128)S(1)}, f32[32,128,128]{2,1,0:T(8,128)S(1)}, u32[]{:S(2)}, u32[]{:S(2)}) collective-permute-start(f32[32,128,128]{2,1,0:T(8,128)S(1)} %collective-permute-done.7.vis_0.refs_4_), channel_id=1, source_target_pairs={{0,1},{1,0},{2,3},{3,2},{4,5},{5,4},{6,7},{7,6},{8,9},{9,8},{10,11... | collective-permute-start | bytes 6291464 | tf_op jit(solution)/shard_map/ppermute | solution.py:510
  198.9 251.2 %collective-permute-start.2 = (f32[2,32,128,128]{3,2,1,0:T(8,128)S(1)}, f32[2,32,128,128]{3,2,1,0:T(8,128)}, u32[]{:S(2)}, u32[]{:S(2)}) collective-permute-start(f32[2,32,128,128]{3,2,1,0:T(8,128)S(1)} %collective-permute-done.own_1.refs_1_), channel_id=1, source_target_pairs={{0,2},{1,3},{2,0},{3,1},{4,6},{5,7},{6,4},{7,5},{8,10},{9,11},{10,... | collective-permute-start | bytes 12582920 | tf_op jit(solution)/shard_map/ppermute | solution.py:510
  200.2 180.4 %collective-permute-start.13 = (f32[32,128,128]{2,1,0:T(8,128)S(1)}, f32[32,128,128]{2,1,0:T(8,128)}, u32[]{:S(2)}, u32[]{:S(2)}) collective-permute-start(f32[32,128,128]{2,1,0:T(8,128)S(1)} %collective-permute-done.7.vis_0.refs_4_), channel_id=1, source_target_pairs={{0,2},{1,3},{2,0},{3,1},{4,6},{5,7},{6,4},{7,5},{8,10},{9,11},{10,... | collective-permute-start | bytes 6291464 | tf_op jit(solution)/shard_map/ppermute | solution.py:510
  203.0 177.7 %collective-permute-start.4 = (f32[32,128,128]{2,1,0:T(8,128)S(1)}, f32[32,128,128]{2,1,0:T(8,128)S(1)}, u32[]{:S(2)}, u32[]{:S(2)}) collective-permute-start(f32[32,128,128]{2,1,0:T(8,128)S(1)} %collective-permute-done.3.vis_0.refs_4_), channel_id=1, source_target_pairs={{0,1},{1,0},{2,3},{3,2},{4,5},{5,4},{6,7},{7,6},{8,9},{9,8},{10,11... | collective-permute-start | bytes 6291464 | tf_op jit(solution)/shard_map/ppermute | solution.py:510
  245.9 179.2 %collective-permute-start.5 = (f32[32,128,128]{2,1,0:T(8,128)S(1)}, f32[32,128,128]{2,1,0:T(8,128)}, u32[]{:S(2)}, u32[]{:S(2)}) collective-permute-start(f32[32,128,128]{2,1,0:T(8,128)S(1)} %collective-permute-done.3.vis_0.refs_4_), channel_id=1, source_target_pairs={{0,2},{1,3},{2,0},{3,1},{4,6},{5,7},{6,4},{7,5},{8,10},{9,11},{10,... | collective-permute-start | bytes 6291464 | tf_op jit(solution)/shard_map/ppermute | solution.py:510
  248.9 201.2 %collective-permute-start.18 = (f32[32,128,128]{2,1,0:T(8,128)}, f32[32,128,128]{2,1,0:T(8,128)}, u32[]{:S(2)}, u32[]{:S(2)}) collective-permute-start(f32[32,128,128]{2,1,0:T(8,128)} %collective-permute-done.17.refs_6_), channel_id=1, source_target_pairs={{0,1},{1,0},{2,3},{3,2},{4,5},{5,4},{6,7},{7,6},{8,9},{9,8},{10,11... | collective-permute-start | bytes 6291464 | tf_op jit(solution)/shard_map/ppermute | solution.py:510
  249.0 138.7 %copy-start.2 = (bf16[256,256]{1,0:T(8,128)(2,1)S(1)}, bf16[256,256]{1,0:T(8,128)(2,1)}, u32[]{:S(2)}) copy-start(bf16[256,256]{1,0:T(8,128)(2,1)} %constant.100.clone.x_low.refs_11_.refs_15_) | copy-start | bytes 393220
  249.0 138.7 %copy-start.3 = (bf16[256,256]{1,0:T(8,128)(2,1)S(1)}, bf16[256,256]{1,0:T(8,128)(2,1)}, u32[]{:S(2)}) copy-start(bf16[256,256]{1,0:T(8,128)(2,1)} %constant.101.clone.y_high.refs_12_.refs_16_) | copy-start | bytes 393220
  249.0 138.7 %copy-start.4 = (bf16[256,256]{1,0:T(8,128)(2,1)S(1)}, bf16[256,256]{1,0:T(8,128)(2,1)}, u32[]{:S(2)}) copy-start(bf16[256,256]{1,0:T(8,128)(2,1)} %constant.102.clone.y_low.refs_13_.refs_17_) | copy-start | bytes 393220
  249.0 138.7 %copy-start.5 = (bf16[256,256]{1,0:T(8,128)(2,1)S(1)}, bf16[256,256]{1,0:T(8,128)(2,1)}, u32[]{:S(2)}) copy-start(bf16[256,256]{1,0:T(8,128)(2,1)} %constant.99.clone.x_high.refs_10_.refs_14_) | copy-start | bytes 393220
  380.7 112.5 %collective-permute-start.16 = (f32[32,128,128]{2,1,0:T(8,128)}, f32[32,128,128]{2,1,0:T(8,128)}, u32[]{:S(2)}, u32[]{:S(2)}) collective-permute-start(f32[32,128,128]{2,1,0:T(8,128)} %collective-permute-done.15.refs_6_), channel_id=1, source_target_pairs={{0,1},{1,0},{2,3},{3,2},{4,5},{5,4},{6,7},{7,6},{8,9},{9,8},{10,11... | collective-permute-start | bytes 6291464 | tf_op jit(solution)/shard_map/ppermute | solution.py:510
  380.7 56.9 %copy-start.10 = (f32[32,128,128]{2,1,0:T(8,128)}, f32[32,128,128]{2,1,0:T(8,128)S(1)}, u32[]{:S(2)}) copy-start(f32[32,128,128]{2,1,0:T(8,128)S(1)} %collective-permute-done.4.vis_1.refs_5_) | copy-start | bytes 6291460
  380.7 156.3 %collective-permute-start.14 = (f32[32,128,128]{2,1,0:T(8,128)}, f32[32,128,128]{2,1,0:T(8,128)}, u32[]{:S(2)}, u32[]{:S(2)}) collective-permute-start(f32[32,128,128]{2,1,0:T(8,128)} %collective-permute-done.13.refs_6_), channel_id=1, source_target_pairs={{0,1},{1,0},{2,3},{3,2},{4,5},{5,4},{6,7},{7,6},{8,9},{9,8},{10,11... | collective-permute-start | bytes 6291464 | tf_op jit(solution)/shard_map/ppermute | solution.py:510
  387.7 12.4 %copy-start.12 = (f32[32,128,128]{2,1,0:T(8,128)S(1)}, f32[32,128,128]{2,1,0:T(8,128)}, u32[]{:S(2)}) copy-start(f32[32,128,128]{2,1,0:T(8,128)} %copy-done.11) | copy-start | bytes 6291460
  400.1 25.0 %copy-start.14 = (f32[32,128,128]{2,1,0:T(8,128)S(1)}, f32[32,128,128]{2,1,0:T(8,128)}, u32[]{:S(2)}) copy-start(f32[32,128,128]{2,1,0:T(8,128)} %copy-done.13) | copy-start | bytes 6291460
  425.1 155.7 %collective-permute-start.6 = (f32[32,128,128]{2,1,0:T(8,128)}, f32[32,128,128]{2,1,0:T(8,128)}, u32[]{:S(2)}, u32[]{:S(2)}) collective-permute-start(f32[32,128,128]{2,1,0:T(8,128)} %collective-permute-done.5.refs_6_), channel_id=1, source_target_pairs={{0,1},{1,0},{2,3},{3,2},{4,5},{5,4},{6,7},{7,6},{8,9},{9,8},{10,11... | collective-permute-start | bytes 6291464 | tf_op jit(solution)/shard_map/ppermute | solution.py:510
  624.5 14.3 %copy-start.20 = (f32[32,128,128]{2,1,0:T(8,128)S(1)}, f32[32,128,128]{2,1,0:T(8,128)}, u32[]{:S(2)}) copy-start(f32[32,128,128]{2,1,0:T(8,128)} %get-tuple-element.32) | copy-start | bytes 6291460
  624.6 24.4 %collective-permute-start.19 = (f32[2,32,128,128]{3,2,1,0:T(8,128)}, f32[2,32,128,128]{3,2,1,0:T(8,128)S(1)}, u32[]{:S(2)}, u32[]{:S(2)}) collective-permute-start(f32[2,32,128,128]{3,2,1,0:T(8,128)} %get-tuple-element.29), channel_id=1, source_target_pairs={{0,1},{1,0},{2,3},{3,2},{4,5},{5,4},{6,7},{7,6},{8,9},{9,8},{10,11... | collective-permute-start | bytes 12582920 | tf_op jit(solution)/shard_map/ppermute | solution.py:510
  625.1 10.0 %collective-permute-start.20 = (f32[32,128,128]{2,1,0:T(8,128)}, f32[32,128,128]{2,1,0:T(8,128)S(1)}, u32[]{:S(2)}, u32[]{:S(2)}) collective-permute-start(f32[32,128,128]{2,1,0:T(8,128)} %get-tuple-element.31), channel_id=1, source_target_pairs={{0,1},{1,0},{2,3},{3,2},{4,5},{5,4},{6,7},{7,6},{8,9},{9,8},{10,11... | collective-permute-start | bytes 6291464 | tf_op jit(solution)/shard_map/ppermute | solution.py:510
  625.2 13.7 %collective-permute-start.22 = (f32[32,128,128]{2,1,0:T(8,128)}, f32[32,128,128]{2,1,0:T(8,128)S(1)}, u32[]{:S(2)}, u32[]{:S(2)}) collective-permute-start(f32[32,128,128]{2,1,0:T(8,128)} %get-tuple-element.33), channel_id=1, source_target_pairs={{0,1},{1,0},{2,3},{3,2},{4,5},{5,4},{6,7},{7,6},{8,9},{9,8},{10,11... | collective-permute-start | bytes 6291464 | tf_op jit(solution)/shard_map/ppermute | solution.py:510
  625.6 15.5 %collective-permute-start.24 = (f32[32,128,128]{2,1,0:T(8,128)}, f32[32,128,128]{2,1,0:T(8,128)S(1)}, u32[]{:S(2)}, u32[]{:S(2)}) collective-permute-start(f32[32,128,128]{2,1,0:T(8,128)} %get-tuple-element.35), channel_id=1, source_target_pairs={{0,1},{1,0},{2,3},{3,2},{4,5},{5,4},{6,7},{7,6},{8,9},{9,8},{10,11... | collective-permute-start | bytes 6291464 | tf_op jit(solution)/shard_map/ppermute | solution.py:510
  625.7 18.4 %collective-permute-start.26 = (f32[32,128,128]{2,1,0:T(8,128)}, f32[32,128,128]{2,1,0:T(8,128)S(1)}, u32[]{:S(2)}, u32[]{:S(2)}) collective-permute-start(f32[32,128,128]{2,1,0:T(8,128)} %get-tuple-element.37), channel_id=1, source_target_pairs={{0,1},{1,0},{2,3},{3,2},{4,5},{5,4},{6,7},{7,6},{8,9},{9,8},{10,11... | collective-permute-start | bytes 6291464 | tf_op jit(solution)/shard_map/ppermute | solution.py:510
  637.1 4.1 copy-start.21
  637.1 48.6 %collective-permute-start.21 = (f32[32,128,128]{2,1,0:T(8,128)S(1)}, f32[32,128,128]{2,1,0:T(8,128)S(1)}, u32[]{:S(2)}, u32[]{:S(2)}) collective-permute-start(f32[32,128,128]{2,1,0:T(8,128)S(1)} %add.245), channel_id=1, source_target_pairs={{4,0},{8,4},{12,8},{16,12},{20,16},{24,20},{28,24},{0,28},{5,1},{9... | collective-permute-start | bytes 6291464 | tf_op jit(solution)/shard_map/ppermute | solution.py:21
  639.2 4.9 copy-start.22
  639.2 91.3 %collective-permute-start.23 = (f32[32,128,128]{2,1,0:T(8,128)S(1)}, f32[32,128,128]{2,1,0:T(8,128)S(1)}, u32[]{:S(2)}, u32[]{:S(2)}) collective-permute-start(f32[32,128,128]{2,1,0:T(8,128)S(1)} %add.246), channel_id=1, source_target_pairs={{4,0},{8,4},{12,8},{16,12},{20,16},{24,20},{28,24},{0,28},{5,1},{9... | collective-permute-start | bytes 6291464 | tf_op jit(solution)/shard_map/ppermute | solution.py:21
  641.5 134.0 %collective-permute-start.25 = (f32[32,128,128]{2,1,0:T(8,128)S(1)}, f32[32,128,128]{2,1,0:T(8,128)S(1)}, u32[]{:S(2)}, u32[]{:S(2)}) collective-permute-start(f32[32,128,128]{2,1,0:T(8,128)S(1)} %add.247), channel_id=1, source_target_pairs={{4,0},{8,4},{12,8},{16,12},{20,16},{24,20},{28,24},{0,28},{5,1},{9... | collective-permute-start | bytes 6291464 | tf_op jit(solution)/shard_map/ppermute | solution.py:21
  644.4 175.5 %collective-permute-start.27 = (f32[32,128,128]{2,1,0:T(8,128)S(1)}, f32[32,128,128]{2,1,0:T(8,128)S(1)}, u32[]{:S(2)}, u32[]{:S(2)}) collective-permute-start(f32[32,128,128]{2,1,0:T(8,128)S(1)} %add.248), channel_id=1, source_target_pairs={{4,0},{8,4},{12,8},{16,12},{20,16},{24,20},{28,24},{0,28},{5,1},{9... | collective-permute-start | bytes 6291464 | tf_op jit(solution)/shard_map/ppermute | solution.py:21
  649.5 37.1 %copy-start.18 = (f32[4,32,128,128]{3,2,1,0:T(8,128)}, f32[4,32,128,128]{3,2,1,0:T(8,128)S(1)}, u32[]{:S(2)}) copy-start(f32[4,32,128,128]{3,2,1,0:T(8,128)S(1)} %constant_dynamic-update-slice_fusion) | copy-start | bytes 25165828
  820.1 3.4 copy-start.17
  (5 other events, 10.9 us)

commit v3 on v2

--- a/solution.py
+++ b/solution.py
@@ -13,6 +13,7 @@
 FRACTION = 0.25
 HIGHEST_PRECISION = lax.Precision.HIGHEST
 CHUNK = 8
+MESH = pl.DeviceIdType.MESH
 
 
 def passed_along(block, axis, distance):
@@ -269,7 +270,7 @@
     )(owned[0], owned[1], visitor[0], visitor[1], order, *tables[:4])
 
 
-def field_kernel(radix, first_call, rank_ref, *refs):
+def field_kernel(radix, first_call, *refs):
     refs = list(refs)
 
     def take(count):
@@ -281,12 +282,16 @@
     near_hbm, weights_hbm = take(2)
     tables = take(8)
     before_hbm = [] if first_call else take(2)
-    held_hbm, sums_hbm = take(2), take(2)
-    own_ref, vis_ref, real_ref, imag_ref, weights_ref, total_ref = take(6)
-    own_sem, vis_sem, near_sem, weights_sem, before_sem, held_sem, sums_sem = refs
+    (held_hbm,), sums_hbm = take(1), take(2)
+    own_ref, vis_ref, real_ref, imag_ref, weights_ref, total_ref, other_ref = take(7)
+    own_sem, vis_sem, near_sem, weights_sem, before_sem, held_sem, sums_sem = take(7)
+    send_sem, recv_sem = refs
     nz, ny, _ = real_ref.shape
     depth = nz // 4
-    rank = rank_ref[0]
+    rank = lax.axis_index("grid")
+    partner = {"grid": lax.bitwise_xor(rank, 1)}
+    barrier = pltpu.get_barrier_semaphore()
+    pl.semaphore_signal(barrier, inc=1, device_id=partner, device_id_type=MESH)
 
     def base(slot):
         return lax.bitwise_xor(rank, slot) * depth
@@ -347,11 +352,12 @@
         real_ref[here] = real
         imag_ref[here] = imag
 
-    def backward(z, kept):
+    def backward(z, kept, other):
         here = pl.ds(z, 2)
         real, imag = transform_planes(real_ref[here], imag_ref[here], loaded(6), loaded(4), True)
         visitor = vis_ref[here]
-        vis_ref[here] = real * own_ref[0, here] + imag * own_ref[1, here]
+        held = real * own_ref[0, here] + imag * own_ref[1, here]
+        vis_ref[here] = held if other is None else held + other_ref[pl.ds(other, 2)]
         for i, part in enumerate((real, imag)):
             part = part * visitor
             if not first_call:
@@ -429,58 +435,81 @@
     lax.fori_loop(0, ny // 8, tile_and_wait, 0)
     arrived(own_in + vis_in + before_in)
 
-    def backward_chunk(index, carry):
-        slot = 1 - index // per_slot
-        first = index % per_slot * CHUNK
+    pl.semaphore_wait(barrier, 1)
+
+    def sent(index):
+        part = pl.ds(index * CHUNK, CHUNK)
+        return pltpu.make_async_remote_copy(
+            src_ref=vis_ref.at[pl.ds(base(1) + index * CHUNK, CHUNK)],
+            dst_ref=other_ref.at[part],
+            send_sem=send_sem.at[index],
+            recv_sem=recv_sem.at[index],
+            device_id=partner,
+            device_id_type=MESH,
+        )
+
+    def summed(slot, index):
+        part = pl.ds(index * CHUNK, CHUNK)
+        return pltpu.make_async_copy(
+            total_ref.at[:, pl.ds(slot * depth + index * CHUNK, CHUNK)],
+            sums_hbm[slot].at[:, part],
+            sums_sem.at[slot],
+        )
+
+    def for_partner(index, carry):
         for pair in range(CHUNK // 2):
-            offset = first + 2 * pair
-            backward(base(slot) + offset, slot * depth + offset)
-        here = pl.ds(first, CHUNK)
-        for s in range(2):
-
-            @pl.when(slot == s)
-            def _():
-                pltpu.make_async_copy(
-                    vis_ref.at[pl.ds(base(s) + first, CHUNK)], held_hbm[s].at[here], held_sem.at[s]
-                ).start()
-                pltpu.make_async_copy(
-                    total_ref.at[:, pl.ds(s * depth + first, CHUNK)],
-                    sums_hbm[s].at[:, here],
-                    sums_sem.at[s],
-                ).start()
-
+            offset = index * CHUNK + 2 * pair
+            backward(base(1) + offset, depth + offset, None)
+        sent(index).start()
+        summed(1, index).start()
         return carry
 
-    lax.fori_loop(0, 2 * per_slot, backward_chunk, 0)
-    for s in (1, 0):
+    def for_self(index, carry):
+        sent(index).wait_recv()
+        for pair in range(CHUNK // 2):
+            offset = index * CHUNK + 2 * pair
+            backward(base(0) + offset, offset, offset)
         pltpu.make_async_copy(
-            vis_ref.at[pl.ds(base(s), depth)], held_hbm[s], held_sem.at[s]
-        ).wait()
+            vis_ref.at[pl.ds(base(0) + index * CHUNK, CHUNK)],
+            held_hbm.at[pl.ds(index * CHUNK, CHUNK)],
+            held_sem,
+        ).start()
+        summed(0, index).start()
+        return carry
+
+    def left(index, carry):
+        sent(index).wait_send()
+        return carry
+
+    lax.fori_loop(0, per_slot, for_partner, 0)
+    lax.fori_loop(0, per_slot, for_self, 0)
+    lax.fori_loop(0, per_slot, left, 0)
+    pltpu.make_async_copy(vis_ref.at[pl.ds(base(0), depth)], held_hbm, held_sem).wait()
+    for s in range(2):
         pltpu.make_async_copy(
             total_ref.at[:, pl.ds(s * depth, depth)], sums_hbm[s], sums_sem.at[s]
         ).wait()
 
 
-def solve_field(rank, owned, visitor, near, weights, tables, before):
+def solve_field(owned, visitor, near, weights, tables, before):
     depth, ny, nx = visitor[0].shape
     nz = 4 * depth
     first_call = before is None
     operands = list(owned) + list(visitor) + [near, weights] + list(tables)
     anywhere = pl.BlockSpec(memory_space=pl.ANY)
-    in_specs = [pl.BlockSpec(memory_space=pltpu.SMEM)] + [anywhere] * 10
+    in_specs = [anywhere] * 10
     in_specs += [pl.BlockSpec(memory_space=pltpu.VMEM)] * 8
     if not first_call:
         in_specs += [anywhere] * 2
         operands += list(before)
-    shapes = [jax.ShapeDtypeStruct(v.shape, v.dtype) for v in visitor[:2]]
-    shapes += [jax.ShapeDtypeStruct(v.shape, v.dtype) for v in owned[:2]]
+    shapes = [jax.ShapeDtypeStruct(v.shape, v.dtype) for v in [visitor[0], *owned[:2]]]
     points = nz * ny * nx
     grid = pltpu.VMEM((nz, ny, nx), jnp.float32)
     results = pl.pallas_call(
         functools.partial(field_kernel, 8, first_call),
         out_shape=shapes,
         in_specs=in_specs,
-        out_specs=[anywhere] * 4,
+        out_specs=[anywhere] * 3,
         scratch_shapes=[
             pltpu.VMEM((2, nz, ny, nx), jnp.float32),
             grid,
@@ -488,21 +517,28 @@
             grid,
             grid,
             pltpu.VMEM((2, 2 * depth, ny, nx), jnp.float32),
+            pltpu.VMEM((depth, ny, nx), jnp.float32),
             pltpu.SemaphoreType.DMA((4, 2)),
             pltpu.SemaphoreType.DMA((4, 2)),
             pltpu.SemaphoreType.DMA((2, 2)),
             pltpu.SemaphoreType.DMA((4,)),
             pltpu.SemaphoreType.DMA((2,)),
+            pltpu.SemaphoreType.DMA,
             pltpu.SemaphoreType.DMA((2,)),
-            pltpu.SemaphoreType.DMA((2,)),
+            pltpu.SemaphoreType.DMA((depth // CHUNK,)),
+            pltpu.SemaphoreType.DMA((depth // CHUNK,)),
         ],
-        compiler_params=pltpu.CompilerParams(vmem_limit_bytes=67043328),
+        compiler_params=pltpu.CompilerParams(
+            vmem_limit_bytes=67043328,
+            collective_id=0 if first_call else 1,
+            has_side_effects=True,
+        ),
         cost_estimate=pl.CostEstimate(
             flops=2 * points * 3 * 4 * nx, bytes_accessed=4 * points * 10, transcendentals=0
         ),
         name="solve_field",
-    )(rank, *operands)
-    return results[:2], results[2:]
+    )(*operands)
+    return results[0], results[1:]
 
 
 def exchanged(block, bit):
@@ -551,7 +587,6 @@
         (nx, True, False),
     ):
         tables += halves(complex_matrix(length, inverse, left))
-    rank_operand = rank.astype(jnp.int32).reshape(1)
 
     nears = []
     for j in range(count_vis):
@@ -561,9 +596,8 @@
     sums = None
     returned = []
     for j in range(count_vis):
-        held, sums = solve_field(rank_operand, owned, visitors[j], nears[j], weights, tables, sums)
-        other = exchanged(held[1], 1)
-        returned.append(passed_along(held[0] + other, "band", -1))
+        held, sums = solve_field(owned, visitors[j], nears[j], weights, tables, sums)
+        returned.append(passed_along(held, "band", -1))
 
     own_other = exchanged(sums[1], 1)
     own_rows = jnp.zeros(own_bands.shape, own_bands.dtype)

time: 824 us -> 818 us (level)
    ppermute x20 -> x16, waiting for transfers between devices: 197 us -> 187 us  [exchanged(): return lax.ppermute(block, 'grid', [(i, i ^ bit) for i in devices])]
  transfers between devices with their start and end apart: 28 -> 24, of which waited for: 16 -> 11; matrix products, arithmetic and copies ran while one was open for 2% -> 2% of each run, Pallas kernels for 22% -> 22%
where the time goes in v3:
time: 818 us; the launch traced here: 817 us
  waiting for transfers between devices  535 us (65%)
  Pallas kernels  226 us (28%)
  local copies, waits for them, and re-layouts  27.7 us (3%)
  starting transfers between devices  20.6 us (3%)
    ppermute x8, waiting for transfers between devices, passed_along(): return lax.ppermute(block, axis, route)  348 us
    ppermute x16, waiting for transfers between devices, exchanged(): return lax.ppermute(block, 'grid', [(i, i ^ bit) for i in devices])  187 us
    pallas_call x4, Pallas kernels, solve_field(): pl.pallas_call(functools.partial(field_kernel, 8, first_call), out_shape=...  176 us
    pallas_call x4, Pallas kernels, near_field(): pl.pallas_call(near_kernel, out_shape=jax.ShapeDtypeStruct((2, 2 * depth,...  50.6 us
  transfers between devices with their start and end apart: 24, of which 11 were waited for; matrix products, arithmetic and copies ran while one was open for 2% of the time, Pallas kernels for 22%

profile of v3, /device:TPU:0, one launch (start us, length us, event | category | flops | bytes accessed | tf_op | source)
XLA Modules:
  0.0 817.2 jit_solution(13732753533321430777)
XLA Ops:
  0.7 5.0 constant_dynamic-slice_fusion.1.own_0.refs_0_
  5.6 1.2 copy-done.17
  6.8 3.5 slice_bitcast_fusion
  10.3 3.0 collective-permute-start.11
  13.3 1.5 collective-permute-start.9
  14.8 2.6 constant_dynamic-slice_fusion
  17.7 1.5 collective-permute-start.7
  19.2 1.5 collective-permute-start.1
  20.7 42.4 %collective-permute-done.11.vis_0.refs_4_ = f32[32,128,128]{2,1,0:T(8,128)} collective-permute-done((f32[32,128,128]{2,1,0:T(8,128)}, f32[32,128,128]{2,1,0:T(8,128)}, u32[]{:S(2)}, u32[]{:S(2)}) %collective-permute-start.11) | collective-permute-done | bytes 2097184 | tf_op jit(solution)/shard_map/ppermute | solution.py:22
  63.1 44.8 %collective-permute-done.9.vis_0.refs_4_ = f32[32,128,128]{2,1,0:T(8,128)S(1)} collective-permute-done((f32[32,128,128]{2,1,0:T(8,128)}, f32[32,128,128]{2,1,0:T(8,128)S(1)}, u32[]{:S(2)}, u32[]{:S(2)}) %collective-permute-start.9) | collective-permute-done | bytes 2097184 | tf_op jit(solution)/shard_map/ppermute | solution.py:22
  108.0 44.9 %collective-permute-done.7.vis_0.refs_4_ = f32[32,128,128]{2,1,0:T(8,128)S(1)} collective-permute-done((f32[32,128,128]{2,1,0:T(8,128)S(1)}, f32[32,128,128]{2,1,0:T(8,128)S(1)}, u32[]{:S(2)}, u32[]{:S(2)}) %collective-permute-start.7) | collective-permute-done | bytes 2097184 | tf_op jit(solution)/shard_map/ppermute | solution.py:22
  152.9 1.7 collective-permute-start.17
  154.6 42.4 %collective-permute-done.3.vis_0.refs_4_ = f32[32,128,128]{2,1,0:T(8,128)S(1)} collective-permute-done((f32[32,128,128]{2,1,0:T(8,128)S(1)}, f32[32,128,128]{2,1,0:T(8,128)S(1)}, u32[]{:S(2)}, u32[]{:S(2)}) %collective-permute-start.3) | collective-permute-done | bytes 2097184 | tf_op jit(solution)/shard_map/ppermute | solution.py:22
  197.0 1.4 copy-done.14
  198.4 1.5 collective-permute-start.15
  200.1 0.5 collective-permute-start.2
  200.6 1.5 collective-permute-start.13
  202.1 44.9 %collective-permute-done.15.refs_6_ = f32[32,128,128]{2,1,0:T(8,128)} collective-permute-done((f32[32,128,128]{2,1,0:T(8,128)S(1)}, f32[32,128,128]{2,1,0:T(8,128)}, u32[]{:S(2)}, u32[]{:S(2)}) %collective-permute-start.15) | collective-permute-done | bytes 2097184 | tf_op jit(solution)/shard_map/ppermute | solution.py:546
  247.0 1.5 collective-permute-start.5
  248.5 1.3 copy-done.12
  250.0 131.8 %collective-permute-done.13.refs_6_ = f32[32,128,128]{2,1,0:T(8,128)} collective-permute-done((f32[32,128,128]{2,1,0:T(8,128)S(1)}, f32[32,128,128]{2,1,0:T(8,128)}, u32[]{:S(2)}, u32[]{:S(2)}) %collective-permute-start.13) | collective-permute-done | bytes 2097184 | tf_op jit(solution)/shard_map/ppermute | solution.py:546
  381.8 1.4 copy-done.10
  383.2 0.5 collective-permute-start.14
  383.7 6.5 fusion.1.order.refs_9_
  390.2 13.4 %near_field.4.order.refs_8_ = f32[2,64,128,128]{3,2,1,0:T(8,128)} custom-call(f32[2,32,128,128]{3,2,1,0:T(8,128)S(1)} %copy-done, f32[2,32,128,128]{3,2,1,0:T(8,128)S(1)} %collective-permute-done.own_1.refs_1_, f32[32,128,128]{2,1,0:T(8,128)} %collective-permute-done.11.vis_0.refs_4_, f32[32,128,128]{2,1,0:T(8,128)S(1)} %copy-done.15, ...), custom_call_target="tpu_custom_call" | custom-call | flops 2147483648 | bytes 20971520 | tf_op jit(solution)/shard_map/near_field/pallas_call | solution.py:253
  403.6 12.4 %near_field.5.order.refs_8_ = f32[2,64,128,128]{3,2,1,0:T(8,128)} custom-call(f32[2,32,128,128]{3,2,1,0:T(8,128)S(1)} %copy-done, f32[2,32,128,128]{3,2,1,0:T(8,128)S(1)} %collective-permute-done.own_1.refs_1_, f32[32,128,128]{2,1,0:T(8,128)S(1)} %collective-permute-done.9.vis_0.refs_4_, f32[32,128,128]{2,1,0:T(8,128)S(1)} %collective-permute-done.10.vis_1.refs_5_, ...), custom_call_target="tpu_custom_call" | custom-call | flops 2147483648 | bytes 20971520 | tf_op jit(solution)/shard_map/near_field/pallas_call | solution.py:253
  416.0 10.2 %collective-permute-done.5.refs_6_ = f32[32,128,128]{2,1,0:T(8,128)} collective-permute-done((f32[32,128,128]{2,1,0:T(8,128)S(1)}, f32[32,128,128]{2,1,0:T(8,128)}, u32[]{:S(2)}, u32[]{:S(2)}) %collective-permute-start.5) | collective-permute-done | bytes 2097184 | tf_op jit(solution)/shard_map/ppermute | solution.py:546
  426.3 12.4 %near_field.6.order.refs_8_ = f32[2,64,128,128]{3,2,1,0:T(8,128)} custom-call(f32[2,32,128,128]{3,2,1,0:T(8,128)S(1)} %copy-done, f32[2,32,128,128]{3,2,1,0:T(8,128)S(1)} %collective-permute-done.own_1.refs_1_, f32[32,128,128]{2,1,0:T(8,128)S(1)} %collective-permute-done.7.vis_0.refs_4_, f32[32,128,128]{2,1,0:T(8,128)S(1)} %copy-done.13, ...), custom_call_target="tpu_custom_call" | custom-call | flops 2147483648 | bytes 20971520 | tf_op jit(solution)/shard_map/near_field/pallas_call | solution.py:253
  438.7 12.4 %near_field.7.refs_8_ = f32[2,64,128,128]{3,2,1,0:T(8,128)} custom-call(f32[2,32,128,128]{3,2,1,0:T(8,128)S(1)} %copy-done, f32[2,32,128,128]{3,2,1,0:T(8,128)S(1)} %collective-permute-done.own_1.refs_1_, f32[32,128,128]{2,1,0:T(8,128)S(1)} %collective-permute-done.3.vis_0.refs_4_, f32[32,128,128]{2,1,0:T(8,128)S(1)} %copy-done.11, ...), custom_call_target="tpu_custom_call" | custom-call | flops 2147483648 | bytes 20971520 | tf_op jit(solution)/shard_map/near_field/pallas_call | solution.py:253
  451.2 43.8 %solve_field.4 = (f32[32,128,128]{2,1,0:T(8,128)}, f32[2,32,128,128]{3,2,1,0:T(8,128)}, f32[2,32,128,128]{3,2,1,0:T(8,128)}) custom-call(f32[2,32,128,128]{3,2,1,0:T(8,128)} %constant_dynamic-slice_fusion.1.own_0.refs_0_, f32[2,32,128,128]{3,2,1,0:T(8,128)} %copy-done.1, f32[2,32,128,128]{3,2,1,0:T(8,128)} %copy-done.16, ...), custom_call_target="tpu_custom_call" | custom-call | flops 6442450944 | bytes 83886080 | tf_op jit(solution)/shard_map/solve_field/pallas_call | solution.py:508
  495.1 44.1 %solve_field.5 = (f32[32,128,128]{2,1,0:T(8,128)}, f32[2,32,128,128]{3,2,1,0:T(8,128)}, f32[2,32,128,128]{3,2,1,0:T(8,128)}) custom-call(f32[2,32,128,128]{3,2,1,0:T(8,128)} %constant_dynamic-slice_fusion.1.own_0.refs_0_, f32[2,32,128,128]{3,2,1,0:T(8,128)} %copy-done.1, f32[2,32,128,128]{3,2,1,0:T(8,128)} %copy-done.16, ...), custom_call_target="tpu_custom_call" | custom-call | flops 6442450944 | bytes 83886080 | tf_op jit(solution)/shard_map/solve_field/pallas_call | solution.py:508
  539.1 43.9 %solve_field.6 = (f32[32,128,128]{2,1,0:T(8,128)}, f32[2,32,128,128]{3,2,1,0:T(8,128)}, f32[2,32,128,128]{3,2,1,0:T(8,128)}) custom-call(f32[2,32,128,128]{3,2,1,0:T(8,128)} %constant_dynamic-slice_fusion.1.own_0.refs_0_, f32[2,32,128,128]{3,2,1,0:T(8,128)} %copy-done.1, f32[2,32,128,128]{3,2,1,0:T(8,128)} %copy-done.16, ...), custom_call_target="tpu_custom_call" | custom-call | flops 6442450944 | bytes 83886080 | tf_op jit(solution)/shard_map/solve_field/pallas_call | solution.py:508
  583.1 43.9 %solve_field.7 = (f32[32,128,128]{2,1,0:T(8,128)}, f32[2,32,128,128]{3,2,1,0:T(8,128)}, f32[2,32,128,128]{3,2,1,0:T(8,128)}) custom-call(f32[2,32,128,128]{3,2,1,0:T(8,128)} %constant_dynamic-slice_fusion.1.own_0.refs_0_, f32[2,32,128,128]{3,2,1,0:T(8,128)} %copy-done.1, f32[2,32,128,128]{3,2,1,0:T(8,128)} %copy-done.16, ...), custom_call_target="tpu_custom_call" | custom-call | flops 6442450944 | bytes 83886080 | tf_op jit(solution)/shard_map/solve_field/pallas_call | solution.py:508
  627.0 0.6 collective-permute-start.19
  627.6 1.7 collective-permute-start.20
  629.3 1.4 collective-permute-start.21
  631.2 1.4 collective-permute-start.23
  632.6 1.0 broadcast.199
  633.7 1.1 copy-done.20
  634.8 0.5 constant_dynamic-update-slice_fusion.1
  635.4 40.9 %collective-permute-done.20 = f32[32,128,128]{2,1,0:T(8,128)S(1)} collective-permute-done((f32[32,128,128]{2,1,0:T(8,128)}, f32[32,128,128]{2,1,0:T(8,128)S(1)}, u32[]{:S(2)}, u32[]{:S(2)}) %collective-permute-start.20) | collective-permute-done | bytes 2097184 | tf_op jit(solution)/shard_map/ppermute | solution.py:22
  676.3 1.0 dynamic_update_slice.20
  677.3 43.9 %collective-permute-done.21 = f32[32,128,128]{2,1,0:T(8,128)S(1)} collective-permute-done((f32[32,128,128]{2,1,0:T(8,128)}, f32[32,128,128]{2,1,0:T(8,128)S(1)}, u32[]{:S(2)}, u32[]{:S(2)}) %collective-permute-start.21) | collective-permute-done | bytes 2097184 | tf_op jit(solution)/shard_map/ppermute | solution.py:22
  721.4 44.7 %collective-permute-done.22 = f32[32,128,128]{2,1,0:T(8,128)S(1)} collective-permute-done((f32[32,128,128]{2,1,0:T(8,128)}, f32[32,128,128]{2,1,0:T(8,128)S(1)}, u32[]{:S(2)}, u32[]{:S(2)}) %collective-permute-start.22) | collective-permute-done | bytes 2097184 | tf_op jit(solution)/shard_map/ppermute | solution.py:22
  766.4 43.8 %collective-permute-done.23 = f32[32,128,128]{2,1,0:T(8,128)S(1)} collective-permute-done((f32[32,128,128]{2,1,0:T(8,128)}, f32[32,128,128]{2,1,0:T(8,128)S(1)}, u32[]{:S(2)}, u32[]{:S(2)}) %collective-permute-start.23) | collective-permute-done | bytes 2097184 | tf_op jit(solution)/shard_map/ppermute | solution.py:22
  810.4 0.6 constant_dynamic-update-slice_fusion
  811.1 2.7 copy-done.18
  813.8 3.4 copy-done.19
  (68 shorter events, 1.8 us)
Async XLA Ops:
  0.6 6.2 copy-start.17
  10.3 52.8 %collective-permute-start.11 = (f32[32,128,128]{2,1,0:T(8,128)}, f32[32,128,128]{2,1,0:T(8,128)}, u32[]{:S(2)}, u32[]{:S(2)}) collective-permute-start(f32[32,128,128]{2,1,0:T(8,128)} %get-tuple-element.30), channel_id=1, source_target_pairs={{28,0},{0,4},{4,8},{8,12},{12,16},{16,20},{20,24},{24,28},{29,1},{... | collective-permute-start | bytes 6291464 | tf_op jit(solution)/shard_map/ppermute | solution.py:22
  13.3 94.7 %collective-permute-start.9 = (f32[32,128,128]{2,1,0:T(8,128)}, f32[32,128,128]{2,1,0:T(8,128)S(1)}, u32[]{:S(2)}, u32[]{:S(2)}) collective-permute-start(f32[32,128,128]{2,1,0:T(8,128)} %get-tuple-element.31), channel_id=1, source_target_pairs={{28,0},{0,4},{4,8},{8,12},{12,16},{16,20},{20,24},{24,28},{29,1},{... | collective-permute-start | bytes 6291464 | tf_op jit(solution)/shard_map/ppermute | solution.py:22
  14.8 2.9 copy-start.22
  14.8 4.4 copy-start
  14.8 48.3 %copy-start.21 = (f32[32,128,128]{2,1,0:T(8,128)S(1)}, f32[32,128,128]{2,1,0:T(8,128)}, u32[]{:S(2)}) copy-start(f32[32,128,128]{2,1,0:T(8,128)} %get-tuple-element.33) | copy-start | bytes 6291460
  17.4 182.5 %collective-permute-start = (f32[2,32,128,128]{3,2,1,0:T(8,128)S(1)}, f32[2,32,128,128]{3,2,1,0:T(8,128)S(1)}, u32[]{:S(2)}, u32[]{:S(2)}) collective-permute-start(f32[2,32,128,128]{3,2,1,0:T(8,128)S(1)} %constant_dynamic-slice_fusion), channel_id=1, source_target_pairs={{0,1},{1,0},{2,3},{3,2},{4,5},{5,4},{6,7},{7,6},{8,9},{9,8},{10,11... | collective-permute-start | bytes 12582920 | tf_op jit(solution)/shard_map/ppermute | solution.py:546
  17.7 135.2 %collective-permute-start.7 = (f32[32,128,128]{2,1,0:T(8,128)S(1)}, f32[32,128,128]{2,1,0:T(8,128)S(1)}, u32[]{:S(2)}, u32[]{:S(2)}) collective-permute-start(f32[32,128,128]{2,1,0:T(8,128)S(1)} %copy-done.22), channel_id=1, source_target_pairs={{28,0},{0,4},{4,8},{8,12},{12,16},{16,20},{20,24},{24,28},{29,1},{... | collective-permute-start | bytes 6291464 | tf_op jit(solution)/shard_map/ppermute | solution.py:22
  19.2 181.4 %collective-permute-start.1 = (f32[2,32,128,128]{3,2,1,0:T(8,128)S(1)}, f32[2,32,128,128]{3,2,1,0:T(8,128)S(1)}, u32[]{:S(2)}, u32[]{:S(2)}) collective-permute-start(f32[2,32,128,128]{3,2,1,0:T(8,128)S(1)} %copy-done), channel_id=1, source_target_pairs={{0,2},{1,3},{2,0},{3,1},{4,6},{5,7},{6,4},{7,5},{8,10},{9,11},{10,... | collective-permute-start | bytes 12582920 | tf_op jit(solution)/shard_map/ppermute | solution.py:546
  63.1 133.9 %collective-permute-start.3 = (f32[32,128,128]{2,1,0:T(8,128)S(1)}, f32[32,128,128]{2,1,0:T(8,128)S(1)}, u32[]{:S(2)}, u32[]{:S(2)}) collective-permute-start(f32[32,128,128]{2,1,0:T(8,128)S(1)} %copy-done.21), channel_id=1, source_target_pairs={{28,0},{0,4},{4,8},{8,12},{12,16},{16,20},{20,24},{24,28},{29,1},{... | collective-permute-start | bytes 6291464 | tf_op jit(solution)/shard_map/ppermute | solution.py:22
  108.0 295.6 %copy-start.6 = (f32[32,128,128]{2,1,0:T(8,128)}, f32[32,128,128]{2,1,0:T(8,128)S(1)}, u32[]{:S(2)}) copy-start(f32[32,128,128]{2,1,0:T(8,128)S(1)} %collective-permute-done.9.vis_0.refs_4_) | copy-start | bytes 6291460
  108.0 89.0 %collective-permute-start.12 = (f32[32,128,128]{2,1,0:T(8,128)}, f32[32,128,128]{2,1,0:T(8,128)S(1)}, u32[]{:S(2)}, u32[]{:S(2)}) collective-permute-start(f32[32,128,128]{2,1,0:T(8,128)} %collective-permute-done.11.vis_0.refs_4_), channel_id=1, source_target_pairs={{0,1},{1,0},{2,3},{3,2},{4,5},{5,4},{6,7},{7,6},{8,9},{9,8},{10,11... | collective-permute-start | bytes 6291464 | tf_op jit(solution)/shard_map/ppermute | solution.py:546
  152.9 273.4 %copy-start.8 = (f32[32,128,128]{2,1,0:T(8,128)}, f32[32,128,128]{2,1,0:T(8,128)S(1)}, u32[]{:S(2)}) copy-start(f32[32,128,128]{2,1,0:T(8,128)S(1)} %collective-permute-done.7.vis_0.refs_4_) | copy-start | bytes 6291460
  152.9 47.2 %collective-permute-start.17 = (f32[32,128,128]{2,1,0:T(8,128)}, f32[32,128,128]{2,1,0:T(8,128)}, u32[]{:S(2)}, u32[]{:S(2)}) collective-permute-start(f32[32,128,128]{2,1,0:T(8,128)} %collective-permute-done.11.vis_0.refs_4_), channel_id=1, source_target_pairs={{0,2},{1,3},{2,0},{3,1},{4,6},{5,7},{6,4},{7,5},{8,10},{9,11},{10,... | collective-permute-start | bytes 6291464 | tf_op jit(solution)/shard_map/ppermute | solution.py:546
  197.0 241.7 %copy-start.7 = (f32[32,128,128]{2,1,0:T(8,128)}, f32[32,128,128]{2,1,0:T(8,128)S(1)}, u32[]{:S(2)}) copy-start(f32[32,128,128]{2,1,0:T(8,128)S(1)} %collective-permute-done.3.vis_0.refs_4_) | copy-start | bytes 6291460
  197.0 5.1 collective-permute-start.10
  197.0 1.4 copy-start.14
  198.4 48.6 %collective-permute-start.15 = (f32[32,128,128]{2,1,0:T(8,128)S(1)}, f32[32,128,128]{2,1,0:T(8,128)}, u32[]{:S(2)}, u32[]{:S(2)}) collective-permute-start(f32[32,128,128]{2,1,0:T(8,128)S(1)} %collective-permute-done.9.vis_0.refs_4_), channel_id=1, source_target_pairs={{0,2},{1,3},{2,0},{3,1},{4,6},{5,7},{6,4},{7,5},{8,10},{9,11},{10,... | collective-permute-start | bytes 6291464 | tf_op jit(solution)/shard_map/ppermute | solution.py:546
  199.9 238.8 %copy-start.1 = (f32[2,32,128,128]{3,2,1,0:T(8,128)}, f32[2,32,128,128]{3,2,1,0:T(8,128)S(1)}, u32[]{:S(2)}) copy-start(f32[2,32,128,128]{3,2,1,0:T(8,128)S(1)} %collective-permute-done.own_1.refs_1_) | copy-start | bytes 12582916
  199.9 48.6 %collective-permute-start.8 = (f32[32,128,128]{2,1,0:T(8,128)S(1)}, f32[32,128,128]{2,1,0:T(8,128)S(1)}, u32[]{:S(2)}, u32[]{:S(2)}) collective-permute-start(f32[32,128,128]{2,1,0:T(8,128)S(1)} %collective-permute-done.7.vis_0.refs_4_), channel_id=1, source_target_pairs={{0,1},{1,0},{2,3},{3,2},{4,5},{5,4},{6,7},{7,6},{8,9},{9,8},{10,11... | collective-permute-start | bytes 6291464 | tf_op jit(solution)/shard_map/ppermute | solution.py:546
  200.1 251.1 %collective-permute-start.2 = (f32[2,32,128,128]{3,2,1,0:T(8,128)S(1)}, f32[2,32,128,128]{3,2,1,0:T(8,128)}, u32[]{:S(2)}, u32[]{:S(2)}) collective-permute-start(f32[2,32,128,128]{3,2,1,0:T(8,128)S(1)} %collective-permute-done.own_1.refs_1_), channel_id=1, source_target_pairs={{0,2},{1,3},{2,0},{3,1},{4,6},{5,7},{6,4},{7,5},{8,10},{9,11},{10,... | collective-permute-start | bytes 12582920 | tf_op jit(solution)/shard_map/ppermute | solution.py:546
  200.6 46.4 %copy-start.16 = (f32[2,32,128,128]{3,2,1,0:T(8,128)}, f32[2,32,128,128]{3,2,1,0:T(8,128)S(1)}, u32[]{:S(2)}) copy-start(f32[2,32,128,128]{3,2,1,0:T(8,128)S(1)} %collective-permute-done.1.refs_2_) | copy-start | bytes 12582916
  200.6 181.2 %collective-permute-start.13 = (f32[32,128,128]{2,1,0:T(8,128)S(1)}, f32[32,128,128]{2,1,0:T(8,128)}, u32[]{:S(2)}, u32[]{:S(2)}) collective-permute-start(f32[32,128,128]{2,1,0:T(8,128)S(1)} %collective-permute-done.7.vis_0.refs_4_), channel_id=1, source_target_pairs={{0,2},{1,3},{2,0},{3,1},{4,6},{5,7},{6,4},{7,5},{8,10},{9,11},{10,... | collective-permute-start | bytes 6291464 | tf_op jit(solution)/shard_map/ppermute | solution.py:546
  202.1 201.4 %copy-start.9 = (f32[32,128,128]{2,1,0:T(8,128)}, f32[32,128,128]{2,1,0:T(8,128)S(1)}, u32[]{:S(2)}) copy-start(f32[32,128,128]{2,1,0:T(8,128)S(1)} %collective-permute-done.10.vis_1.refs_5_) | copy-start | bytes 6291460
  202.1 179.7 %collective-permute-start.4 = (f32[32,128,128]{2,1,0:T(8,128)S(1)}, f32[32,128,128]{2,1,0:T(8,128)S(1)}, u32[]{:S(2)}, u32[]{:S(2)}) collective-permute-start(f32[32,128,128]{2,1,0:T(8,128)S(1)} %collective-permute-done.3.vis_0.refs_4_), channel_id=1, source_target_pairs={{0,1},{1,0},{2,3},{3,2},{4,5},{5,4},{6,7},{7,6},{8,9},{9,8},{10,11... | collective-permute-start | bytes 6291464 | tf_op jit(solution)/shard_map/ppermute | solution.py:546
  247.0 179.3 %collective-permute-start.5 = (f32[32,128,128]{2,1,0:T(8,128)S(1)}, f32[32,128,128]{2,1,0:T(8,128)}, u32[]{:S(2)}, u32[]{:S(2)}) collective-permute-start(f32[32,128,128]{2,1,0:T(8,128)S(1)} %collective-permute-done.3.vis_0.refs_4_), channel_id=1, source_target_pairs={{0,2},{1,3},{2,0},{3,1},{4,6},{5,7},{6,4},{7,5},{8,10},{9,11},{10,... | collective-permute-start | bytes 6291464 | tf_op jit(solution)/shard_map/ppermute | solution.py:546
  248.5 1.3 copy-start.12
  249.8 201.3 %collective-permute-start.18 = (f32[32,128,128]{2,1,0:T(8,128)}, f32[32,128,128]{2,1,0:T(8,128)}, u32[]{:S(2)}, u32[]{:S(2)}) collective-permute-start(f32[32,128,128]{2,1,0:T(8,128)} %collective-permute-done.17.refs_6_), channel_id=1, source_target_pairs={{0,1},{1,0},{2,3},{3,2},{4,5},{5,4},{6,7},{7,6},{8,9},{9,8},{10,11... | collective-permute-start | bytes 6291464 | tf_op jit(solution)/shard_map/ppermute | solution.py:546
  249.9 140.2 %copy-start.2 = (bf16[256,256]{1,0:T(8,128)(2,1)S(1)}, bf16[256,256]{1,0:T(8,128)(2,1)}, u32[]{:S(2)}) copy-start(bf16[256,256]{1,0:T(8,128)(2,1)} %constant.100.clone.x_low.refs_11_.refs_15_) | copy-start | bytes 393220
  249.9 140.2 %copy-start.3 = (bf16[256,256]{1,0:T(8,128)(2,1)S(1)}, bf16[256,256]{1,0:T(8,128)(2,1)}, u32[]{:S(2)}) copy-start(bf16[256,256]{1,0:T(8,128)(2,1)} %constant.101.clone.y_high.refs_12_.refs_16_) | copy-start | bytes 393220
  249.9 140.2 %copy-start.4 = (bf16[256,256]{1,0:T(8,128)(2,1)S(1)}, bf16[256,256]{1,0:T(8,128)(2,1)}, u32[]{:S(2)}) copy-start(bf16[256,256]{1,0:T(8,128)(2,1)} %constant.102.clone.y_low.refs_13_.refs_17_) | copy-start | bytes 393220
  250.0 140.2 %copy-start.5 = (bf16[256,256]{1,0:T(8,128)(2,1)S(1)}, bf16[256,256]{1,0:T(8,128)(2,1)}, u32[]{:S(2)}) copy-start(bf16[256,256]{1,0:T(8,128)(2,1)} %constant.99.clone.x_high.refs_10_.refs_14_) | copy-start | bytes 393220
  250.0 140.2 %copy-start.15 = (f32[32,128,128]{2,1,0:T(8,128)S(1)}, f32[32,128,128]{2,1,0:T(8,128)}, u32[]{:S(2)}) copy-start(f32[32,128,128]{2,1,0:T(8,128)} %copy-done.14) | copy-start | bytes 6291460
  381.8 113.2 %collective-permute-start.16 = (f32[32,128,128]{2,1,0:T(8,128)}, f32[32,128,128]{2,1,0:T(8,128)}, u32[]{:S(2)}, u32[]{:S(2)}) collective-permute-start(f32[32,128,128]{2,1,0:T(8,128)} %collective-permute-done.15.refs_6_), channel_id=1, source_target_pairs={{0,1},{1,0},{2,3},{3,2},{4,5},{5,4},{6,7},{7,6},{8,9},{9,8},{10,11... | collective-permute-start | bytes 6291464 | tf_op jit(solution)/shard_map/ppermute | solution.py:546
  381.8 1.4 copy-start.10
  383.2 155.9 %collective-permute-start.14 = (f32[32,128,128]{2,1,0:T(8,128)}, f32[32,128,128]{2,1,0:T(8,128)}, u32[]{:S(2)}, u32[]{:S(2)}) collective-permute-start(f32[32,128,128]{2,1,0:T(8,128)} %collective-permute-done.13.refs_6_), channel_id=1, source_target_pairs={{0,1},{1,0},{2,3},{3,2},{4,5},{5,4},{6,7},{7,6},{8,9},{9,8},{10,11... | collective-permute-start | bytes 6291464 | tf_op jit(solution)/shard_map/ppermute | solution.py:546
  403.6 22.7 %copy-start.13 = (f32[32,128,128]{2,1,0:T(8,128)S(1)}, f32[32,128,128]{2,1,0:T(8,128)}, u32[]{:S(2)}) copy-start(f32[32,128,128]{2,1,0:T(8,128)} %copy-done.12) | copy-start | bytes 6291460
  416.0 22.7 %copy-start.11 = (f32[32,128,128]{2,1,0:T(8,128)S(1)}, f32[32,128,128]{2,1,0:T(8,128)}, u32[]{:S(2)}) copy-start(f32[32,128,128]{2,1,0:T(8,128)} %copy-done.10) | copy-start | bytes 6291460
  426.3 156.8 %collective-permute-start.6 = (f32[32,128,128]{2,1,0:T(8,128)}, f32[32,128,128]{2,1,0:T(8,128)}, u32[]{:S(2)}, u32[]{:S(2)}) collective-permute-start(f32[32,128,128]{2,1,0:T(8,128)} %collective-permute-done.5.refs_6_), channel_id=1, source_target_pairs={{0,1},{1,0},{2,3},{3,2},{4,5},{5,4},{6,7},{7,6},{8,9},{9,8},{10,11... | collective-permute-start | bytes 6291464 | tf_op jit(solution)/shard_map/ppermute | solution.py:546
  627.0 183.4 %collective-permute-start.19 = (f32[2,32,128,128]{3,2,1,0:T(8,128)}, f32[2,32,128,128]{3,2,1,0:T(8,128)S(1)}, u32[]{:S(2)}, u32[]{:S(2)}) collective-permute-start(f32[2,32,128,128]{3,2,1,0:T(8,128)} %get-tuple-element.25), channel_id=1, source_target_pairs={{0,1},{1,0},{2,3},{3,2},{4,5},{5,4},{6,7},{7,6},{8,9},{9,8},{10,11... | collective-permute-start | bytes 12582920 | tf_op jit(solution)/shard_map/ppermute | solution.py:546
  627.6 48.7 %collective-permute-start.20 = (f32[32,128,128]{2,1,0:T(8,128)}, f32[32,128,128]{2,1,0:T(8,128)S(1)}, u32[]{:S(2)}, u32[]{:S(2)}) collective-permute-start(f32[32,128,128]{2,1,0:T(8,128)} %get-tuple-element.26), channel_id=1, source_target_pairs={{4,0},{8,4},{12,8},{16,12},{20,16},{24,20},{28,24},{0,28},{5,1},{9... | collective-permute-start | bytes 6291464 | tf_op jit(solution)/shard_map/ppermute | solution.py:22
  629.3 91.9 %collective-permute-start.21 = (f32[32,128,128]{2,1,0:T(8,128)}, f32[32,128,128]{2,1,0:T(8,128)S(1)}, u32[]{:S(2)}, u32[]{:S(2)}) collective-permute-start(f32[32,128,128]{2,1,0:T(8,128)} %get-tuple-element.27), channel_id=1, source_target_pairs={{4,0},{8,4},{12,8},{16,12},{20,16},{24,20},{28,24},{0,28},{5,1},{9... | collective-permute-start | bytes 6291464 | tf_op jit(solution)/shard_map/ppermute | solution.py:22
  630.7 135.4 %collective-permute-start.22 = (f32[32,128,128]{2,1,0:T(8,128)}, f32[32,128,128]{2,1,0:T(8,128)S(1)}, u32[]{:S(2)}, u32[]{:S(2)}) collective-permute-start(f32[32,128,128]{2,1,0:T(8,128)} %get-tuple-element.28), channel_id=1, source_target_pairs={{4,0},{8,4},{12,8},{16,12},{20,16},{24,20},{28,24},{0,28},{5,1},{9... | collective-permute-start | bytes 6291464 | tf_op jit(solution)/shard_map/ppermute | solution.py:22
  631.2 179.0 %collective-permute-start.23 = (f32[32,128,128]{2,1,0:T(8,128)}, f32[32,128,128]{2,1,0:T(8,128)S(1)}, u32[]{:S(2)}, u32[]{:S(2)}) collective-permute-start(f32[32,128,128]{2,1,0:T(8,128)} %get-tuple-element.29), channel_id=1, source_target_pairs={{4,0},{8,4},{12,8},{16,12},{20,16},{24,20},{28,24},{0,28},{5,1},{9... | collective-permute-start | bytes 6291464 | tf_op jit(solution)/shard_map/ppermute | solution.py:22
  632.6 2.2 copy-start.20
  810.4 3.4 copy-start.18
  813.8 3.4 copy-start.19

commit v4 on v3

--- a/solution.py
+++ b/solution.py
@@ -278,14 +278,14 @@
         del refs[:count]
         return taken
 
-    own_hbm, vis_hbm = take(4), take(4)
+    own_hbm, vis_hbm = take(4), take(3)
     near_hbm, weights_hbm = take(2)
     tables = take(8)
     before_hbm = [] if first_call else take(2)
     (held_hbm,), sums_hbm = take(1), take(2)
     own_ref, vis_ref, real_ref, imag_ref, weights_ref, total_ref, other_ref = take(7)
     own_sem, vis_sem, near_sem, weights_sem, before_sem, held_sem, sums_sem = take(7)
-    send_sem, recv_sem = refs
+    send_sem, recv_sem, cross_sem, crossed_sem = refs
     nz, ny, _ = real_ref.shape
     depth = nz // 4
     rank = lax.axis_index("grid")
@@ -317,12 +317,15 @@
                 [
                     pltpu.make_async_copy(
                         own_hbm[s].at[:, part], own_ref.at[:, here], own_sem.at[s, h]
-                    ),
+                    )
+                ]
+            )
+            if s == 2:
+                far_in[-1].append(
                     pltpu.make_async_copy(
                         vis_hbm[s].at[part], vis_ref.at[here], vis_sem.at[s, h]
-                    ),
-                ]
-            )
+                    )
+                )
     stripes = weights_sem.shape[0]
     stripe = ny // stripes
     weights_in = []
@@ -338,7 +341,19 @@
         for copy in copies:
             copy.start()
 
+    def crossing(h):
+        return pltpu.make_async_remote_copy(
+            src_ref=vis_hbm[2].at[pl.ds(h * half, half)],
+            dst_ref=vis_ref.at[pl.ds(base(2) + h * half, half)],
+            send_sem=cross_sem.at[h],
+            recv_sem=crossed_sem.at[h],
+            device_id=partner,
+            device_id_type=MESH,
+        )
+
     start(far_in[0])
+    pl.semaphore_wait(barrier, 1)
+    start([crossing(0), crossing(1)])
 
     def loaded(index):
         return tables[index][...], tables[index + 1][...]
@@ -411,6 +426,8 @@
             @pl.when(index == h * per_half)
             def _():
                 arrived(far_in[h])
+                if h >= 2:
+                    crossing(h - 2).wait_recv()
                 start(later)
 
         first = base(2 + index // per_slot) + index % per_slot * CHUNK
@@ -434,8 +451,6 @@
 
     lax.fori_loop(0, ny // 8, tile_and_wait, 0)
     arrived(own_in + vis_in + before_in)
-
-    pl.semaphore_wait(barrier, 1)
 
     def sent(index):
         part = pl.ds(index * CHUNK, CHUNK)
@@ -484,6 +499,8 @@
     lax.fori_loop(0, per_slot, for_partner, 0)
     lax.fori_loop(0, per_slot, for_self, 0)
     lax.fori_loop(0, per_slot, left, 0)
+    for h in range(2):
+        crossing(h).wait_send()
     pltpu.make_async_copy(vis_ref.at[pl.ds(base(0), depth)], held_hbm, held_sem).wait()
     for s in range(2):
         pltpu.make_async_copy(
@@ -497,7 +514,7 @@
     first_call = before is None
     operands = list(owned) + list(visitor) + [near, weights] + list(tables)
     anywhere = pl.BlockSpec(memory_space=pl.ANY)
-    in_specs = [anywhere] * 10
+    in_specs = [anywhere] * 9
     in_specs += [pl.BlockSpec(memory_space=pltpu.VMEM)] * 8
     if not first_call:
         in_specs += [anywhere] * 2
@@ -527,6 +544,8 @@
             pltpu.SemaphoreType.DMA((2,)),
             pltpu.SemaphoreType.DMA((depth // CHUNK,)),
             pltpu.SemaphoreType.DMA((depth // CHUNK,)),
+            pltpu.SemaphoreType.DMA((2,)),
+            pltpu.SemaphoreType.DMA((2,)),
         ],
         compiler_params=pltpu.CompilerParams(
             vmem_limit_bytes=67043328,
@@ -570,8 +589,7 @@
         near = passed_along(travel_bands[j], "band", 1)
         far = exchanged(near, 2)
         side = exchanged(near, 1)
-        cross = exchanged(far, 1)
-        visitors.append([near, side, far, cross])
+        visitors.append([near, side, far])
 
     radix = 8
     slot = jnp.arange(nz, dtype=jnp.int32)

time: 818 us -> 708 us (0.87)
  waiting for transfers between devices: 535 us -> 427 us
    ppermute x16 -> x12, waiting for transfers between devices: 187 us -> 78.1 us  [exchanged(): return lax.ppermute(block, 'grid', [(i, i ^ bit) for i in devices])]
  transfers between devices with their start and end apart: 24 -> 20, of which waited for: 11 -> 13; matrix products, arithmetic and copies ran while one was open for 2% -> 2% of each run, Pallas kernels for 22% -> 26%
where the time goes in v4:
time: 708 us; the launch traced here: 707 us
  waiting for transfers between devices  427 us (60%)
  Pallas kernels  228 us (32%)
  local copies, waits for them, and re-layouts  23.5 us (3%)
  starting transfers between devices  21.4 us (3%)
    ppermute x8, waiting for transfers between devices, passed_along(): return lax.ppermute(block, axis, route)  349 us
    pallas_call x4, Pallas kernels, solve_field(): pl.pallas_call(functools.partial(field_kernel, 8, first_call), out_shape=...  175 us
    ppermute x12, waiting for transfers between devices, exchanged(): return lax.ppermute(block, 'grid', [(i, i ^ bit) for i in devices])  78.1 us
    pallas_call x4, Pallas kernels, near_field(): pl.pallas_call(near_kernel, out_shape=jax.ShapeDtypeStruct((2, 2 * depth,...  52.7 us
  transfers between devices with their start and end apart: 20, of which 13 were waited for; matrix products, arithmetic and copies ran while one was open for 2% of the time, Pallas kernels for 26%

profile of v4, /device:TPU:0, one launch (start us, length us, event | category | flops | bytes accessed | tf_op | source)
XLA Modules:
  0.0 707.1 jit_solution(6780169692429524258)
XLA Ops:
  0.6 4.7 constant_dynamic-slice_fusion.1.own_0.refs_0_
  5.3 2.6 constant_dynamic-slice_fusion
  8.0 0.6 collective-permute-start
  8.5 1.5 copy-done.11
  10.0 3.5 slice_bitcast_fusion
  13.5 3.0 collective-permute-start.10
  16.5 1.5 collective-permute-start.8
  18.0 1.5 collective-permute-start.6
  19.5 1.5 collective-permute-start.3
  21.1 45.2 %collective-permute-done.10.vis_0.refs_4_ = f32[32,128,128]{2,1,0:T(8,128)S(1)} collective-permute-done((f32[32,128,128]{2,1,0:T(8,128)}, f32[32,128,128]{2,1,0:T(8,128)S(1)}, u32[]{:S(2)}, u32[]{:S(2)}) %collective-permute-start.10) | collective-permute-done | bytes 2097184 | tf_op jit(solution)/shard_map/ppermute | solution.py:22
  66.2 45.0 %collective-permute-done.8.vis_0.refs_4_ = f32[32,128,128]{2,1,0:T(8,128)} collective-permute-done((f32[32,128,128]{2,1,0:T(8,128)}, f32[32,128,128]{2,1,0:T(8,128)}, u32[]{:S(2)}, u32[]{:S(2)}) %collective-permute-start.8) | collective-permute-done | bytes 2097184 | tf_op jit(solution)/shard_map/ppermute | solution.py:22
  111.3 1.7 collective-permute-start.14
  112.9 43.3 %collective-permute-done.6.vis_0.refs_4_ = f32[32,128,128]{2,1,0:T(8,128)} collective-permute-done((f32[32,128,128]{2,1,0:T(8,128)}, f32[32,128,128]{2,1,0:T(8,128)}, u32[]{:S(2)}, u32[]{:S(2)}) %collective-permute-start.6) | collective-permute-done | bytes 2097184 | tf_op jit(solution)/shard_map/ppermute | solution.py:22
  156.2 1.7 collective-permute-start.1
  158.2 42.1 %collective-permute-done.3.vis_0.refs_4_ = f32[32,128,128]{2,1,0:T(8,128)} collective-permute-done((f32[32,128,128]{2,1,0:T(8,128)}, f32[32,128,128]{2,1,0:T(8,128)}, u32[]{:S(2)}, u32[]{:S(2)}) %collective-permute-start.3) | collective-permute-done | bytes 2097184 | tf_op jit(solution)/shard_map/ppermute | solution.py:22
  200.3 0.5 collective-permute-start.7
  201.1 3.6 collective-permute-done.9.vis_1.refs_5_
  204.7 1.5 collective-permute-start.13
  206.2 1.5 collective-permute-done.7.vis_1.refs_5_
  207.7 1.5 collective-permute-start.12
  209.2 6.5 fusion.1.order.refs_8_
  215.7 12.4 %near_field.4.order.refs_7_ = f32[2,64,128,128]{3,2,1,0:T(8,128)} custom-call(f32[2,32,128,128]{3,2,1,0:T(8,128)S(1)} %copy-done, f32[2,32,128,128]{3,2,1,0:T(8,128)S(1)} %collective-permute-done.own_1.refs_1_, f32[32,128,128]{2,1,0:T(8,128)S(1)} %collective-permute-done.10.vis_0.refs_4_, f32[32,128,128]{2,1,0:T(8,128)S(1)} %collective-permute-done.11.vis_1.refs_5_, ...), custom_call_target="tpu_custom_call" | custom-call | flops 2147483648 | bytes 20971520 | tf_op jit(solution)/shard_map/near_field/pallas_call | solution.py:253
  228.1 13.5 %near_field.5.order.refs_7_ = f32[2,64,128,128]{3,2,1,0:T(8,128)} custom-call(f32[2,32,128,128]{3,2,1,0:T(8,128)S(1)} %copy-done, f32[2,32,128,128]{3,2,1,0:T(8,128)S(1)} %collective-permute-done.own_1.refs_1_, f32[32,128,128]{2,1,0:T(8,128)} %collective-permute-done.8.vis_0.refs_4_, f32[32,128,128]{2,1,0:T(8,128)S(1)} %collective-permute-done.9.vis_1.refs_5_, ...), custom_call_target="tpu_custom_call" | custom-call | flops 2147483648 | bytes 20971520 | tf_op jit(solution)/shard_map/near_field/pallas_call | solution.py:253
  241.5 0.6 collective-permute-start.5
  242.1 13.4 %near_field.6.order.refs_7_ = f32[2,64,128,128]{3,2,1,0:T(8,128)} custom-call(f32[2,32,128,128]{3,2,1,0:T(8,128)S(1)} %copy-done, f32[2,32,128,128]{3,2,1,0:T(8,128)S(1)} %collective-permute-done.own_1.refs_1_, f32[32,128,128]{2,1,0:T(8,128)} %collective-permute-done.6.vis_0.refs_4_, f32[32,128,128]{2,1,0:T(8,128)S(1)} %collective-permute-done.7.vis_1.refs_5_, ...), custom_call_target="tpu_custom_call" | custom-call | flops 2147483648 | bytes 20971520 | tf_op jit(solution)/shard_map/near_field/pallas_call | solution.py:253
  255.6 13.5 %near_field.7.refs_7_ = f32[2,64,128,128]{3,2,1,0:T(8,128)} custom-call(f32[2,32,128,128]{3,2,1,0:T(8,128)S(1)} %copy-done, f32[2,32,128,128]{3,2,1,0:T(8,128)S(1)} %collective-permute-done.own_1.refs_1_, f32[32,128,128]{2,1,0:T(8,128)} %collective-permute-done.3.vis_0.refs_4_, f32[32,128,128]{2,1,0:T(8,128)S(1)} %collective-permute-done.4.vis_1.refs_5_, ...), custom_call_target="tpu_custom_call" | custom-call | flops 2147483648 | bytes 20971520 | tf_op jit(solution)/shard_map/near_field/pallas_call | solution.py:253
  269.1 70.6 %collective-permute-done.2.refs_3_ = f32[2,32,128,128]{3,2,1,0:T(8,128)} collective-permute-done((f32[2,32,128,128]{3,2,1,0:T(8,128)S(1)}, f32[2,32,128,128]{3,2,1,0:T(8,128)}, u32[]{:S(2)}, u32[]{:S(2)}) %collective-permute-start.2) | collective-permute-done | bytes 4194336 | tf_op jit(solution)/shard_map/ppermute | solution.py:565
  339.6 43.6 %solve_field.4 = (f32[32,128,128]{2,1,0:T(8,128)}, f32[2,32,128,128]{3,2,1,0:T(8,128)}, f32[2,32,128,128]{3,2,1,0:T(8,128)}) custom-call(f32[2,32,128,128]{3,2,1,0:T(8,128)} %constant_dynamic-slice_fusion.1.own_0.refs_0_, f32[2,32,128,128]{3,2,1,0:T(8,128)} %copy-done.1, f32[2,32,128,128]{3,2,1,0:T(8,128)} %collective-permute-done.1.refs_2_, ...), custom_call_target="tpu_custom_call" | custom-call | flops 6442450944 | bytes 83886080 | tf_op jit(solution)/shard_map/solve_field/pallas_call | solution.py:525
  383.3 1.3 collective-permute-done.13.refs_6_
  384.6 43.9 %solve_field.5 = (f32[32,128,128]{2,1,0:T(8,128)}, f32[2,32,128,128]{3,2,1,0:T(8,128)}, f32[2,32,128,128]{3,2,1,0:T(8,128)}) custom-call(f32[2,32,128,128]{3,2,1,0:T(8,128)} %constant_dynamic-slice_fusion.1.own_0.refs_0_, f32[2,32,128,128]{3,2,1,0:T(8,128)} %copy-done.1, f32[2,32,128,128]{3,2,1,0:T(8,128)} %collective-permute-done.1.refs_2_, ...), custom_call_target="tpu_custom_call" | custom-call | flops 6442450944 | bytes 83886080 | tf_op jit(solution)/shard_map/solve_field/pallas_call | solution.py:525
  428.5 1.1 collective-permute-done.12.refs_6_
  429.5 43.7 %solve_field.6 = (f32[32,128,128]{2,1,0:T(8,128)}, f32[2,32,128,128]{3,2,1,0:T(8,128)}, f32[2,32,128,128]{3,2,1,0:T(8,128)}) custom-call(f32[2,32,128,128]{3,2,1,0:T(8,128)} %constant_dynamic-slice_fusion.1.own_0.refs_0_, f32[2,32,128,128]{3,2,1,0:T(8,128)} %copy-done.1, f32[2,32,128,128]{3,2,1,0:T(8,128)} %collective-permute-done.1.refs_2_, ...), custom_call_target="tpu_custom_call" | custom-call | flops 6442450944 | bytes 83886080 | tf_op jit(solution)/shard_map/solve_field/pallas_call | solution.py:525
  473.3 43.7 %solve_field.7 = (f32[32,128,128]{2,1,0:T(8,128)}, f32[2,32,128,128]{3,2,1,0:T(8,128)}, f32[2,32,128,128]{3,2,1,0:T(8,128)}) custom-call(f32[2,32,128,128]{3,2,1,0:T(8,128)} %constant_dynamic-slice_fusion.1.own_0.refs_0_, f32[2,32,128,128]{3,2,1,0:T(8,128)} %copy-done.1, f32[2,32,128,128]{3,2,1,0:T(8,128)} %collective-permute-done.1.refs_2_, ...), custom_call_target="tpu_custom_call" | custom-call | flops 6442450944 | bytes 83886080 | tf_op jit(solution)/shard_map/solve_field/pallas_call | solution.py:525
  517.0 2.1 collective-permute-start.16
  519.1 1.4 collective-permute-start.17
  520.5 0.5 collective-permute-start.18
  521.0 1.4 collective-permute-start.19
  522.4 1.0 broadcast.199
  523.5 1.1 copy-done.14
  524.6 0.5 constant_dynamic-update-slice_fusion.1
  525.2 40.6 %collective-permute-done.16 = f32[32,128,128]{2,1,0:T(8,128)S(1)} collective-permute-done((f32[32,128,128]{2,1,0:T(8,128)}, f32[32,128,128]{2,1,0:T(8,128)S(1)}, u32[]{:S(2)}, u32[]{:S(2)}) %collective-permute-start.16) | collective-permute-done | bytes 2097184 | tf_op jit(solution)/shard_map/ppermute | solution.py:22
  565.8 1.0 dynamic_update_slice.20
  566.8 43.9 %collective-permute-done.17 = f32[32,128,128]{2,1,0:T(8,128)S(1)} collective-permute-done((f32[32,128,128]{2,1,0:T(8,128)}, f32[32,128,128]{2,1,0:T(8,128)S(1)}, u32[]{:S(2)}, u32[]{:S(2)}) %collective-permute-start.17) | collective-permute-done | bytes 2097184 | tf_op jit(solution)/shard_map/ppermute | solution.py:22
  611.0 44.7 %collective-permute-done.18 = f32[32,128,128]{2,1,0:T(8,128)S(1)} collective-permute-done((f32[32,128,128]{2,1,0:T(8,128)}, f32[32,128,128]{2,1,0:T(8,128)S(1)}, u32[]{:S(2)}, u32[]{:S(2)}) %collective-permute-start.18) | collective-permute-done | bytes 2097184 | tf_op jit(solution)/shard_map/ppermute | solution.py:22
  655.9 44.2 %collective-permute-done.19 = f32[32,128,128]{2,1,0:T(8,128)S(1)} collective-permute-done((f32[32,128,128]{2,1,0:T(8,128)}, f32[32,128,128]{2,1,0:T(8,128)S(1)}, u32[]{:S(2)}, u32[]{:S(2)}) %collective-permute-start.19) | collective-permute-done | bytes 2097184 | tf_op jit(solution)/shard_map/ppermute | solution.py:22
  700.3 0.6 constant_dynamic-update-slice_fusion
  701.0 2.7 copy-done.12
  703.7 3.4 copy-done.13
  (44 shorter events, 1.4 us)
Async XLA Ops:
  5.3 4.6 copy-start.11
  8.0 148.2 %copy-start = (f32[2,32,128,128]{3,2,1,0:T(8,128)S(1)}, f32[2,32,128,128]{3,2,1,0:T(8,128)}, u32[]{:S(2)}) copy-start(f32[2,32,128,128]{3,2,1,0:T(8,128)} %constant_dynamic-slice_fusion.1.own_0.refs_0_) | copy-start | bytes 12582916
  8.0 149.9 %collective-permute-start = (f32[2,32,128,128]{3,2,1,0:T(8,128)S(1)}, f32[2,32,128,128]{3,2,1,0:T(8,128)S(1)}, u32[]{:S(2)}, u32[]{:S(2)}) collective-permute-start(f32[2,32,128,128]{3,2,1,0:T(8,128)S(1)} %constant_dynamic-slice_fusion), channel_id=1, source_target_pairs={{0,1},{1,0},{2,3},{3,2},{4,5},{5,4},{6,7},{7,6},{8,9},{9,8},{10,11... | collective-permute-start | bytes 12582920 | tf_op jit(solution)/shard_map/ppermute | solution.py:565
  13.5 52.7 %collective-permute-start.10 = (f32[32,128,128]{2,1,0:T(8,128)}, f32[32,128,128]{2,1,0:T(8,128)S(1)}, u32[]{:S(2)}, u32[]{:S(2)}) collective-permute-start(f32[32,128,128]{2,1,0:T(8,128)} %get-tuple-element.30), channel_id=1, source_target_pairs={{28,0},{0,4},{4,8},{8,12},{12,16},{16,20},{20,24},{24,28},{29,1},{... | collective-permute-start | bytes 6291464 | tf_op jit(solution)/shard_map/ppermute | solution.py:22
  16.5 94.8 %collective-permute-start.8 = (f32[32,128,128]{2,1,0:T(8,128)}, f32[32,128,128]{2,1,0:T(8,128)}, u32[]{:S(2)}, u32[]{:S(2)}) collective-permute-start(f32[32,128,128]{2,1,0:T(8,128)} %get-tuple-element.31), channel_id=1, source_target_pairs={{28,0},{0,4},{4,8},{8,12},{12,16},{16,20},{20,24},{24,28},{29,1},{... | collective-permute-start | bytes 6291464 | tf_op jit(solution)/shard_map/ppermute | solution.py:22
  18.0 138.2 %collective-permute-start.6 = (f32[32,128,128]{2,1,0:T(8,128)}, f32[32,128,128]{2,1,0:T(8,128)}, u32[]{:S(2)}, u32[]{:S(2)}) collective-permute-start(f32[32,128,128]{2,1,0:T(8,128)} %get-tuple-element.32), channel_id=1, source_target_pairs={{28,0},{0,4},{4,8},{8,12},{12,16},{16,20},{20,24},{24,28},{29,1},{... | collective-permute-start | bytes 6291464 | tf_op jit(solution)/shard_map/ppermute | solution.py:22
  19.5 180.8 %collective-permute-start.3 = (f32[32,128,128]{2,1,0:T(8,128)}, f32[32,128,128]{2,1,0:T(8,128)}, u32[]{:S(2)}, u32[]{:S(2)}) collective-permute-start(f32[32,128,128]{2,1,0:T(8,128)} %get-tuple-element.33), channel_id=1, source_target_pairs={{28,0},{0,4},{4,8},{8,12},{12,16},{16,20},{20,24},{24,28},{29,1},{... | collective-permute-start | bytes 6291464 | tf_op jit(solution)/shard_map/ppermute | solution.py:22
  66.2 149.4 %copy-start.6 = (f32[32,128,128]{2,1,0:T(8,128)}, f32[32,128,128]{2,1,0:T(8,128)S(1)}, u32[]{:S(2)}) copy-start(f32[32,128,128]{2,1,0:T(8,128)S(1)} %collective-permute-done.10.vis_0.refs_4_) | copy-start | bytes 6291460
  66.2 134.1 %collective-permute-start.11 = (f32[32,128,128]{2,1,0:T(8,128)S(1)}, f32[32,128,128]{2,1,0:T(8,128)S(1)}, u32[]{:S(2)}, u32[]{:S(2)}) collective-permute-start(f32[32,128,128]{2,1,0:T(8,128)S(1)} %collective-permute-done.10.vis_0.refs_4_), channel_id=1, source_target_pairs={{0,1},{1,0},{2,3},{3,2},{4,5},{5,4},{6,7},{7,6},{8,9},{9,8},{10,11... | collective-permute-start | bytes 6291464 | tf_op jit(solution)/shard_map/ppermute | solution.py:565
  111.3 89.6 %collective-permute-start.14 = (f32[32,128,128]{2,1,0:T(8,128)S(1)}, f32[32,128,128]{2,1,0:T(8,128)}, u32[]{:S(2)}, u32[]{:S(2)}) collective-permute-start(f32[32,128,128]{2,1,0:T(8,128)S(1)} %collective-permute-done.10.vis_0.refs_4_), channel_id=1, source_target_pairs={{0,2},{1,3},{2,0},{3,1},{4,6},{5,7},{6,4},{7,5},{8,10},{9,11},{10,... | collective-permute-start | bytes 6291464 | tf_op jit(solution)/shard_map/ppermute | solution.py:565
  156.2 112.8 %collective-permute-start.1 = (f32[2,32,128,128]{3,2,1,0:T(8,128)S(1)}, f32[2,32,128,128]{3,2,1,0:T(8,128)}, u32[]{:S(2)}, u32[]{:S(2)}) collective-permute-start(f32[2,32,128,128]{3,2,1,0:T(8,128)S(1)} %copy-done), channel_id=1, source_target_pairs={{0,2},{1,3},{2,0},{3,1},{4,6},{5,7},{6,4},{7,5},{8,10},{9,11},{10,... | collective-permute-start | bytes 12582920 | tf_op jit(solution)/shard_map/ppermute | solution.py:565
  157.9 97.7 %copy-start.1 = (f32[2,32,128,128]{3,2,1,0:T(8,128)}, f32[2,32,128,128]{3,2,1,0:T(8,128)S(1)}, u32[]{:S(2)}) copy-start(f32[2,32,128,128]{3,2,1,0:T(8,128)S(1)} %collective-permute-done.own_1.refs_1_) | copy-start | bytes 12582916
  157.9 181.8 %collective-permute-start.2 = (f32[2,32,128,128]{3,2,1,0:T(8,128)S(1)}, f32[2,32,128,128]{3,2,1,0:T(8,128)}, u32[]{:S(2)}, u32[]{:S(2)}) collective-permute-start(f32[2,32,128,128]{3,2,1,0:T(8,128)S(1)} %collective-permute-done.own_1.refs_1_), channel_id=1, source_target_pairs={{0,2},{1,3},{2,0},{3,1},{4,6},{5,7},{6,4},{7,5},{8,10},{9,11},{10,... | collective-permute-start | bytes 12582920 | tf_op jit(solution)/shard_map/ppermute | solution.py:565
  200.3 4.4 collective-permute-start.9
  200.3 15.3 %copy-start.7 = (f32[32,128,128]{2,1,0:T(8,128)}, f32[32,128,128]{2,1,0:T(8,128)S(1)}, u32[]{:S(2)}) copy-start(f32[32,128,128]{2,1,0:T(8,128)S(1)} %collective-permute-done.11.vis_1.refs_5_) | copy-start | bytes 6291460
  200.3 7.4 %collective-permute-start.7 = (f32[32,128,128]{2,1,0:T(8,128)}, f32[32,128,128]{2,1,0:T(8,128)S(1)}, u32[]{:S(2)}, u32[]{:S(2)}) collective-permute-start(f32[32,128,128]{2,1,0:T(8,128)} %collective-permute-done.6.vis_0.refs_4_), channel_id=1, source_target_pairs={{0,1},{1,0},{2,3},{3,2},{4,5},{5,4},{6,7},{7,6},{8,9},{9,8},{10,11... | collective-permute-start | bytes 6291464 | tf_op jit(solution)/shard_map/ppermute | solution.py:565
  200.8 40.7 %collective-permute-start.4 = (f32[32,128,128]{2,1,0:T(8,128)}, f32[32,128,128]{2,1,0:T(8,128)S(1)}, u32[]{:S(2)}, u32[]{:S(2)}) collective-permute-start(f32[32,128,128]{2,1,0:T(8,128)} %collective-permute-done.3.vis_0.refs_4_), channel_id=1, source_target_pairs={{0,1},{1,0},{2,3},{3,2},{4,5},{5,4},{6,7},{7,6},{8,9},{9,8},{10,11... | collective-permute-start | bytes 6291464 | tf_op jit(solution)/shard_map/ppermute | solution.py:565
  201.0 14.6 %copy-start.2 = (bf16[256,256]{1,0:T(8,128)(2,1)S(1)}, bf16[256,256]{1,0:T(8,128)(2,1)}, u32[]{:S(2)}) copy-start(bf16[256,256]{1,0:T(8,128)(2,1)} %constant.100.clone.x_low.refs_10_.refs_14_) | copy-start | bytes 393220
  201.0 14.6 %copy-start.3 = (bf16[256,256]{1,0:T(8,128)(2,1)S(1)}, bf16[256,256]{1,0:T(8,128)(2,1)}, u32[]{:S(2)}) copy-start(bf16[256,256]{1,0:T(8,128)(2,1)} %constant.101.clone.y_high.refs_11_.refs_15_) | copy-start | bytes 393220
  201.0 14.6 %copy-start.4 = (bf16[256,256]{1,0:T(8,128)(2,1)S(1)}, bf16[256,256]{1,0:T(8,128)(2,1)}, u32[]{:S(2)}) copy-start(bf16[256,256]{1,0:T(8,128)(2,1)} %constant.102.clone.y_low.refs_12_.refs_16_) | copy-start | bytes 393220
  201.1 14.6 %copy-start.5 = (bf16[256,256]{1,0:T(8,128)(2,1)S(1)}, bf16[256,256]{1,0:T(8,128)(2,1)}, u32[]{:S(2)}) copy-start(bf16[256,256]{1,0:T(8,128)(2,1)} %constant.99.clone.x_high.refs_9_.refs_13_) | copy-start | bytes 393220
  204.7 23.4 %copy-start.10 = (f32[32,128,128]{2,1,0:T(8,128)}, f32[32,128,128]{2,1,0:T(8,128)S(1)}, u32[]{:S(2)}) copy-start(f32[32,128,128]{2,1,0:T(8,128)S(1)} %collective-permute-done.9.vis_1.refs_5_) | copy-start | bytes 6291460
  204.7 179.9 %collective-permute-start.13 = (f32[32,128,128]{2,1,0:T(8,128)}, f32[32,128,128]{2,1,0:T(8,128)}, u32[]{:S(2)}, u32[]{:S(2)}) collective-permute-start(f32[32,128,128]{2,1,0:T(8,128)} %collective-permute-done.8.vis_0.refs_4_), channel_id=1, source_target_pairs={{0,2},{1,3},{2,0},{3,1},{4,6},{5,7},{6,4},{7,5},{8,10},{9,11},{10,... | collective-permute-start | bytes 6291464 | tf_op jit(solution)/shard_map/ppermute | solution.py:565
  207.7 34.5 %copy-start.9 = (f32[32,128,128]{2,1,0:T(8,128)}, f32[32,128,128]{2,1,0:T(8,128)S(1)}, u32[]{:S(2)}) copy-start(f32[32,128,128]{2,1,0:T(8,128)S(1)} %collective-permute-done.7.vis_1.refs_5_) | copy-start | bytes 6291460
  207.7 221.9 %collective-permute-start.12 = (f32[32,128,128]{2,1,0:T(8,128)}, f32[32,128,128]{2,1,0:T(8,128)}, u32[]{:S(2)}, u32[]{:S(2)}) collective-permute-start(f32[32,128,128]{2,1,0:T(8,128)} %collective-permute-done.6.vis_0.refs_4_), channel_id=1, source_target_pairs={{0,2},{1,3},{2,0},{3,1},{4,6},{5,7},{6,4},{7,5},{8,10},{9,11},{10,... | collective-permute-start | bytes 6291464 | tf_op jit(solution)/shard_map/ppermute | solution.py:565
  241.5 14.0 %copy-start.8 = (f32[32,128,128]{2,1,0:T(8,128)}, f32[32,128,128]{2,1,0:T(8,128)S(1)}, u32[]{:S(2)}) copy-start(f32[32,128,128]{2,1,0:T(8,128)S(1)} %collective-permute-done.4.vis_1.refs_5_) | copy-start | bytes 6291460
  241.5 231.7 %collective-permute-start.5 = (f32[32,128,128]{2,1,0:T(8,128)}, f32[32,128,128]{2,1,0:T(8,128)}, u32[]{:S(2)}, u32[]{:S(2)}) collective-permute-start(f32[32,128,128]{2,1,0:T(8,128)} %collective-permute-done.3.vis_0.refs_4_), channel_id=1, source_target_pairs={{0,2},{1,3},{2,0},{3,1},{4,6},{5,7},{6,4},{7,5},{8,10},{9,11},{10,... | collective-permute-start | bytes 6291464 | tf_op jit(solution)/shard_map/ppermute | solution.py:565
  516.9 183.4 %collective-permute-start.15 = (f32[2,32,128,128]{3,2,1,0:T(8,128)}, f32[2,32,128,128]{3,2,1,0:T(8,128)S(1)}, u32[]{:S(2)}, u32[]{:S(2)}) collective-permute-start(f32[2,32,128,128]{3,2,1,0:T(8,128)} %get-tuple-element.25), channel_id=1, source_target_pairs={{0,1},{1,0},{2,3},{3,2},{4,5},{5,4},{6,7},{7,6},{8,9},{9,8},{10,11... | collective-permute-start | bytes 12582920 | tf_op jit(solution)/shard_map/ppermute | solution.py:565
  517.0 48.8 %collective-permute-start.16 = (f32[32,128,128]{2,1,0:T(8,128)}, f32[32,128,128]{2,1,0:T(8,128)S(1)}, u32[]{:S(2)}, u32[]{:S(2)}) collective-permute-start(f32[32,128,128]{2,1,0:T(8,128)} %get-tuple-element.26), channel_id=1, source_target_pairs={{4,0},{8,4},{12,8},{16,12},{20,16},{24,20},{28,24},{0,28},{5,1},{9... | collective-permute-start | bytes 6291464 | tf_op jit(solution)/shard_map/ppermute | solution.py:22
  519.1 91.6 %collective-permute-start.17 = (f32[32,128,128]{2,1,0:T(8,128)}, f32[32,128,128]{2,1,0:T(8,128)S(1)}, u32[]{:S(2)}, u32[]{:S(2)}) collective-permute-start(f32[32,128,128]{2,1,0:T(8,128)} %get-tuple-element.27), channel_id=1, source_target_pairs={{4,0},{8,4},{12,8},{16,12},{20,16},{24,20},{28,24},{0,28},{5,1},{9... | collective-permute-start | bytes 6291464 | tf_op jit(solution)/shard_map/ppermute | solution.py:22
  520.5 135.2 %collective-permute-start.18 = (f32[32,128,128]{2,1,0:T(8,128)}, f32[32,128,128]{2,1,0:T(8,128)S(1)}, u32[]{:S(2)}, u32[]{:S(2)}) collective-permute-start(f32[32,128,128]{2,1,0:T(8,128)} %get-tuple-element.28), channel_id=1, source_target_pairs={{4,0},{8,4},{12,8},{16,12},{20,16},{24,20},{28,24},{0,28},{5,1},{9... | collective-permute-start | bytes 6291464 | tf_op jit(solution)/shard_map/ppermute | solution.py:22
  521.0 179.1 %collective-permute-start.19 = (f32[32,128,128]{2,1,0:T(8,128)}, f32[32,128,128]{2,1,0:T(8,128)S(1)}, u32[]{:S(2)}, u32[]{:S(2)}) collective-permute-start(f32[32,128,128]{2,1,0:T(8,128)} %get-tuple-element.29), channel_id=1, source_target_pairs={{4,0},{8,4},{12,8},{16,12},{20,16},{24,20},{28,24},{0,28},{5,1},{9... | collective-permute-start | bytes 6291464 | tf_op jit(solution)/shard_map/ppermute | solution.py:22
  522.4 2.2 copy-start.14
  700.3 3.4 copy-start.12
  703.7 3.4 copy-start.13

commit v5 on v4

--- a/solution.py
+++ b/solution.py
@@ -560,6 +560,26 @@
     return results[0], results[1:]
 
 
+def place_kernel(place, _, row, out, sem):
+    copy = pltpu.make_async_copy(row, out.at[place], sem)
+    copy.start()
+    copy.wait()
+
+
+def placed_row(rows, row, place):
+    anywhere = pl.BlockSpec(memory_space=pl.ANY)
+    return pl.pallas_call(
+        functools.partial(place_kernel, place),
+        out_shape=jax.ShapeDtypeStruct(rows.shape, rows.dtype),
+        in_specs=[anywhere, pl.BlockSpec(memory_space=pltpu.VMEM)],
+        out_specs=anywhere,
+        scratch_shapes=[pltpu.SemaphoreType.DMA],
+        input_output_aliases={0: 0},
+        compiler_params=pltpu.CompilerParams(vmem_limit_bytes=50 * 1024 * 1024),
+        name="place_row",
+    )(rows, row)
+
+
 def exchanged(block, bit):
     devices = range(lax.axis_size("grid"))
     return lax.ppermute(block, "grid", [(i, i ^ bit) for i in devices])
@@ -622,8 +642,9 @@
     own_rows = lax.dynamic_update_slice_in_dim(own_rows, sums[0], core * half_own, 0)
     own_rows = lax.dynamic_update_slice_in_dim(own_rows, own_other, (1 - core) * half_own, 0)
     held_rows = jnp.zeros(travel_bands.shape, travel_bands.dtype)
-    for j in range(count_vis):
+    for j in range(count_vis - 1):
         held_rows = lax.dynamic_update_slice_in_dim(held_rows, returned[j][None], j, 0)
+    held_rows = placed_row(held_rows, returned[-1], count_vis - 1)
     return own_rows, held_rows
 
 

time: 708 us -> 707 us (level)
  no operation moved by 1% of the time
where the time goes in v5:
time: 707 us; the launch traced here: 706 us
  waiting for transfers between devices  427 us (60%)
  Pallas kernels  229 us (32%)
  starting transfers between devices  21.4 us (3%)
  local copies, waits for them, and re-layouts  21.1 us (3%)
    ppermute x8, waiting for transfers between devices, passed_along(): return lax.ppermute(block, axis, route)  349 us
    pallas_call x4, Pallas kernels, solve_field(): pl.pallas_call(functools.partial(field_kernel, 8, first_call), out_shape=...  175 us
    ppermute x12, waiting for transfers between devices, exchanged(): return lax.ppermute(block, 'grid', [(i, i ^ bit) for i in devices])  78.1 us
    pallas_call x4, Pallas kernels, near_field(): pl.pallas_call(near_kernel, out_shape=jax.ShapeDtypeStruct((2, 2 * depth,...  52.7 us
  transfers between devices with their start and end apart: 20, of which 13 were waited for; matrix products, arithmetic and copies ran while one was open for 2% of the time, Pallas kernels for 26%

profile of v5, /device:TPU:0, one launch (start us, length us, event | category | flops | bytes accessed | tf_op | source)
XLA Modules:
  0.0 706.1 jit_solution(12039499005767029858)
XLA Ops:
  0.6 4.7 constant_dynamic-slice_fusion.1.own_0.refs_0_
  5.3 2.6 constant_dynamic-slice_fusion
  8.0 0.6 collective-permute-start
  8.5 1.5 copy-done.12
  10.0 3.5 slice_bitcast_fusion
  13.5 3.0 collective-permute-start.10
  16.5 1.5 collective-permute-start.8
  18.0 1.5 collective-permute-start.6
  19.5 1.5 collective-permute-start.3
  21.1 45.2 %collective-permute-done.10.vis_0.refs_4_ = f32[32,128,128]{2,1,0:T(8,128)S(1)} collective-permute-done((f32[32,128,128]{2,1,0:T(8,128)}, f32[32,128,128]{2,1,0:T(8,128)S(1)}, u32[]{:S(2)}, u32[]{:S(2)}) %collective-permute-start.10) | collective-permute-done | bytes 2097184 | tf_op jit(solution)/shard_map/ppermute | solution.py:22
  66.2 45.0 %collective-permute-done.8.vis_0.refs_4_ = f32[32,128,128]{2,1,0:T(8,128)} collective-permute-done((f32[32,128,128]{2,1,0:T(8,128)}, f32[32,128,128]{2,1,0:T(8,128)}, u32[]{:S(2)}, u32[]{:S(2)}) %collective-permute-start.8) | collective-permute-done | bytes 2097184 | tf_op jit(solution)/shard_map/ppermute | solution.py:22
  111.3 1.7 collective-permute-start.14
  112.9 43.3 %collective-permute-done.6.vis_0.refs_4_ = f32[32,128,128]{2,1,0:T(8,128)} collective-permute-done((f32[32,128,128]{2,1,0:T(8,128)}, f32[32,128,128]{2,1,0:T(8,128)}, u32[]{:S(2)}, u32[]{:S(2)}) %collective-permute-start.6) | collective-permute-done | bytes 2097184 | tf_op jit(solution)/shard_map/ppermute | solution.py:22
  156.2 1.7 collective-permute-start.1
  157.9 0.4 collective-permute-start.2
  158.2 42.1 %collective-permute-done.3.vis_0.refs_4_ = f32[32,128,128]{2,1,0:T(8,128)} collective-permute-done((f32[32,128,128]{2,1,0:T(8,128)}, f32[32,128,128]{2,1,0:T(8,128)}, u32[]{:S(2)}, u32[]{:S(2)}) %collective-permute-start.3) | collective-permute-done | bytes 2097184 | tf_op jit(solution)/shard_map/ppermute | solution.py:22
  200.3 0.5 collective-permute-start.7
  201.1 3.6 collective-permute-done.9.vis_1.refs_5_
  204.7 1.5 collective-permute-start.13
  206.2 1.5 collective-permute-done.7.vis_1.refs_5_
  207.7 1.5 collective-permute-start.12
  209.2 6.5 fusion.1.order.refs_8_
  215.7 12.4 %near_field.4.order.refs_7_ = f32[2,64,128,128]{3,2,1,0:T(8,128)} custom-call(f32[2,32,128,128]{3,2,1,0:T(8,128)S(1)} %copy-done, f32[2,32,128,128]{3,2,1,0:T(8,128)S(1)} %collective-permute-done.own_1.refs_1_, f32[32,128,128]{2,1,0:T(8,128)S(1)} %collective-permute-done.10.vis_0.refs_4_, f32[32,128,128]{2,1,0:T(8,128)S(1)} %collective-permute-done.11.vis_1.refs_5_, ...), custom_call_target="tpu_custom_call" | custom-call | flops 2147483648 | bytes 20971520 | tf_op jit(solution)/shard_map/near_field/pallas_call | solution.py:253
  228.1 13.5 %near_field.5.order.refs_7_ = f32[2,64,128,128]{3,2,1,0:T(8,128)} custom-call(f32[2,32,128,128]{3,2,1,0:T(8,128)S(1)} %copy-done, f32[2,32,128,128]{3,2,1,0:T(8,128)S(1)} %collective-permute-done.own_1.refs_1_, f32[32,128,128]{2,1,0:T(8,128)} %collective-permute-done.8.vis_0.refs_4_, f32[32,128,128]{2,1,0:T(8,128)S(1)} %collective-permute-done.9.vis_1.refs_5_, ...), custom_call_target="tpu_custom_call" | custom-call | flops 2147483648 | bytes 20971520 | tf_op jit(solution)/shard_map/near_field/pallas_call | solution.py:253
  241.5 0.6 collective-permute-start.5
  242.1 13.4 %near_field.6.order.refs_7_ = f32[2,64,128,128]{3,2,1,0:T(8,128)} custom-call(f32[2,32,128,128]{3,2,1,0:T(8,128)S(1)} %copy-done, f32[2,32,128,128]{3,2,1,0:T(8,128)S(1)} %collective-permute-done.own_1.refs_1_, f32[32,128,128]{2,1,0:T(8,128)} %collective-permute-done.6.vis_0.refs_4_, f32[32,128,128]{2,1,0:T(8,128)S(1)} %collective-permute-done.7.vis_1.refs_5_, ...), custom_call_target="tpu_custom_call" | custom-call | flops 2147483648 | bytes 20971520 | tf_op jit(solution)/shard_map/near_field/pallas_call | solution.py:253
  255.6 13.5 %near_field.7.refs_7_ = f32[2,64,128,128]{3,2,1,0:T(8,128)} custom-call(f32[2,32,128,128]{3,2,1,0:T(8,128)S(1)} %copy-done, f32[2,32,128,128]{3,2,1,0:T(8,128)S(1)} %collective-permute-done.own_1.refs_1_, f32[32,128,128]{2,1,0:T(8,128)} %collective-permute-done.3.vis_0.refs_4_, f32[32,128,128]{2,1,0:T(8,128)S(1)} %collective-permute-done.4.vis_1.refs_5_, ...), custom_call_target="tpu_custom_call" | custom-call | flops 2147483648 | bytes 20971520 | tf_op jit(solution)/shard_map/near_field/pallas_call | solution.py:253
  269.1 70.6 %collective-permute-done.2.refs_3_ = f32[2,32,128,128]{3,2,1,0:T(8,128)} collective-permute-done((f32[2,32,128,128]{3,2,1,0:T(8,128)S(1)}, f32[2,32,128,128]{3,2,1,0:T(8,128)}, u32[]{:S(2)}, u32[]{:S(2)}) %collective-permute-start.2) | collective-permute-done | bytes 4194336 | tf_op jit(solution)/shard_map/ppermute | solution.py:585
  339.6 43.6 %solve_field.4 = (f32[32,128,128]{2,1,0:T(8,128)}, f32[2,32,128,128]{3,2,1,0:T(8,128)}, f32[2,32,128,128]{3,2,1,0:T(8,128)}) custom-call(f32[2,32,128,128]{3,2,1,0:T(8,128)} %constant_dynamic-slice_fusion.1.own_0.refs_0_, f32[2,32,128,128]{3,2,1,0:T(8,128)} %copy-done.1, f32[2,32,128,128]{3,2,1,0:T(8,128)} %collective-permute-done.1.refs_2_, ...), custom_call_target="tpu_custom_call" | custom-call | flops 6442450944 | bytes 83886080 | tf_op jit(solution)/shard_map/solve_field/pallas_call | solution.py:525
  383.2 1.3 collective-permute-done.13.refs_6_
  384.6 43.9 %solve_field.5 = (f32[32,128,128]{2,1,0:T(8,128)}, f32[2,32,128,128]{3,2,1,0:T(8,128)}, f32[2,32,128,128]{3,2,1,0:T(8,128)}) custom-call(f32[2,32,128,128]{3,2,1,0:T(8,128)} %constant_dynamic-slice_fusion.1.own_0.refs_0_, f32[2,32,128,128]{3,2,1,0:T(8,128)} %copy-done.1, f32[2,32,128,128]{3,2,1,0:T(8,128)} %collective-permute-done.1.refs_2_, ...), custom_call_target="tpu_custom_call" | custom-call | flops 6442450944 | bytes 83886080 | tf_op jit(solution)/shard_map/solve_field/pallas_call | solution.py:525
  428.5 1.1 collective-permute-done.12.refs_6_
  429.5 43.7 %solve_field.6 = (f32[32,128,128]{2,1,0:T(8,128)}, f32[2,32,128,128]{3,2,1,0:T(8,128)}, f32[2,32,128,128]{3,2,1,0:T(8,128)}) custom-call(f32[2,32,128,128]{3,2,1,0:T(8,128)} %constant_dynamic-slice_fusion.1.own_0.refs_0_, f32[2,32,128,128]{3,2,1,0:T(8,128)} %copy-done.1, f32[2,32,128,128]{3,2,1,0:T(8,128)} %collective-permute-done.1.refs_2_, ...), custom_call_target="tpu_custom_call" | custom-call | flops 6442450944 | bytes 83886080 | tf_op jit(solution)/shard_map/solve_field/pallas_call | solution.py:525
  473.3 43.7 %solve_field.7 = (f32[32,128,128]{2,1,0:T(8,128)}, f32[2,32,128,128]{3,2,1,0:T(8,128)}, f32[2,32,128,128]{3,2,1,0:T(8,128)}) custom-call(f32[2,32,128,128]{3,2,1,0:T(8,128)} %constant_dynamic-slice_fusion.1.own_0.refs_0_, f32[2,32,128,128]{3,2,1,0:T(8,128)} %copy-done.1, f32[2,32,128,128]{3,2,1,0:T(8,128)} %collective-permute-done.1.refs_2_, ...), custom_call_target="tpu_custom_call" | custom-call | flops 6442450944 | bytes 83886080 | tf_op jit(solution)/shard_map/solve_field/pallas_call | solution.py:525
  517.0 2.1 collective-permute-start.16
  519.1 1.4 collective-permute-start.17
  520.5 0.5 collective-permute-start.18
  521.0 1.4 collective-permute-start.19
  522.4 1.0 broadcast.199
  523.5 1.1 copy-done.14
  524.6 0.6 constant_dynamic-update-slice_fusion.1
  525.2 40.5 %collective-permute-done.16 = f32[32,128,128]{2,1,0:T(8,128)S(1)} collective-permute-done((f32[32,128,128]{2,1,0:T(8,128)}, f32[32,128,128]{2,1,0:T(8,128)S(1)}, u32[]{:S(2)}, u32[]{:S(2)}) %collective-permute-start.16) | collective-permute-done | bytes 2097184 | tf_op jit(solution)/shard_map/ppermute | solution.py:22
  565.8 1.0 dynamic_update_slice.17
  566.8 43.9 %collective-permute-done.17 = f32[32,128,128]{2,1,0:T(8,128)S(1)} collective-permute-done((f32[32,128,128]{2,1,0:T(8,128)}, f32[32,128,128]{2,1,0:T(8,128)S(1)}, u32[]{:S(2)}, u32[]{:S(2)}) %collective-permute-start.17) | collective-permute-done | bytes 2097184 | tf_op jit(solution)/shard_map/ppermute | solution.py:22
  610.9 44.8 %collective-permute-done.18 = f32[32,128,128]{2,1,0:T(8,128)S(1)} collective-permute-done((f32[32,128,128]{2,1,0:T(8,128)}, f32[32,128,128]{2,1,0:T(8,128)S(1)}, u32[]{:S(2)}, u32[]{:S(2)}) %collective-permute-start.18) | collective-permute-done | bytes 2097184 | tf_op jit(solution)/shard_map/ppermute | solution.py:22
  655.8 44.3 %collective-permute-done.19.row = f32[32,128,128]{2,1,0:T(8,128)S(1)} collective-permute-done((f32[32,128,128]{2,1,0:T(8,128)}, f32[32,128,128]{2,1,0:T(8,128)S(1)}, u32[]{:S(2)}, u32[]{:S(2)}) %collective-permute-start.19) | collective-permute-done | bytes 2097184 | tf_op jit(solution)/shard_map/ppermute | solution.py:22
  700.1 1.3 place_row.1
  701.4 4.7 constant_dynamic-update-slice_fusion
  (44 shorter events, 0.6 us)
Async XLA Ops:
  5.3 4.6 copy-start.12
  8.0 148.2 %copy-start = (f32[2,32,128,128]{3,2,1,0:T(8,128)S(1)}, f32[2,32,128,128]{3,2,1,0:T(8,128)}, u32[]{:S(2)}) copy-start(f32[2,32,128,128]{3,2,1,0:T(8,128)} %constant_dynamic-slice_fusion.1.own_0.refs_0_) | copy-start | bytes 12582916
  8.0 149.9 %collective-permute-start = (f32[2,32,128,128]{3,2,1,0:T(8,128)S(1)}, f32[2,32,128,128]{3,2,1,0:T(8,128)S(1)}, u32[]{:S(2)}, u32[]{:S(2)}) collective-permute-start(f32[2,32,128,128]{3,2,1,0:T(8,128)S(1)} %constant_dynamic-slice_fusion), channel_id=1, source_target_pairs={{0,1},{1,0},{2,3},{3,2},{4,5},{5,4},{6,7},{7,6},{8,9},{9,8},{10,11... | collective-permute-start | bytes 12582920 | tf_op jit(solution)/shard_map/ppermute | solution.py:585
  13.5 52.7 %collective-permute-start.10 = (f32[32,128,128]{2,1,0:T(8,128)}, f32[32,128,128]{2,1,0:T(8,128)S(1)}, u32[]{:S(2)}, u32[]{:S(2)}) collective-permute-start(f32[32,128,128]{2,1,0:T(8,128)} %get-tuple-element.30), channel_id=1, source_target_pairs={{28,0},{0,4},{4,8},{8,12},{12,16},{16,20},{20,24},{24,28},{29,1},{... | collective-permute-start | bytes 6291464 | tf_op jit(solution)/shard_map/ppermute | solution.py:22
  16.5 94.8 %collective-permute-start.8 = (f32[32,128,128]{2,1,0:T(8,128)}, f32[32,128,128]{2,1,0:T(8,128)}, u32[]{:S(2)}, u32[]{:S(2)}) collective-permute-start(f32[32,128,128]{2,1,0:T(8,128)} %get-tuple-element.31), channel_id=1, source_target_pairs={{28,0},{0,4},{4,8},{8,12},{12,16},{16,20},{20,24},{24,28},{29,1},{... | collective-permute-start | bytes 6291464 | tf_op jit(solution)/shard_map/ppermute | solution.py:22
  18.0 138.2 %collective-permute-start.6 = (f32[32,128,128]{2,1,0:T(8,128)}, f32[32,128,128]{2,1,0:T(8,128)}, u32[]{:S(2)}, u32[]{:S(2)}) collective-permute-start(f32[32,128,128]{2,1,0:T(8,128)} %get-tuple-element.32), channel_id=1, source_target_pairs={{28,0},{0,4},{4,8},{8,12},{12,16},{16,20},{20,24},{24,28},{29,1},{... | collective-permute-start | bytes 6291464 | tf_op jit(solution)/shard_map/ppermute | solution.py:22
  19.5 180.8 %collective-permute-start.3 = (f32[32,128,128]{2,1,0:T(8,128)}, f32[32,128,128]{2,1,0:T(8,128)}, u32[]{:S(2)}, u32[]{:S(2)}) collective-permute-start(f32[32,128,128]{2,1,0:T(8,128)} %get-tuple-element.33), channel_id=1, source_target_pairs={{28,0},{0,4},{4,8},{8,12},{12,16},{16,20},{20,24},{24,28},{29,1},{... | collective-permute-start | bytes 6291464 | tf_op jit(solution)/shard_map/ppermute | solution.py:22
  66.2 149.4 %copy-start.6 = (f32[32,128,128]{2,1,0:T(8,128)}, f32[32,128,128]{2,1,0:T(8,128)S(1)}, u32[]{:S(2)}) copy-start(f32[32,128,128]{2,1,0:T(8,128)S(1)} %collective-permute-done.10.vis_0.refs_4_) | copy-start | bytes 6291460
  66.2 134.1 %collective-permute-start.11 = (f32[32,128,128]{2,1,0:T(8,128)S(1)}, f32[32,128,128]{2,1,0:T(8,128)S(1)}, u32[]{:S(2)}, u32[]{:S(2)}) collective-permute-start(f32[32,128,128]{2,1,0:T(8,128)S(1)} %collective-permute-done.10.vis_0.refs_4_), channel_id=1, source_target_pairs={{0,1},{1,0},{2,3},{3,2},{4,5},{5,4},{6,7},{7,6},{8,9},{9,8},{10,11... | collective-permute-start | bytes 6291464 | tf_op jit(solution)/shard_map/ppermute | solution.py:585
  111.3 89.6 %collective-permute-start.14 = (f32[32,128,128]{2,1,0:T(8,128)S(1)}, f32[32,128,128]{2,1,0:T(8,128)}, u32[]{:S(2)}, u32[]{:S(2)}) collective-permute-start(f32[32,128,128]{2,1,0:T(8,128)S(1)} %collective-permute-done.10.vis_0.refs_4_), channel_id=1, source_target_pairs={{0,2},{1,3},{2,0},{3,1},{4,6},{5,7},{6,4},{7,5},{8,10},{9,11},{10,... | collective-permute-start | bytes 6291464 | tf_op jit(solution)/shard_map/ppermute | solution.py:585
  156.2 112.8 %collective-permute-start.1 = (f32[2,32,128,128]{3,2,1,0:T(8,128)S(1)}, f32[2,32,128,128]{3,2,1,0:T(8,128)}, u32[]{:S(2)}, u32[]{:S(2)}) collective-permute-start(f32[2,32,128,128]{3,2,1,0:T(8,128)S(1)} %copy-done), channel_id=1, source_target_pairs={{0,2},{1,3},{2,0},{3,1},{4,6},{5,7},{6,4},{7,5},{8,10},{9,11},{10,... | collective-permute-start | bytes 12582920 | tf_op jit(solution)/shard_map/ppermute | solution.py:585
  157.9 97.7 %copy-start.1 = (f32[2,32,128,128]{3,2,1,0:T(8,128)}, f32[2,32,128,128]{3,2,1,0:T(8,128)S(1)}, u32[]{:S(2)}) copy-start(f32[2,32,128,128]{3,2,1,0:T(8,128)S(1)} %collective-permute-done.own_1.refs_1_) | copy-start | bytes 12582916
  157.9 181.8 %collective-permute-start.2 = (f32[2,32,128,128]{3,2,1,0:T(8,128)S(1)}, f32[2,32,128,128]{3,2,1,0:T(8,128)}, u32[]{:S(2)}, u32[]{:S(2)}) collective-permute-start(f32[2,32,128,128]{3,2,1,0:T(8,128)S(1)} %collective-permute-done.own_1.refs_1_), channel_id=1, source_target_pairs={{0,2},{1,3},{2,0},{3,1},{4,6},{5,7},{6,4},{7,5},{8,10},{9,11},{10,... | collective-permute-start | bytes 12582920 | tf_op jit(solution)/shard_map/ppermute | solution.py:585
  200.3 4.4 collective-permute-start.9
  200.3 15.3 %copy-start.7 = (f32[32,128,128]{2,1,0:T(8,128)}, f32[32,128,128]{2,1,0:T(8,128)S(1)}, u32[]{:S(2)}) copy-start(f32[32,128,128]{2,1,0:T(8,128)S(1)} %collective-permute-done.11.vis_1.refs_5_) | copy-start | bytes 6291460
  200.3 7.4 %collective-permute-start.7 = (f32[32,128,128]{2,1,0:T(8,128)}, f32[32,128,128]{2,1,0:T(8,128)S(1)}, u32[]{:S(2)}, u32[]{:S(2)}) collective-permute-start(f32[32,128,128]{2,1,0:T(8,128)} %collective-permute-done.6.vis_0.refs_4_), channel_id=1, source_target_pairs={{0,1},{1,0},{2,3},{3,2},{4,5},{5,4},{6,7},{7,6},{8,9},{9,8},{10,11... | collective-permute-start | bytes 6291464 | tf_op jit(solution)/shard_map/ppermute | solution.py:585
  200.8 40.7 %collective-permute-start.4 = (f32[32,128,128]{2,1,0:T(8,128)}, f32[32,128,128]{2,1,0:T(8,128)S(1)}, u32[]{:S(2)}, u32[]{:S(2)}) collective-permute-start(f32[32,128,128]{2,1,0:T(8,128)} %collective-permute-done.3.vis_0.refs_4_), channel_id=1, source_target_pairs={{0,1},{1,0},{2,3},{3,2},{4,5},{5,4},{6,7},{7,6},{8,9},{9,8},{10,11... | collective-permute-start | bytes 6291464 | tf_op jit(solution)/shard_map/ppermute | solution.py:585
  201.0 14.6 %copy-start.2 = (bf16[256,256]{1,0:T(8,128)(2,1)S(1)}, bf16[256,256]{1,0:T(8,128)(2,1)}, u32[]{:S(2)}) copy-start(bf16[256,256]{1,0:T(8,128)(2,1)} %constant.100.clone.y_high.refs_11_.refs_15_) | copy-start | bytes 393220
  201.0 14.6 %copy-start.3 = (bf16[256,256]{1,0:T(8,128)(2,1)S(1)}, bf16[256,256]{1,0:T(8,128)(2,1)}, u32[]{:S(2)}) copy-start(bf16[256,256]{1,0:T(8,128)(2,1)} %constant.101.clone.y_low.refs_12_.refs_16_) | copy-start | bytes 393220
  201.0 14.6 %copy-start.4 = (bf16[256,256]{1,0:T(8,128)(2,1)S(1)}, bf16[256,256]{1,0:T(8,128)(2,1)}, u32[]{:S(2)}) copy-start(bf16[256,256]{1,0:T(8,128)(2,1)} %constant.98.clone.x_high.refs_9_.refs_13_) | copy-start | bytes 393220
  201.1 14.6 %copy-start.5 = (bf16[256,256]{1,0:T(8,128)(2,1)S(1)}, bf16[256,256]{1,0:T(8,128)(2,1)}, u32[]{:S(2)}) copy-start(bf16[256,256]{1,0:T(8,128)(2,1)} %constant.99.clone.x_low.refs_10_.refs_14_) | copy-start | bytes 393220
  204.7 23.4 %copy-start.10 = (f32[32,128,128]{2,1,0:T(8,128)}, f32[32,128,128]{2,1,0:T(8,128)S(1)}, u32[]{:S(2)}) copy-start(f32[32,128,128]{2,1,0:T(8,128)S(1)} %collective-permute-done.9.vis_1.refs_5_) | copy-start | bytes 6291460
  204.7 179.9 %collective-permute-start.13 = (f32[32,128,128]{2,1,0:T(8,128)}, f32[32,128,128]{2,1,0:T(8,128)}, u32[]{:S(2)}, u32[]{:S(2)}) collective-permute-start(f32[32,128,128]{2,1,0:T(8,128)} %collective-permute-done.8.vis_0.refs_4_), channel_id=1, source_target_pairs={{0,2},{1,3},{2,0},{3,1},{4,6},{5,7},{6,4},{7,5},{8,10},{9,11},{10,... | collective-permute-start | bytes 6291464 | tf_op jit(solution)/shard_map/ppermute | solution.py:585
  207.7 34.5 %copy-start.9 = (f32[32,128,128]{2,1,0:T(8,128)}, f32[32,128,128]{2,1,0:T(8,128)S(1)}, u32[]{:S(2)}) copy-start(f32[32,128,128]{2,1,0:T(8,128)S(1)} %collective-permute-done.7.vis_1.refs_5_) | copy-start | bytes 6291460
  207.7 221.9 %collective-permute-start.12 = (f32[32,128,128]{2,1,0:T(8,128)}, f32[32,128,128]{2,1,0:T(8,128)}, u32[]{:S(2)}, u32[]{:S(2)}) collective-permute-start(f32[32,128,128]{2,1,0:T(8,128)} %collective-permute-done.6.vis_0.refs_4_), channel_id=1, source_target_pairs={{0,2},{1,3},{2,0},{3,1},{4,6},{5,7},{6,4},{7,5},{8,10},{9,11},{10,... | collective-permute-start | bytes 6291464 | tf_op jit(solution)/shard_map/ppermute | solution.py:585
  241.5 14.0 %copy-start.8 = (f32[32,128,128]{2,1,0:T(8,128)}, f32[32,128,128]{2,1,0:T(8,128)S(1)}, u32[]{:S(2)}) copy-start(f32[32,128,128]{2,1,0:T(8,128)S(1)} %collective-permute-done.4.vis_1.refs_5_) | copy-start | bytes 6291460
  241.5 231.7 %collective-permute-start.5 = (f32[32,128,128]{2,1,0:T(8,128)}, f32[32,128,128]{2,1,0:T(8,128)}, u32[]{:S(2)}, u32[]{:S(2)}) collective-permute-start(f32[32,128,128]{2,1,0:T(8,128)} %collective-permute-done.3.vis_0.refs_4_), channel_id=1, source_target_pairs={{0,2},{1,3},{2,0},{3,1},{4,6},{5,7},{6,4},{7,5},{8,10},{9,11},{10,... | collective-permute-start | bytes 6291464 | tf_op jit(solution)/shard_map/ppermute | solution.py:585
  516.9 184.5 %collective-permute-start.15 = (f32[2,32,128,128]{3,2,1,0:T(8,128)}, f32[2,32,128,128]{3,2,1,0:T(8,128)}, u32[]{:S(2)}, u32[]{:S(2)}) collective-permute-start(f32[2,32,128,128]{3,2,1,0:T(8,128)} %get-tuple-element.25), channel_id=1, source_target_pairs={{0,1},{1,0},{2,3},{3,2},{4,5},{5,4},{6,7},{7,6},{8,9},{9,8},{10,11... | collective-permute-start | bytes 12582920 | tf_op jit(solution)/shard_map/ppermute | solution.py:585
  517.0 48.8 %collective-permute-start.16 = (f32[32,128,128]{2,1,0:T(8,128)}, f32[32,128,128]{2,1,0:T(8,128)S(1)}, u32[]{:S(2)}, u32[]{:S(2)}) collective-permute-start(f32[32,128,128]{2,1,0:T(8,128)} %get-tuple-element.26), channel_id=1, source_target_pairs={{4,0},{8,4},{12,8},{16,12},{20,16},{24,20},{28,24},{0,28},{5,1},{9... | collective-permute-start | bytes 6291464 | tf_op jit(solution)/shard_map/ppermute | solution.py:22
  519.1 91.6 %collective-permute-start.17 = (f32[32,128,128]{2,1,0:T(8,128)}, f32[32,128,128]{2,1,0:T(8,128)S(1)}, u32[]{:S(2)}, u32[]{:S(2)}) collective-permute-start(f32[32,128,128]{2,1,0:T(8,128)} %get-tuple-element.27), channel_id=1, source_target_pairs={{4,0},{8,4},{12,8},{16,12},{20,16},{24,20},{28,24},{0,28},{5,1},{9... | collective-permute-start | bytes 6291464 | tf_op jit(solution)/shard_map/ppermute | solution.py:22
  520.5 135.2 %collective-permute-start.18 = (f32[32,128,128]{2,1,0:T(8,128)}, f32[32,128,128]{2,1,0:T(8,128)S(1)}, u32[]{:S(2)}, u32[]{:S(2)}) collective-permute-start(f32[32,128,128]{2,1,0:T(8,128)} %get-tuple-element.28), channel_id=1, source_target_pairs={{4,0},{8,4},{12,8},{16,12},{20,16},{24,20},{28,24},{0,28},{5,1},{9... | collective-permute-start | bytes 6291464 | tf_op jit(solution)/shard_map/ppermute | solution.py:22
  521.0 179.1 %collective-permute-start.19 = (f32[32,128,128]{2,1,0:T(8,128)}, f32[32,128,128]{2,1,0:T(8,128)S(1)}, u32[]{:S(2)}, u32[]{:S(2)}) collective-permute-start(f32[32,128,128]{2,1,0:T(8,128)} %get-tuple-element.29), channel_id=1, source_target_pairs={{4,0},{8,4},{12,8},{16,12},{20,16},{24,20},{28,24},{0,28},{5,1},{9... | collective-permute-start | bytes 6291464 | tf_op jit(solution)/shard_map/ppermute | solution.py:22
  522.4 2.2 copy-start.14
  525.2 40.6 %copy-start.13 = (f32[4,32,128,128]{3,2,1,0:T(8,128)}, f32[4,32,128,128]{3,2,1,0:T(8,128)S(1)}, u32[]{:S(2)}) copy-start(f32[4,32,128,128]{3,2,1,0:T(8,128)S(1)} %constant_dynamic-update-slice_fusion.1) | copy-start | bytes 25165828
  655.8 44.3 %copy-start.11 = (f32[4,32,128,128]{3,2,1,0:T(8,128)}, f32[4,32,128,128]{3,2,1,0:T(8,128)S(1)}, u32[]{:S(2)}) copy-start(f32[4,32,128,128]{3,2,1,0:T(8,128)S(1)} %bitcast_dynamic-update-slice_fusion._) | copy-start | bytes 25165828
